TPU v7x, 128 devices: a whole 4x4x4 slice. The times are simulated.
128 devices in a mesh: mesh: 2 (over core), dom: 64 (over z, x, y).
Axes of the slice: x: 4, y: 4, z: 4, core: 2. Of those that a mesh axis runs over, the one named last changes fastest.
Arguments:
- donor_fields: float32 [5, 512, 16384], P(None, None, ('mesh', 'dom')), may hold values from -6 to 6
- interp_weights: float32 [3, 8, 262144], P(None, None, ('mesh', 'dom')), may hold values from -1 to 1, as said below
- donor_owner: int32 [262144, 1], P(('mesh', 'dom')), may hold values from 0 to 63, as said below
- donor_element: int32 [262144], P(('mesh', 'dom')), may hold values from 0 to 127
- geometry: float32 [4, 16384], P(None, ('mesh', 'dom')), may hold values from 0.25 to 4
- wall_flag: int32 [2, 1024], P(None, ('mesh', 'dom')), may hold values 0 or 1
- forcing: float32 [512, 16384], P(None, ('mesh', 'dom')), may hold values from -6 to 6
Outputs:
- velocity: float32 [512, 16384], P(None, ('mesh', 'dom'))
- residual: float32 [512, 16384], P(None, ('mesh', 'dom'))
- interface_values: float32 [5, 262144], P(None, ('mesh', 'dom'))
Inputs may be any that keep to these rules, and one draw needn't show every extreme that they name: `interp_weights`: for each receptor and direction, the 8 entries are the Lagrange polynomials of the order-7 Gauss-Lobatto-Legendre points evaluated at one point of [-1, 1]. `donor_owner`: the receptors of block q of a mesh (the rows of one device) name donor dom indices from q - 2 to q + 2 only; among them one index is named exactly 1024 times and no index more often.
All inputs are finite; a program needn't handle non-finite values. No bound on the sum of `wall_flag` on one device may be relied on, other than what follows from the above.
Results may differ from a plain program's by a relative error of at most 0.00026.
Values sent between devices are 32-bit elements; how exact they have to be, the bound alone decides.
No kernel may reach another device: no remote copies, remote signals or barrier semaphores. Data moves between devices by JAX's collectives and lax.ppermute only.
A program may use at most 192 MiB of HBM per device.

v0:
```python
import jax
import jax.numpy as jnp
import numpy as np
from jax import lax
from jax.sharding import PartitionSpec as P

EX = 8
EY = 16
EZ_DEV = 1
ITERS = 3


HIGHEST = lax.Precision.HIGHEST


def with_halo(value, sides, width):
    for axis, dim in sides:
        size, length = (lax.axis_size(axis), value.shape[dim])
        up = [(i, (i + 1) % size) for i in range(size - 1)]
        down = [(j, i) for i, j in up]
        last = lax.slice_in_dim(value, length - width, length, axis=dim)
        leading = lax.slice_in_dim(value, 0, width, axis=dim)
        before = lax.ppermute(last, axis, up)
        after = lax.ppermute(leading, axis, down)
        value = jnp.concatenate([before, value, after], axis=dim)
    return value


def swapped(block, axis, stride):
    count = lax.axis_size(axis)
    route = []
    for low in range(count):
        high = low | 1 << stride
        if high != low and high < count:
            route += [(low, high), (high, low)]
    return lax.ppermute(block, axis, route)


def from_behind(value, axis, steps):
    count = lax.axis_size(axis)
    leading, last = (max(0, -steps), min(count, count - steps))
    return lax.ppermute(value, axis, [(source, source + steps) for source in range(leading, last)])


def from_everyone(value, axis):
    length = lax.axis_size(axis)
    return lax.all_to_all(
        jnp.broadcast_to(value[None], (length, *value.shape)), axis, 0, 0, tiled=True
    )


def taken_together(value, axis):
    return from_everyone(value, axis).sum(axis=0)


def in_one(arrays, axis):
    ends = [0]
    for a in arrays:
        ends.append(ends[-1] + a.size)
    running = taken_together(jnp.concatenate([a.ravel() for a in arrays]), axis)
    return tuple((running[b:e].reshape(a.shape) for a, b, e in zip(arrays, ends, ends[1:])))


def legendre_pair(values, degree):
    previous = values * 0.0 + 1.0
    current = values * 1.0
    for poly_order in range(2, degree + 1):
        previous, current = (
            current,
            ((2 * poly_order - 1) * values * current - (poly_order - 1) * previous) / poly_order,
        )
    return (current, previous)


def gll_tables():
    degree = 7
    points_count = degree + 1
    abscissae = np.cos(np.pi * np.arange(points_count) / degree)
    for newton_turn in range(80):
        top_poly, lower_poly = legendre_pair(abscissae, degree)
        abscissae = abscissae - (abscissae * top_poly - lower_poly) / (points_count * top_poly)
    abscissae = np.sort(abscissae)
    top_poly, lower_poly = legendre_pair(abscissae, degree)
    quad_weights = 2.0 / (degree * points_count * top_poly * top_poly)
    identity_mat = np.eye(points_count)
    spacing = abscissae[:, None] - abscissae[None, :] + identity_mat
    derivative = top_poly[:, None] / (top_poly[None, :] * spacing) * (1.0 - identity_mat)
    derivative[0, 0] = -degree * points_count / 4.0
    derivative[degree, degree] = degree * points_count / 4.0
    return (jnp.asarray(derivative, jnp.float32), jnp.asarray(quad_weights, jnp.float32))


def cube_weights(quad_weights):
    return (
        quad_weights[:, None, None, None]
        * quad_weights[None, :, None, None]
        * quad_weights[None, None, :, None]
    )


def local_operator(field_data, geometry, derivative, quad_weights):
    weights_cube = cube_weights(quad_weights)
    grad_x = jnp.einsum("ai,kjie->kjae", derivative, field_data, precision=HIGHEST)
    grad_y = jnp.einsum("aj,kjie->kaie", derivative, field_data, precision=HIGHEST)
    grad_z = jnp.einsum("ak,kjie->ajie", derivative, field_data, precision=HIGHEST)
    result = jnp.einsum(
        "ai,kjae->kjie", derivative, grad_x * (weights_cube * geometry[0]), precision=HIGHEST
    )
    result = result + jnp.einsum(
        "aj,kaie->kjie", derivative, grad_y * (weights_cube * geometry[1]), precision=HIGHEST
    )
    result = result + jnp.einsum(
        "ak,ajie->kjie", derivative, grad_z * (weights_cube * geometry[2]), precision=HIGHEST
    )
    return result + weights_cube * geometry[3] * field_data


def local_diagonal(geometry, derivative, quad_weights):
    stiff_diag = jnp.sum(derivative * derivative * quad_weights[:, None], axis=0)
    along_x = (
        quad_weights[:, None, None] * quad_weights[None, :, None] * stiff_diag[None, None, :]
    )[..., None]
    along_y = (
        quad_weights[:, None, None] * stiff_diag[None, :, None] * quad_weights[None, None, :]
    )[..., None]
    along_z = (
        stiff_diag[:, None, None] * quad_weights[None, :, None] * quad_weights[None, None, :]
    )[..., None]
    return (
        along_x * geometry[0]
        + along_y * geometry[1]
        + along_z * geometry[2]
        + cube_weights(quad_weights) * geometry[3]
    )


def pair_faces(field_data, axis, stride, has_next):
    has_prev = jnp.roll(has_next, stride)
    low_face = lax.index_in_dim(field_data, 0, axis, keepdims=True)
    high_face = lax.index_in_dim(field_data, 7, axis, keepdims=True)
    next_low = jnp.roll(low_face, -stride, axis=-1)
    prev_high = jnp.roll(high_face, stride, axis=-1)
    new_high = jnp.where(has_next, high_face + next_low, high_face)
    new_low = jnp.where(has_prev, prev_high + low_face, low_face)
    return jnp.concatenate([new_low, lax.slice_in_dim(field_data, 1, 7, axis=axis), new_high], axis)


def direct_sum(field_data):
    elem_count = field_data.shape[-1]
    layer_size = EX * EY
    element_ids = jnp.arange(elem_count, dtype=jnp.int32)
    field_data = pair_faces(field_data, 3, 1, element_ids % EX < EX - 1)
    field_data = pair_faces(field_data, 2, EX, element_ids // EX % EY < EY - 1)
    field_data = pair_faces(field_data, 1, layer_size, element_ids < elem_count - layer_size)
    bottom = field_data[:, 0, :, :, :layer_size]
    top_face = field_data[:, 7, :, :, elem_count - layer_size :]
    face_pair = jnp.stack([bottom, top_face], 0).reshape(2, -1)
    padded = with_halo(face_pair, (("dom", 0),), 1)
    bottom = bottom + padded[0].reshape(bottom.shape)
    top_face = top_face + padded[3].reshape(top_face.shape)
    low_slab = jnp.concatenate([bottom, field_data[:, 0, :, :, layer_size:]], -1)
    high_slab = jnp.concatenate([field_data[:, 7, :, :, : elem_count - layer_size], top_face], -1)
    return jnp.concatenate([low_slab[:, None], field_data[:, 1:7], high_slab[:, None]], 1)


def body(donor_fields, interp_weights, donor_owner, donor_element, geometry, wall_flag, forcing):
    derivative, quad_weights = gll_tables()
    rec_count = donor_element.shape[0]
    elem_count = geometry.shape[1]
    slot_count = rec_count // 2
    field_count = donor_fields.shape[0]
    my_slab = lax.axis_index("dom")
    owner_dom = donor_owner[:, 0]
    distance = owner_dom - my_slab + 2
    onehot = (distance[:, None] == jnp.arange(5, dtype=jnp.int32)[None, :]).astype(jnp.int32)
    position = jnp.sum((jnp.cumsum(onehot, axis=0) - onehot) * onehot, axis=1)
    slot_index = distance * slot_count + position
    source_row = (
        jnp.zeros((5 * slot_count,), jnp.int32)
        .at[slot_index]
        .set(jnp.arange(rec_count, dtype=jnp.int32))
    )
    packed = jnp.concatenate(
        [interp_weights.reshape(24, rec_count), donor_element.astype(jnp.float32)[None, :]], 0
    )
    outgoing = jnp.take(packed, source_row, axis=1)
    crossed = swapped(outgoing, "mesh", 0)
    answers = []
    for slot in range(5):
        piece = crossed[:, slot * slot_count : (slot + 1) * slot_count]
        if slot != 2:
            piece = from_behind(piece, "dom", slot - 2)
        lookups = piece[24].astype(jnp.int32)
        count = lookups.shape[0]
        gathered = jnp.take(donor_fields, lookups, axis=2).reshape(field_count, 64, 8, count)
        reduced = jnp.sum(gathered * piece[0:8][None, None], axis=2).reshape(
            field_count, 8, 8, count
        )
        reduced = jnp.sum(reduced * piece[8:16][None, None], axis=2)
        answers.append(jnp.sum(reduced * piece[16:24][None], axis=1))
    returned = []
    for slot in range(5):
        if slot == 2:
            returned.append(answers[slot])
        else:
            returned.append(from_behind(answers[slot], "dom", 2 - slot))
    answered = swapped(jnp.concatenate(returned, 1), "mesh", 0)
    interface_values = jnp.take(answered, slot_index, axis=1)
    flat_shape = (8, 8, 8, elem_count)
    weights_cube = cube_weights(quad_weights)
    column_count = EZ_DEV * EY
    received = interface_values[0].reshape(2, column_count, 64)
    side_values = jnp.transpose(received, (0, 2, 1)).reshape(2, 8, 8, column_count, 1)
    side_values = jnp.broadcast_to(side_values, (2, 8, 8, column_count, EX)).reshape(
        2, 8, 8, elem_count
    )
    element_ids = jnp.arange(elem_count, dtype=jnp.int32)
    x_index = element_ids % EX
    y_index = element_ids // EX % EY
    z_index = element_ids // (EX * EY)
    node_ids = jnp.arange(8, dtype=jnp.int32)
    low_x = (node_ids[None, None, :, None] == 0) & (x_index[None, None, None, :] == 0)
    high_x = (node_ids[None, None, :, None] == 7) & (x_index[None, None, None, :] == EX - 1)
    rec_value = jnp.where(
        low_x, side_values[0][:, :, None, :], jnp.where(high_x, side_values[1][:, :, None, :], 0.0)
    )
    rec_mark = jnp.where(low_x | high_x, 1.0, 0.0) * jnp.ones(flat_shape, jnp.float32)
    wall_bits = wall_flag.astype(jnp.float32)
    wall_column = z_index * EX + x_index
    wall_low = jnp.take(wall_bits[0], wall_column)
    wall_high = jnp.take(wall_bits[1], wall_column)
    low_y = (node_ids[None, :, None, None] == 0) & (y_index[None, None, None, :] == 0)
    high_y = (node_ids[None, :, None, None] == 7) & (y_index[None, None, None, :] == EY - 1)
    wall_mark = jnp.where(low_y, wall_low, 0.0) + jnp.where(high_y, wall_high, 0.0)
    wall_mark = wall_mark * jnp.ones(flat_shape, jnp.float32)
    diag_local = local_diagonal(geometry, derivative, quad_weights)
    unit_field = jnp.ones(flat_shape, jnp.float32)
    summed = direct_sum(jnp.stack([rec_value, rec_mark, wall_mark, unit_field, diag_local], 0))
    free_mask = 1.0 - jnp.minimum(summed[1] + summed[2], 1.0)
    boundary = summed[0] / jnp.maximum(summed[1], 1.0)
    multiplicity = summed[3]
    inverse = free_mask / summed[4]

    def apply_operator(vector):
        local_term = local_operator(vector, geometry, derivative, quad_weights)
        return free_mask * direct_sum(local_term[None])[0]

    def paired_dots(residual_now, precond, operator_image):
        return in_one(
            (
                jnp.sum(residual_now * precond / multiplicity),
                jnp.sum(precond * operator_image / multiplicity),
            ),
            "dom",
        )

    source = forcing.reshape(flat_shape)
    loaded = weights_cube * geometry[3] * source - local_operator(
        boundary, geometry, derivative, quad_weights
    )
    rhs = free_mask * direct_sum(loaded[None])[0]
    solution = jnp.zeros(flat_shape, jnp.float32)
    residual_now = rhs
    precond = inverse * residual_now
    operator_image = apply_operator(precond)
    precond_norm, curvature = paired_dots(residual_now, precond, operator_image)
    step_length = precond_norm / curvature
    direction = precond
    direction_image = operator_image
    for iteration in range(ITERS):
        solution = solution + step_length * direction
        residual_now = residual_now - step_length * direction_image
        if iteration + 1 < ITERS:
            precond = inverse * residual_now
            operator_image = apply_operator(precond)
            norm_next, curvature = paired_dots(residual_now, precond, operator_image)
            beta_ratio = norm_next / precond_norm
            step_length = norm_next / (curvature - beta_ratio * norm_next / step_length)
            direction = precond + beta_ratio * direction
            direction_image = operator_image + beta_ratio * direction_image
            precond_norm = norm_next
    velocity = (boundary + solution).reshape(-1, elem_count)
    return (velocity, residual_now.reshape(-1, elem_count), interface_values)


def solution(mesh):
    in_specs = (
        P(None, None, ("mesh", "dom")),
        P(None, None, ("mesh", "dom")),
        P(("mesh", "dom"), None),
        P(("mesh", "dom")),
        P(None, ("mesh", "dom")),
        P(None, ("mesh", "dom")),
        P(None, ("mesh", "dom")),
    )
    out_specs = (P(None, ("mesh", "dom")), P(None, ("mesh", "dom")), P(None, ("mesh", "dom")))
    return jax.shard_map(body, mesh=mesh, in_specs=in_specs, out_specs=out_specs, check_vma=False)
```

profile of v0, /device:TPU:0, one launch (start us, length us, event | category | flops | bytes accessed | tf_op | source)
XLA Modules:
  0.0 528.5 jit_solution(16142488344229456810)
XLA Ops:
  4.1 8.1 %scatter_custom_fusion = s32[5120]{0:T(1024)S(1)} fusion(s32[2048]{0:T(1024)S(1)} %bitcast.440, s32[2048]{0:T(1024)S(1)} %iota.92, s32[]{:T(128)} %constant.173.clone.1), kind=kCustom, calls=%fused_computation.310 | custom fusion | bytes 20484 | tf_op jit(solution)/shard_map/scatter | solution.py:181
  14.2 17.7 %gather_fusion = f32[5120,25]{1,0:T(8,128)} fusion(f32[25,2048]{0,1:T(8,128)S(1)} %copy.277, s32[5120]{0:T(1024)S(1)} %fusion.113), kind=kCustom, calls=%fused_computation.5 | custom fusion | bytes 1044480 | tf_op jit(solution)/shard_map/jit(_take)/gather | solution.py:186
  72.8 13.6 %gather_fusion.6 = f32[1024,5,512]{2,1,0:T(8,128)} fusion(f32[5,512,128]{1,0,2:T(8,128)S(1)} %copy.279, s32[1024]{0:T(1024)S(1)} %fusion.120), kind=kCustom, calls=%fused_computation.4.clone | custom fusion | bytes 20975616 | tf_op jit(solution)/shard_map/jit(_take)/gather | solution.py:195
  86.4 12.3 %select_bitcast_fusion = f32[5,512,1024]{1,0,2:T(8,128)} fusion(f32[1024,5,512]{2,1,0:T(8,128)} %gather_fusion.6, pred[1024]{0:T(1024)(128)(4,1)S(1)} %compare_and_fusion.1), kind=kLoop, calls=%fused_computation.8 | loop fusion | flops 2621440 | bytes 20972544 | tf_op jit(solution)/shard_map/jit(_take)/select_n | solution.py:195
  98.7 14.7 %copy.288 = f32[5,512,1024]{2,1,0:T(8,128)} copy(f32[5,512,1024]{1,0,2:T(8,128)} %select_bitcast_fusion) | data formatting | bytes 20971520 | tf_op jit(solution)/shard_map/jit(_take)/select_n | solution.py:195
  113.4 7.8 %fusion = f32[5,64,1024]{2,1,0:T(8,128)S(1)} fusion(f32[5,512,1024]{2,1,0:T(8,128)} %copy.288, f32[8,1024]{1,0:T(8,128)S(1)} %get-tuple-element.93), kind=kLoop, calls=%fused_computation.14 | loop fusion | flops 4915200 | bytes 11829248 | tf_op jit(solution)/shard_map/reduce_sum | solution.py:196
  123.6 13.6 %gather_fusion.5 = f32[1024,5,512]{2,1,0:T(8,128)} fusion(f32[5,512,128]{1,0,2:T(8,128)S(1)} %copy.279, s32[1024]{0:T(1024)S(1)} %get-tuple-element.153), kind=kCustom, calls=%fused_computation.3.clone | custom fusion | bytes 20975616 | tf_op jit(solution)/shard_map/jit(_take)/gather | solution.py:195
  137.2 12.3 %select_bitcast_fusion.1 = f32[5,512,1024]{1,0,2:T(8,128)} fusion(f32[1024,5,512]{2,1,0:T(8,128)} %gather_fusion.5, pred[1024]{0:T(1024)(128)(4,1)S(1)} %compare_and_fusion.2), kind=kLoop, calls=%fused_computation.9 | loop fusion | flops 2621440 | bytes 20972544 | tf_op jit(solution)/shard_map/jit(_take)/select_n | solution.py:195
  149.5 14.7 %copy.286 = f32[5,512,1024]{2,1,0:T(8,128)} copy(f32[5,512,1024]{1,0,2:T(8,128)} %select_bitcast_fusion.1) | data formatting | bytes 20971520 | tf_op jit(solution)/shard_map/jit(_take)/select_n | solution.py:195
  164.1 7.8 %fusion.1 = f32[5,64,1024]{2,1,0:T(8,128)S(1)} fusion(f32[5,512,1024]{2,1,0:T(8,128)} %copy.286, f32[8,1024]{1,0:T(8,128)S(1)} %get-tuple-element.96), kind=kLoop, calls=%fused_computation.16 | loop fusion | flops 4915200 | bytes 11829248 | tf_op jit(solution)/shard_map/reduce_sum | solution.py:196
  173.9 13.6 %gather_fusion.4 = f32[1024,5,512]{2,1,0:T(8,128)} fusion(f32[5,512,128]{1,0,2:T(8,128)S(1)} %copy.279, s32[1024]{0:T(1024)S(1)} %get-tuple-element.152), kind=kCustom, calls=%fused_computation.2.clone | custom fusion | bytes 20975616 | tf_op jit(solution)/shard_map/jit(_take)/gather | solution.py:195
  187.5 12.3 %select_bitcast_fusion.2 = f32[5,512,1024]{1,0,2:T(8,128)} fusion(f32[1024,5,512]{2,1,0:T(8,128)} %gather_fusion.4, pred[1024]{0:T(1024)(128)(4,1)S(1)} %compare_and_fusion.3), kind=kLoop, calls=%fused_computation.10 | loop fusion | flops 2621440 | bytes 20972544 | tf_op jit(solution)/shard_map/jit(_take)/select_n | solution.py:195
  199.8 14.6 %copy.284 = f32[5,512,1024]{2,1,0:T(8,128)} copy(f32[5,512,1024]{1,0,2:T(8,128)} %select_bitcast_fusion.2) | data formatting | bytes 20971520 | tf_op jit(solution)/shard_map/jit(_take)/select_n | solution.py:195
  214.5 13.6 %gather_fusion.3 = f32[1024,5,512]{2,1,0:T(8,128)} fusion(f32[5,512,128]{1,0,2:T(8,128)S(1)} %copy.279, s32[1024]{0:T(1024)S(1)} %get-tuple-element.151), kind=kCustom, calls=%fused_computation.1.clone | custom fusion | bytes 20975616 | tf_op jit(solution)/shard_map/jit(_take)/gather | solution.py:195
  228.1 12.3 %select_bitcast_fusion.3 = f32[5,512,1024]{1,0,2:T(8,128)} fusion(f32[1024,5,512]{2,1,0:T(8,128)} %gather_fusion.3, pred[1024]{0:T(1024)(128)(4,1)S(1)} %compare_and_fusion.4), kind=kLoop, calls=%fused_computation.11 | loop fusion | flops 2621440 | bytes 20972544 | tf_op jit(solution)/shard_map/jit(_take)/select_n | solution.py:195
  240.4 14.7 %copy.282 = f32[5,512,1024]{2,1,0:T(8,128)} copy(f32[5,512,1024]{1,0,2:T(8,128)} %select_bitcast_fusion.3) | data formatting | bytes 20971520 | tf_op jit(solution)/shard_map/jit(_take)/select_n | solution.py:195
  255.1 7.8 %fusion.3 = f32[5,64,1024]{2,1,0:T(8,128)S(1)} fusion(f32[5,512,1024]{2,1,0:T(8,128)} %copy.282, f32[8,1024]{1,0:T(8,128)S(1)} %get-tuple-element.99), kind=kLoop, calls=%fused_computation.20 | loop fusion | flops 4915200 | bytes 11829248 | tf_op jit(solution)/shard_map/reduce_sum | solution.py:196
  268.2 13.6 %gather_fusion.2 = f32[1024,5,512]{2,1,0:T(8,128)} fusion(f32[5,512,128]{1,0,2:T(8,128)S(1)} %copy.279, s32[1024]{0:T(1024)S(1)} %get-tuple-element.150), kind=kCustom, calls=%fused_computation.clone | custom fusion | bytes 20975616 | tf_op jit(solution)/shard_map/jit(_take)/gather | solution.py:195
  281.8 12.3 %select_bitcast_fusion.4 = f32[5,512,1024]{1,0,2:T(8,128)} fusion(f32[1024,5,512]{2,1,0:T(8,128)} %gather_fusion.2, pred[1024]{0:T(1024)(128)(4,1)S(1)} %compare_and_fusion.5), kind=kLoop, calls=%fused_computation.12 | loop fusion | flops 2621440 | bytes 20972544 | tf_op jit(solution)/shard_map/jit(_take)/select_n | solution.py:195
  294.1 14.7 %copy.280 = f32[5,512,1024]{2,1,0:T(8,128)} copy(f32[5,512,1024]{1,0,2:T(8,128)} %select_bitcast_fusion.4) | data formatting | bytes 20971520 | tf_op jit(solution)/shard_map/jit(_take)/select_n | solution.py:195
  399.2 36.9 %all_to_all.18 = f32[64,1,2]{2,1,0:T(1,128)S(1)} all-to-all(f32[64,1,2]{2,1,0:T(1,128)S(1)} %broadcast_in_dim.299), channel_id=1, replica_groups=mesh['mesh'=2,'dom'=64] {'dom'}, dimensions={0} | all-to-all | bytes 1024 | tf_op jit(solution)/shard_map/all_to_all | solution.py:47
  454.7 22.3 %all_to_all.19 = f32[64,1,2]{2,1,0:T(1,128)S(1)} all-to-all(f32[64,1,2]{2,1,0:T(1,128)S(1)} %broadcast_in_dim.301), channel_id=1, replica_groups=mesh['mesh'=2,'dom'=64] {'dom'}, dimensions={0} | all-to-all | bytes 1024 | tf_op jit(solution)/shard_map/all_to_all | solution.py:47
  499.7 12.6 %all-to-all-start.2 = ((f32[64,1,2]{2,1,0:T(1,128)}), f32[64,1,2]{2,1,0:T(1,128)S(1)}, u32[]{:S(2)}, u32[]{:S(2)}) async-start(f32[64,1,2]{2,1,0:T(1,128)} %broadcast_in_dim.303), calls=%async_computation.2 | async-start | bytes 65536 | tf_op jit(solution)/shard_map/all_to_all | solution.py:47
  513.2 8.6 %all-to-all-done.2 = f32[64,1,2]{2,1,0:T(1,128)S(1)} async-done(((f32[64,1,2]{2,1,0:T(1,128)}), f32[64,1,2]{2,1,0:T(1,128)S(1)}, u32[]{:S(2)}, u32[]{:S(2)}) %all-to-all-start.2) | async-done | bytes 544 | tf_op jit(solution)/shard_map/all_to_all | solution.py:47
  (267 shorter events, 184.6 us)
Async XLA Ops:
  37.9 14.6 %collective-permute-start = (f32[25,5120]{1,0:T(8,128)}, f32[25,5120]{1,0:T(8,128)S(1)}, u32[]{:S(2)}, u32[]{:S(2)}) collective-permute-start(f32[25,5120]{1,0:T(8,128)} %copy.278), channel_id=1, source_target_pairs={{0,64},{64,0},{1,65},{65,1},{2,66},{66,2},{3,67},{67,3},{4,68},{68... | collective-permute-start | bytes 1536008 | tf_op jit(solution)/shard_map/ppermute | solution.py:36
  52.6 10.4 %collective-permute-start.7 = (f32[25,1024]{1,0:T(8,128)S(1)}, f32[25,1024]{1,0:T(8,128)S(1)}, u32[]{:S(2)}, u32[]{:S(2)}) collective-permute-start(f32[25,1024]{1,0:T(8,128)S(1)} %get-tuple-element.57), channel_id=1, source_target_pairs={{0,2},{1,3},{2,4},{3,5},{4,6},{5,7},{6,8},{7,9},{8,10},{9,11},{10,... | collective-permute-start | bytes 307208 | tf_op jit(solution)/shard_map/ppermute | solution.py:42
  57.8 6.2 %collective-permute-start.5 = (f32[25,1024]{1,0:T(8,128)S(1)}, f32[25,1024]{1,0:T(8,128)S(1)}, u32[]{:S(2)}, u32[]{:S(2)}) collective-permute-start(f32[25,1024]{1,0:T(8,128)S(1)} %get-tuple-element.58), channel_id=1, source_target_pairs={{0,1},{1,2},{2,3},{3,4},{4,5},{5,6},{6,7},{7,8},{8,9},{9,10},{10,1... | collective-permute-start | bytes 307208 | tf_op jit(solution)/shard_map/ppermute | solution.py:42
  60.4 7.2 %collective-permute-start.3 = (f32[25,1024]{1,0:T(8,128)S(1)}, f32[25,1024]{1,0:T(8,128)S(1)}, u32[]{:S(2)}, u32[]{:S(2)}) collective-permute-start(f32[25,1024]{1,0:T(8,128)S(1)} %get-tuple-element.59), channel_id=1, source_target_pairs={{1,0},{2,1},{3,2},{4,3},{5,4},{6,5},{7,6},{8,7},{9,8},{10,9},{11,1... | collective-permute-start | bytes 307208 | tf_op jit(solution)/shard_map/ppermute | solution.py:42
  61.7 11.1 %collective-permute-start.1 = (f32[25,1024]{1,0:T(8,128)S(1)}, f32[25,1024]{1,0:T(8,128)S(1)}, u32[]{:S(2)}, u32[]{:S(2)}) collective-permute-start(f32[25,1024]{1,0:T(8,128)S(1)} %get-tuple-element.60), channel_id=1, source_target_pairs={{2,0},{3,1},{4,2},{5,3},{6,4},{7,5},{8,6},{9,7},{10,8},{11,9},{12,... | collective-permute-start | bytes 307208 | tf_op jit(solution)/shard_map/ppermute | solution.py:42
  121.7 209.8 %collective-permute-start.8 = (f32[5,1024]{1,0:T(8,128)S(1)}, f32[5,1024]{1,0:T(8,128)S(1)}, u32[]{:S(2)}, u32[]{:S(2)}) collective-permute-start(f32[5,1024]{1,0:T(8,128)S(1)} %multiply_reduce_fusion), channel_id=1, source_target_pairs={{2,0},{3,1},{4,2},{5,3},{6,4},{7,5},{8,6},{9,7},{10,8},{11,9},{12,... | collective-permute-start | bytes 61448 | tf_op jit(solution)/shard_map/ppermute | solution.py:42
  172.5 159.1 %collective-permute-start.6 = (f32[5,1024]{1,0:T(8,128)S(1)}, f32[5,1024]{1,0:T(8,128)S(1)}, u32[]{:S(2)}, u32[]{:S(2)}) collective-permute-start(f32[5,1024]{1,0:T(8,128)S(1)} %multiply_reduce_fusion.1), channel_id=1, source_target_pairs={{1,0},{2,1},{3,2},{4,3},{5,4},{6,5},{7,6},{8,7},{9,8},{10,9},{11,1... | collective-permute-start | bytes 61448 | tf_op jit(solution)/shard_map/ppermute | solution.py:42
  263.4 68.1 %collective-permute-start.4 = (f32[5,1024]{1,0:T(8,128)S(1)}, f32[5,1024]{1,0:T(8,128)S(1)}, u32[]{:S(2)}, u32[]{:S(2)}) collective-permute-start(f32[5,1024]{1,0:T(8,128)S(1)} %multiply_reduce_fusion.3), channel_id=1, source_target_pairs={{0,1},{1,2},{2,3},{3,4},{4,5},{5,6},{6,7},{7,8},{8,9},{9,10},{10,1... | collective-permute-start | bytes 61448 | tf_op jit(solution)/shard_map/ppermute | solution.py:42
  317.1 14.4 %collective-permute-start.2 = (f32[5,1024]{1,0:T(8,128)S(1)}, f32[5,1024]{1,0:T(8,128)S(1)}, u32[]{:S(2)}, u32[]{:S(2)}) collective-permute-start(f32[5,1024]{1,0:T(8,128)S(1)} %multiply_reduce_fusion.4), channel_id=1, source_target_pairs={{0,2},{1,3},{2,4},{3,5},{4,6},{5,7},{6,8},{7,9},{8,10},{9,11},{10,... | collective-permute-start | bytes 61448 | tf_op jit(solution)/shard_map/ppermute | solution.py:42
  331.6 1.9 collective-permute-start.9
  348.6 8.6 %collective-permute-start.10 = (f32[1,40960]{1,0:T(1,128)S(1)}, f32[1,40960]{1,0:T(1,128)S(1)}, u32[]{:S(2)}, u32[]{:S(2)}) collective-permute-start(f32[1,40960]{1,0:T(1,128)S(1)} %bitcast.409), channel_id=1, source_target_pairs={{0,1},{1,2},{2,3},{3,4},{4,5},{5,6},{6,7},{7,8},{8,9},{9,10},{10,1... | collective-permute-start | bytes 491528 | tf_op jit(solution)/shard_map/ppermute | solution.py:23
  357.3 8.0 %collective-permute-start.11 = (f32[1,40960]{1,0:T(1,128)S(1)}, f32[1,40960]{1,0:T(1,128)S(1)}, u32[]{:S(2)}, u32[]{:S(2)}) collective-permute-start(f32[1,40960]{1,0:T(1,128)S(1)} %bitcast.412), channel_id=1, source_target_pairs={{1,0},{2,1},{3,2},{4,3},{5,4},{6,5},{7,6},{8,7},{9,8},{10,9},{11,1... | collective-permute-start | bytes 491528 | tf_op jit(solution)/shard_map/ppermute | solution.py:24
  369.8 5.2 collective-permute-start.12
  375.0 6.1 %collective-permute-start.13 = (f32[1,8192]{1,0:T(1,128)S(1)}, f32[1,8192]{1,0:T(1,128)S(1)}, u32[]{:S(2)}, u32[]{:S(2)}) collective-permute-start(f32[1,8192]{1,0:T(1,128)S(1)} %bitcast.442), channel_id=1, source_target_pairs={{1,0},{2,1},{3,2},{4,3},{5,4},{6,5},{7,6},{8,7},{9,8},{10,9},{11,1... | collective-permute-start | bytes 98312 | tf_op jit(solution)/shard_map/ppermute | solution.py:24
  381.2 100.7 %copy-start.2 = (f32[1,8,8,8,128]{4,3,2,1,0:T(8,128)}, f32[1,8,8,8,128]{4,3,2,1,0:T(8,128)S(1)}, u32[]{:S(2)}) copy-start(f32[1,8,8,8,128]{4,3,2,1,0:T(8,128)S(1)} %get-tuple-element.41) | copy-start | bytes 786436
  384.9 6.0 %collective-permute-start.14 = (f32[1,8192]{1,0:T(1,128)S(1)}, f32[1,8192]{1,0:T(1,128)S(1)}, u32[]{:S(2)}, u32[]{:S(2)}) collective-permute-start(f32[1,8192]{1,0:T(1,128)S(1)} %bitcast.416), channel_id=1, source_target_pairs={{0,1},{1,2},{2,3},{3,4},{4,5},{5,6},{6,7},{7,8},{8,9},{9,10},{10,1... | collective-permute-start | bytes 98312 | tf_op jit(solution)/shard_map/ppermute | solution.py:23
  391.0 6.1 %collective-permute-start.15 = (f32[1,8192]{1,0:T(1,128)S(1)}, f32[1,8192]{1,0:T(1,128)S(1)}, u32[]{:S(2)}, u32[]{:S(2)}) collective-permute-start(f32[1,8192]{1,0:T(1,128)S(1)} %bitcast.443), channel_id=1, source_target_pairs={{1,0},{2,1},{3,2},{4,3},{5,4},{6,5},{7,6},{8,7},{9,8},{10,9},{11,1... | collective-permute-start | bytes 98312 | tf_op jit(solution)/shard_map/ppermute | solution.py:24
  441.8 4.1 collective-permute-start.16
  445.9 6.1 %collective-permute-start.17 = (f32[1,8192]{1,0:T(1,128)S(1)}, f32[1,8192]{1,0:T(1,128)S(1)}, u32[]{:S(2)}, u32[]{:S(2)}) collective-permute-start(f32[1,8192]{1,0:T(1,128)S(1)} %bitcast.444), channel_id=1, source_target_pairs={{1,0},{2,1},{3,2},{4,3},{5,4},{6,5},{7,6},{8,7},{9,8},{10,9},{11,1... | collective-permute-start | bytes 98312 | tf_op jit(solution)/shard_map/ppermute | solution.py:24
  486.7 4.0 collective-permute-start.18
  490.7 6.1 %collective-permute-start.19 = (f32[1,8192]{1,0:T(1,128)S(1)}, f32[1,8192]{1,0:T(1,128)S(1)}, u32[]{:S(2)}, u32[]{:S(2)}) collective-permute-start(f32[1,8192]{1,0:T(1,128)S(1)} %bitcast.445), channel_id=1, source_target_pairs={{1,0},{2,1},{3,2},{4,3},{5,4},{6,5},{7,6},{8,7},{9,8},{10,9},{11,1... | collective-permute-start | bytes 98312 | tf_op jit(solution)/shard_map/ppermute | solution.py:24
  497.7 29.7 %copy-start.1 = (f32[1,8,8,8,128]{4,3,2,1,0:T(8,128)S(1)}, f32[1,8,8,8,128]{4,3,2,1,0:T(8,128)}, u32[]{:S(2)}) copy-start(f32[1,8,8,8,128]{4,3,2,1,0:T(8,128)} %copy-done) | copy-start | bytes 786436
  497.7 29.7 %copy-start.3 = (f32[1,8,8,8,128]{4,3,2,1,0:T(8,128)S(1)}, f32[1,8,8,8,128]{4,3,2,1,0:T(8,128)}, u32[]{:S(2)}) copy-start(f32[1,8,8,8,128]{4,3,2,1,0:T(8,128)} %copy-done.2) | copy-start | bytes 786436
  499.7 22.2 %all-to-all-start.2 = ((f32[64,1,2]{2,1,0:T(1,128)}), f32[64,1,2]{2,1,0:T(1,128)S(1)}, u32[]{:S(2)}, u32[]{:S(2)}) async-start(f32[64,1,2]{2,1,0:T(1,128)} %broadcast_in_dim.303), calls=%async_computation.2 | async-start | bytes 65536 | tf_op jit(solution)/shard_map/all_to_all | solution.py:47
  (11 other events, 66.4 us)
where the time goes:
time: 539 us; the launch traced here: 529 us
  local copies, waits for them, and re-layouts  189 us (35%)
  other arithmetic  141 us (26%)
  starting transfers between devices  62.1 us (12%)
  blocking collectives  59.2 us (11%)
  waiting for transfers between devices  55.5 us (10%)
  between operations  11.5 us (2%)
  matrix products  10.3 us (2%)
    select_n x5, local copies, waits for them, and re-layouts, body(): jnp.take(donor_fields, lookups, axis=2).reshape(field_count, 64, 8, count)  73.3 us
    gather x5, local copies, waits for them, and re-layouts, body(): jnp.take(donor_fields, lookups, axis=2).reshape(field_count, 64, 8, count)  68 us
    select_n x5, other arithmetic, body(): jnp.take(donor_fields, lookups, axis=2).reshape(field_count, 64, 8, count)  61.5 us
    all_to_all x2, blocking collectives, from_everyone(): lax.all_to_all(jnp.broadcast_to(value[None], (length, *value.shape)), axi...  59.2 us
    reduce_sum x5, other arithmetic, body(): jnp.sum(gathered * piece[0:8][None, None], axis=2)  39.1 us
    ppermute x5, waiting for transfers between devices, with_halo(): after = lax.ppermute(leading, axis, down)  25.8 us
    ppermute x8, starting transfers between devices, from_behind(): lax.ppermute(value, axis, [(source, source + steps) for source in range(l...  24.5 us
    ppermute x5, starting transfers between devices, with_halo(): before = lax.ppermute(last, axis, up)  17.9 us
  transfers between devices with their start and end apart: 21, of which 15 were waited for; matrix products, arithmetic and copies ran while one was open for 40% of the time, Pallas kernels for 0%

commit v1 on v0

v1 whole, which is shorter than its diff:
```python
import functools

import jax
import jax.numpy as jnp
import numpy as np
from jax import lax
from jax.experimental import pallas as pl
from jax.experimental.pallas import tpu as pltpu
from jax.sharding import PartitionSpec as P

HIGHEST = lax.Precision.HIGHEST
N_DOM = 64
N_REC = 2048
CAP = 1024
FIELDS = 5
LANES = 128
BLOCK = 256
ALIGNED = [[4 * g + t for t in range(4)] for g in range(16)]
SHIFTED = [[(4 * g + 2 + t) % N_DOM for t in range(4)] for g in range(16)]
UP = [(i, i + 1) for i in range(N_DOM - 1)]
DOWN = [(i + 1, i) for i in range(N_DOM - 1)]


def legendre_pair(values, degree):
    previous = values * 0.0 + 1.0
    current = values * 1.0
    for order in range(2, degree + 1):
        previous, current = (
            current,
            ((2 * order - 1) * values * current - (order - 1) * previous) / order,
        )
    return current, previous


def gll_tables():
    degree = 7
    count = degree + 1
    nodes = np.cos(np.pi * np.arange(count) / degree)
    for _ in range(80):
        top, lower = legendre_pair(nodes, degree)
        nodes = nodes - (nodes * top - lower) / (count * top)
    nodes = np.sort(nodes)
    top, lower = legendre_pair(nodes, degree)
    weights = 2.0 / (degree * count * top * top)
    identity = np.eye(count)
    spacing = nodes[:, None] - nodes[None, :] + identity
    derivative = top[:, None] / (top[None, :] * spacing) * (1.0 - identity)
    derivative[0, 0] = -degree * count / 4.0
    derivative[degree, degree] = degree * count / 4.0
    return nodes, weights, derivative


NODES, WEIGHTS, DERIV = gll_tables()
STIFF = DERIV.T @ (WEIGHTS[:, None] * DERIV)
STIFF = 0.5 * (STIFF + STIFF.T)
BARY = np.array([1.0 / np.prod([NODES[i] - NODES[j] for j in range(8) if j != i]) for i in range(8)])


def x_matrix():
    out = np.zeros((512, 256))
    for k in range(8):
        for j in range(8):
            row = (k * 8 + j) * 8
            col = row % 256
            out[row : row + 8, col : col + 8] = WEIGHTS[k] * WEIGHTS[j] * STIFF
    return out.astype(np.float32)


def iota(shape, dim):
    return lax.broadcasted_iota(jnp.int32, shape, dim)


def w_column():
    row = iota((8, LANES), 0)
    out = jnp.full((8, LANES), float(WEIGHTS[0]), jnp.float32)
    for i in range(1, 8):
        out = jnp.where(row == i, float(WEIGHTS[i]), out)
    return out


def s_column():
    row = iota((8, LANES), 0)
    out = jnp.full((8, LANES), float(STIFF[0, 0]), jnp.float32)
    for i in range(1, 8):
        out = jnp.where(row == i, float(STIFF[i, i]), out)
    return out


def sum_xy(ref, planes):
    rows = planes * 8
    lane = iota((rows, LANES), 1)
    low = ref[pl.ds(0, rows, stride=8), :]
    high = ref[pl.ds(7, rows, stride=8), :]
    ref[pl.ds(7, rows, stride=8), :] = high + jnp.where(
        lane % 8 < 7, pltpu.roll(low, LANES - 1, 1), 0.0
    )
    ref[pl.ds(0, rows, stride=8), :] = low + jnp.where(lane % 8 > 0, pltpu.roll(high, 1, 1), 0.0)
    lane = iota((8, LANES), 1)
    for k in range(planes):
        low = ref[k * 64 : k * 64 + 8, :]
        high = ref[k * 64 + 56 : k * 64 + 64, :]
        ref[k * 64 + 56 : k * 64 + 64, :] = high + jnp.where(
            lane < 120, pltpu.roll(low, LANES - 8, 1), 0.0
        )
        ref[k * 64 : k * 64 + 8, :] = low + jnp.where(lane >= 8, pltpu.roll(high, 8, 1), 0.0)


def apply_local(v_ref, geometry, xmat_ref, out_ref, planes, dot_with_v=False):
    wcol = w_column()
    gx = geometry[0:1, :]
    gyw = geometry[1:2, :] * wcol
    gzw = geometry[2:3, :] * wcol
    gmw = geometry[3:4, :] * wcol
    total = jnp.zeros((8, LANES), jnp.float32)
    if len(planes) == 8:
        along_x = [
            lax.dot(
                xmat_ref[256 * h : 256 * h + 256, :],
                v_ref[256 * h : 256 * h + 256, :],
                precision=HIGHEST,
                preferred_element_type=jnp.float32,
            )
            for h in range(2)
        ]
        for h in range(2):
            out_ref[256 * h : 256 * h + 256, :] = along_x[h]
    else:
        for at, k in enumerate(planes):
            h = k // 4
            out_ref[at * 64 : at * 64 + 64, :] = lax.dot(
                xmat_ref[k * 64 : k * 64 + 64, :],
                v_ref[256 * h : 256 * h + 256, :],
                precision=HIGHEST,
                preferred_element_type=jnp.float32,
            )
    for at, k in enumerate(planes):
        plane = [v_ref[(k * 8 + j) * 8 : (k * 8 + j) * 8 + 8, :] for j in range(8)]
        for j in range(8):
            ysum = plane[0] * float(STIFF[j, 0] * WEIGHTS[k])
            for jj in range(1, 8):
                ysum = ysum + plane[jj] * float(STIFF[j, jj] * WEIGHTS[k])
            zsum = None
            for kk in range(8):
                term = v_ref[(kk * 8 + j) * 8 : (kk * 8 + j) * 8 + 8, :] * float(
                    STIFF[k, kk] * WEIGHTS[j]
                )
                zsum = term if zsum is None else zsum + term
            row = (at * 8 + j) * 8
            value = (
                out_ref[row : row + 8, :] * gx
                + gyw * ysum
                + gzw * zsum
                + gmw * (plane[j] * float(WEIGHTS[k] * WEIGHTS[j]))
            )
            out_ref[row : row + 8, :] = value
            if dot_with_v:
                total = total + value * plane[j]
    return total


def lane_value(value, at):
    return jnp.where(iota((1, LANES), 1) == at, value, 0.0)


def route_kernel(place_ref, weights_ref, owner_ref, element_ref, near_ref, far_ref, moves_ref, slots_ref):
    q = place_ref[0]
    width = N_REC
    lane = iota((8, width), 1)
    row = iota((8, width), 0)
    distance = owner_ref[...] - q + 2
    mine = distance == row
    count = mine.astype(jnp.int32)
    step = 1
    while step < width:
        count = count + jnp.where(lane >= step, pltpu.roll(count, step, 1), 0)
        step *= 2
    moves = jnp.where(mine, lane - (count - 1), 0)
    totals = count[:, width - 1 : width]
    node_rows = iota((8, width), 0)
    node = jnp.full((8, width), float(NODES[0]), jnp.float32)
    for i in range(1, 8):
        node = jnp.where(node_rows == i, float(NODES[i]), node)
    coords = [jnp.sum(weights_ref[d] * node, axis=0, keepdims=True) for d in range(3)]
    words = element_ref[...].astype(jnp.float32)
    base = jnp.where(row % 4 == 3, words, 0.0)
    for d in range(3):
        base = jnp.where(row % 4 == d, coords[d], base)
    packs = [base, base, base]
    for b in range(11):
        step = 1 << b
        incoming = pltpu.roll(moves, width - step, 1)
        moved = (incoming >> b) & 1
        for n in range(3):
            first = jnp.broadcast_to(moved[2 * n : 2 * n + 1, :], (8, width))
            if n < 2:
                second = jnp.broadcast_to(moved[2 * n + 1 : 2 * n + 2, :], (8, width))
                first = jnp.where(row < 4, first, second)
            packs[n] = jnp.where(first == 1, pltpu.roll(packs[n], width - step, 1), packs[n])
        moves = jnp.where(moved == 1, incoming, jnp.where((moves >> b) & 1 == 1, 0, moves))
    moves_ref[...] = moves[:, :CAP]
    slots_ref[...] = jnp.full(slots_ref.shape, -1.0, jnp.float32)
    lane = iota((4, CAP), 1)
    for s in range(5):
        at = (s % 2) * 4
        slots_ref[s + 4] = jnp.where(
            lane < totals[s : s + 1, :], packs[s // 2][at : at + 4, :CAP], -1.0
        )
    r = q % 4
    rs = (q + 2) % 4
    for t in range(4):
        near_ref[t] = slots_ref[t - r + 6]
        off = t - rs
        inside = (r + off >= 0) & (r + off <= 3)
        far_ref[t] = slots_ref[jnp.where(inside, 0, off + 6)]


def split_kernel(fields_ref, out_ref):
    for f in range(FIELDS):
        value = fields_ref[f]
        high = value.astype(jnp.bfloat16)
        out_ref[f, :, 0:LANES] = high
        out_ref[f, :, LANES : 2 * LANES] = (value - high.astype(jnp.float32)).astype(jnp.bfloat16)


def basis_rows(coordinate):
    gaps = [coordinate - float(NODES[i]) for i in range(8)]
    before = [None] * 8
    after = [None] * 8
    for i in range(1, 8):
        before[i] = gaps[i - 1] if i == 1 else before[i - 1] * gaps[i - 1]
    for i in range(6, -1, -1):
        after[i] = gaps[i + 1] if i == 6 else after[i + 1] * gaps[i + 1]
    out = []
    for i in range(8):
        if i == 0:
            value = after[0]
        elif i == 7:
            value = before[7]
        else:
            value = before[i] * after[i]
        out.append(value * float(BARY[i]))
    return out


def eval_kernel(near_ref, far_ref, fields_ref, near_out_ref, far_out_ref):
    for source, target in ((near_ref, near_out_ref), (far_ref, far_out_ref)):
        valid = (source[:, 3, :] >= 0.0).astype(jnp.int32)
        for c in range(4):
            blocks = (jnp.sum(valid[c : c + 1, :]) + BLOCK - 1) // BLOCK

            def one_block(b, carry, c=c, source=source, target=target):
                start = pl.multiple_of(b * BLOCK, BLOCK)
                words = source[c, :, pl.ds(start, BLOCK)]
                element = words[3:4, :].astype(jnp.int32)
                hot = (iota((LANES, BLOCK), 0) == element).astype(jnp.float32).astype(jnp.bfloat16)
                hot = jnp.concatenate([hot, hot], axis=0)
                along = [basis_rows(words[d : d + 1, :]) for d in range(3)]
                row = iota((8, BLOCK), 0)
                wx = jnp.broadcast_to(along[0][0], (8, BLOCK))
                for i in range(1, 8):
                    wx = jnp.where(row == i, along[0][i], wx)
                for f in range(FIELDS):
                    picked = lax.dot(
                        fields_ref[f], hot, preferred_element_type=jnp.float32
                    )
                    over_k = picked[0:64, :] * along[2][0]
                    for k in range(1, 8):
                        over_k = over_k + picked[64 * k : 64 * k + 64, :] * along[2][k]
                    over_j = over_k[0:8, :] * along[1][0]
                    for j in range(1, 8):
                        over_j = over_j + over_k[8 * j : 8 * j + 8, :] * along[1][j]
                    target[c, f : f + 1, pl.ds(start, BLOCK)] = jnp.sum(
                        over_j * wx, axis=0, keepdims=True
                    )
                return carry

            lax.fori_loop(0, blocks, one_block, 0)


def unpack_kernel(place_ref, near_ref, far_ref, moves_ref, owner_ref, out_ref):
    q = place_ref[0]
    r = q % 4
    rs = (q + 2) % 4
    width = N_REC
    zeros = jnp.zeros((FIELDS, CAP), jnp.float32)
    values = []
    for s in range(5):
        off = s - 2
        inside = (r + off >= 0) & (r + off <= 3)
        near = near_ref[jnp.clip(r + off, 0, 3)]
        far = far_ref[jnp.clip(rs + off, 0, 3)]
        values.append(jnp.concatenate([jnp.where(inside, near, far), zeros], axis=1))
    moves = jnp.concatenate([moves_ref[...], jnp.zeros((8, CAP), jnp.int32)], axis=1)
    for b in range(10, -1, -1):
        step = 1 << b
        incoming = pltpu.roll(moves, step, 1)
        moved = (incoming >> b) & 1
        for s in range(5):
            flag = jnp.broadcast_to(moved[s : s + 1, :], (FIELDS, width))
            values[s] = jnp.where(flag == 1, pltpu.roll(values[s], step, 1), values[s])
        moves = jnp.where(moved == 1, incoming, jnp.where((moves >> b) & 1 == 1, 0, moves))
    distance = jnp.broadcast_to(owner_ref[...] - q + 2, (FIELDS, width))
    out = values[0]
    for s in range(1, 5):
        out = jnp.where(distance == s, values[s], out)
    out_ref[...] = out


def prep_kernel(
    place_ref, geometry_ref, wall_ref, forcing_ref, below_ref, above_ref,
    inverse_ref, free_ref, load_ref, plane_ref,
):
    q = place_ref[0]
    wcol = w_column()
    scol = s_column()

    def diagonal(geometry, k, j):
        wk, wj = float(WEIGHTS[k]), float(WEIGHTS[j])
        sk, sj = float(STIFF[k, k]), float(STIFF[j, j])
        return (
            geometry[0:1, :] * (scol * (wk * wj))
            + geometry[1:2, :] * (wcol * (wk * sj))
            + geometry[2:3, :] * (wcol * (sk * wj))
            + geometry[3:4, :] * (wcol * (wk * wj))
        )

    geometry = geometry_ref[...]
    below = below_ref[0:8, :]
    above = above_ref[0:8, :]
    lane = iota((8, LANES), 1)
    row = iota((8, LANES), 0)
    zero = jnp.zeros((8, LANES), jnp.float32)

    def wall_plane(low, high):
        for j in range(8):
            plane_ref[8 * j : 8 * j + 8, :] = zero
        plane_ref[0:8, :] = jnp.where(lane < 8, low, 0.0) + zero
        plane_ref[56:64, :] = jnp.where(lane >= 120, high, 0.0) + zero
        sum_xy(plane_ref, 1)
        return plane_ref[...]

    wall = wall_plane(wall_ref[0:1, :], wall_ref[1:2, :])
    wall_below = wall_plane(below[4:5, :], below[5:6, :])
    wall_above = wall_plane(above[4:5, :], above[5:6, :])
    mark = jnp.where(
        ((row == 0) & (lane % 8 == 0)) | ((row == 7) & (lane % 8 == 7)), 1.0, 0.0
    )
    for j in range(8):
        plane_ref[8 * j : 8 * j + 8, :] = mark
    sum_xy(plane_ref, 1)
    rec = plane_ref[...]
    has_below = jnp.where(q > 0, 1.0, 0.0)
    has_above = jnp.where(q < N_DOM - 1, 1.0, 0.0)
    inner = 1.0 - jnp.minimum(rec + wall, 1.0)
    bottom = 1.0 - jnp.minimum(rec + rec * has_below + (wall + wall_below), 1.0)
    top = 1.0 - jnp.minimum(rec + rec * has_above + (wall + wall_above), 1.0)
    free_ref[0:64, :] = bottom
    free_ref[448:512, :] = top
    for k in range(1, 7):
        free_ref[64 * k : 64 * k + 64, :] = inner

    for k in range(8):
        for j in range(8):
            inverse_ref[(k * 8 + j) * 8 : (k * 8 + j) * 8 + 8, :] = diagonal(geometry, k, j)
    sum_xy(inverse_ref, 8)
    for j in range(8):
        plane_ref[8 * j : 8 * j + 8, :] = diagonal(below, 7, j)
    sum_xy(plane_ref, 1)
    inverse_ref[0:64, :] = inverse_ref[0:64, :] + plane_ref[...]
    for j in range(8):
        plane_ref[8 * j : 8 * j + 8, :] = diagonal(above, 0, j)
    sum_xy(plane_ref, 1)
    inverse_ref[448:512, :] = inverse_ref[448:512, :] + plane_ref[...]
    for k in range(8):
        at = slice(64 * k, 64 * k + 64)
        inverse_ref[at, :] = free_ref[at, :] / inverse_ref[at, :]

    for k in range(8):
        for j in range(8):
            at = slice((k * 8 + j) * 8, (k * 8 + j) * 8 + 8)
            load_ref[at, :] = forcing_ref[at, :] * (
                geometry[3:4, :] * (wcol * float(WEIGHTS[k] * WEIGHTS[j]))
            )
    sum_xy(load_ref, 8)
    for other_ref, k, base in ((below_ref, 7, 0), (above_ref, 0, 448)):
        for j in range(8):
            plane_ref[8 * j : 8 * j + 8, :] = other_ref[8 + 8 * j : 16 + 8 * j, :] * (
                other_ref[3:4, :] * (wcol * float(WEIGHTS[k] * WEIGHTS[j]))
            )
        sum_xy(plane_ref, 1)
        load_ref[base : base + 64, :] = load_ref[base : base + 64, :] + plane_ref[...]


def inverse_multiplicity(q):
    row = iota((64, LANES), 0)
    lane = iota((64, LANES), 1)
    i, j = row % 8, row // 8
    x, y = lane % 8, lane // 8
    along_x = ((i == 0) & (x > 0)) | ((i == 7) & (x < 7))
    along_y = ((j == 0) & (y > 0)) | ((j == 7) & (y < 15))
    inner = jnp.where(along_x, 0.5, 1.0) * jnp.where(along_y, 0.5, 1.0)
    return (
        inner,
        inner * jnp.where(q > 0, 0.5, 1.0),
        inner * jnp.where(q < N_DOM - 1, 0.5, 1.0),
    )


def krylov_step(q, w_ref, inverse_ref, geometry_ref, xmat_ref, v_ref, u_ref, at, moments):
    inner, bottom, top = inverse_multiplicity(q)
    norm = jnp.zeros((64, LANES), jnp.float32)
    for k in range(8):
        rows = slice(64 * k, 64 * k + 64)
        w = w_ref[rows, :]
        v = inverse_ref[rows, :] * w
        v_ref[rows, :] = v
        norm = norm + v * w * (bottom if k == 0 else top if k == 7 else inner)
    energy = apply_local(
        v_ref, geometry_ref[...], xmat_ref, u_ref, tuple(range(8)), dot_with_v=True
    )
    sum_xy(u_ref, 8)
    return moments + lane_value(jnp.sum(norm), at) + lane_value(jnp.sum(energy), at + 1)


def first_kernel(
    place_ref, near_ref, far_ref, geometry_ref, below_ref, above_ref, inverse_ref, free_ref,
    load_ref, xmat_ref, w_ref, u_ref, edge_ref, moments_ref, v_ref, face_ref,
):
    q = place_ref[0]
    r = q % 4
    rs = (q + 2) % 4
    pick_row = iota((16, LANES), 0)
    pick_lane = iota((16, LANES), 1)
    picks = [
        jnp.where(pick_lane == pick_row * 8 + (0 if s == 0 else 7), 1.0, 0.0) for s in range(2)
    ]

    def planes(off):
        inside = (r + off >= 0) & (r + off <= 3)
        exists = (q + off >= 0) & (q + off < N_DOM)
        near = near_ref[jnp.clip(r + off, 0, 3)]
        far = far_ref[jnp.clip(rs + off, 0, 3)]
        values = jnp.where(exists, jnp.where(inside, near, far), 0.0)
        out = []
        for s in range(2):
            plane = lax.dot_general(
                values[16 * s : 16 * s + 16, :], picks[s], (((0,), (0,)), ((), ())),
                precision=HIGHEST, preferred_element_type=jnp.float32,
            )
            out.append([plane[8 * k : 8 * k + 8, :] for k in range(8)])
        return out

    received = {off: planes(off) for off in range(-2, 3)}
    lane = iota((8, LANES), 1)
    j_row = iota((8, LANES), 0)
    low = (j_row == 0) & (lane >= 8)
    high = (j_row == 7) & (lane < 120)

    def sum_y(value):
        down = jnp.broadcast_to(pltpu.roll(value, LANES - 8, 1)[0:1, :], (8, LANES))
        up = jnp.broadcast_to(pltpu.roll(value, 8, 1)[7:8, :], (8, LANES))
        return value + jnp.where(high, down, 0.0) + jnp.where(low, up, 0.0)

    count_y = jnp.where(low | high, 2.0, 1.0)
    on_side = [jnp.where(lane % 8 == x, 1.0, 0.0) for x in (0, 7)]

    def boundary(off):
        out = []
        has_below = jnp.where(q + off > 0, 1.0, 0.0)
        has_above = jnp.where(q + off < N_DOM - 1, 1.0, 0.0)
        for s in range(2):
            side = []
            for k in range(8):
                total = received[off][s][k]
                count = count_y * on_side[s]
                if k == 0:
                    total = total + received[off - 1][s][7]
                    count = count + count * has_below
                if k == 7:
                    total = total + received[off + 1][s][0]
                    count = count + count * has_above
                side.append(sum_y(total) / jnp.maximum(count, 1.0))
            out.append(jnp.concatenate(side, axis=0))
        return out

    zero = jnp.zeros((64, LANES), jnp.float32)
    for k in range(8):
        v_ref[64 * k : 64 * k + 64, :] = zero
    for off, geometry, plane in ((-1, below_ref[0:4, :], 7), (1, above_ref[0:4, :], 0)):
        sides = boundary(off)
        v_ref[pl.ds(0, 64, stride=8), :] = sides[0]
        v_ref[pl.ds(7, 64, stride=8), :] = sides[1]
        at = 0 if off < 0 else 64
        apply_local(v_ref, geometry, xmat_ref, face_ref.at[at : at + 64, :], (plane,))
        sum_xy(face_ref.at[at : at + 64, :], 1)
    sides = boundary(0)
    v_ref[pl.ds(0, 64, stride=8), :] = sides[0]
    v_ref[pl.ds(7, 64, stride=8), :] = sides[1]
    edge_ref[0:64, :] = sides[0]
    edge_ref[64:128, :] = sides[1]
    apply_local(v_ref, geometry_ref[...], xmat_ref, u_ref, tuple(range(8)))
    sum_xy(u_ref, 8)
    u_ref[0:64, :] = u_ref[0:64, :] + face_ref[0:64, :]
    u_ref[448:512, :] = u_ref[448:512, :] + face_ref[64:128, :]
    for k in range(8):
        rows = slice(64 * k, 64 * k + 64)
        w_ref[rows, :] = free_ref[rows, :] * (load_ref[rows, :] - u_ref[rows, :])
    moments_ref[...] = krylov_step(
        q, w_ref, inverse_ref, geometry_ref, xmat_ref, v_ref, u_ref, 0,
        jnp.zeros((1, LANES), jnp.float32),
    )


def next_kernel(
    at, last, place_ref, w_old_ref, u_old_ref, below_ref, above_ref, geometry_ref, inverse_ref,
    free_ref, xmat_ref, moments_old_ref, w_ref, u_ref, moments_ref, v_ref,
):
    q = place_ref[0]
    for k in range(8):
        rows = slice(64 * k, 64 * k + 64)
        image = u_old_ref[rows, :]
        if k == 0:
            image = image + below_ref[...]
        if k == 7:
            image = image + above_ref[...]
        w_ref[rows, :] = free_ref[rows, :] * image - w_old_ref[rows, :]
    row = krylov_step(
        q, w_ref, inverse_ref, geometry_ref, xmat_ref, v_ref, u_ref, at, moments_old_ref[...]
    )
    moments_ref[...] = jnp.broadcast_to(row, moments_ref.shape)


def last_kernel(
    w0_ref, w1_ref, w2_ref, u_ref, below_ref, above_ref, inverse_ref, free_ref, edge_ref,
    moments_ref, velocity_ref, residual_ref,
):
    sums = jnp.sum(moments_ref[...], axis=0, keepdims=True)
    h0, a0, h2, a1, h4, a2 = [sums[:, m : m + 1] for m in range(6)]
    h1, h3 = a0 - h0, a1 - h2
    g00, g01, g02, g11, g12, g22 = a0, h2 + h1, h3 + h2, a1, h4 + h3, a2
    b0, b1, b2 = h0, h1, h2
    l10 = g01 / g00
    l20 = g02 / g00
    d1 = g11 - l10 * g01
    e12 = g12 - l10 * g02
    l21 = e12 / d1
    d2 = g22 - l20 * g02 - l21 * e12
    y1 = b1 - l10 * b0
    y2 = b2 - l20 * b0 - l21 * y1
    c2 = y2 / d2
    c1 = y1 / d1 - l21 * c2
    c0 = b0 / g00 - l10 * c1 - l20 * c2
    c0, c1, c2 = [jnp.broadcast_to(c, (64, LANES)) for c in (c0, c1, c2)]
    for k in range(8):
        rows = slice(64 * k, 64 * k + 64)
        image = u_ref[rows, :]
        if k == 0:
            image = image + below_ref[...]
        if k == 7:
            image = image + above_ref[...]
        w0, w1, w2 = w0_ref[rows, :], w1_ref[rows, :], w2_ref[rows, :]
        velocity_ref[rows, :] = inverse_ref[rows, :] * (c0 * w0 + c1 * w1 + c2 * w2)
        residual_ref[rows, :] = (
            w0 - c0 * (w1 + w0) - c1 * (w2 + w1) - c2 * (free_ref[rows, :] * image)
        )
    for s in range(2):
        rows = pl.ds(7 * s, 64, stride=8)
        velocity_ref[rows, :] = velocity_ref[rows, :] + edge_ref[64 * s : 64 * s + 64, :]


VMEM = pl.BlockSpec(memory_space=pltpu.VMEM)
SMEM = pl.BlockSpec(memory_space=pltpu.SMEM)


def call(kernel, operands, outs, scratch=(), flops=100_000, smem_first=True, name=None):
    specs = [VMEM] * len(operands)
    if smem_first:
        specs[0] = SMEM
    out_shape = [jax.ShapeDtypeStruct(shape, dtype) for shape, dtype in outs]
    return pl.pallas_call(
        kernel,
        out_shape=out_shape,
        in_specs=specs,
        out_specs=[VMEM] * len(outs),
        scratch_shapes=[pltpu.VMEM(shape, dtype) for shape, dtype in scratch],
        cost_estimate=pl.CostEstimate(flops=flops, bytes_accessed=1_000_000, transcendentals=0),
        name=name,
    )(*operands)


F32 = jnp.float32
FIELD = ((512, LANES), F32)


def to_all(value):
    return lax.all_to_all(value, "dom", 0, 0, tiled=True)


def to_group(value, groups):
    return lax.all_to_all(value, "dom", 0, 0, tiled=True, axis_index_groups=groups)


def body(donor_fields, interp_weights, donor_owner, donor_element, geometry, wall_flag, forcing):
    place = lax.axis_index("dom").astype(jnp.int32).reshape(1)
    xmat = jnp.asarray(x_matrix())
    donors = lax.ppermute(donor_fields, "mesh", [(0, 1), (1, 0)])
    owner = donor_owner.reshape(1, N_REC)
    element = donor_element.reshape(1, N_REC)
    near, far, moves = call(
        route_kernel, (place, interp_weights, owner, element),
        (((4, 4, CAP), F32), ((4, 4, CAP), F32), ((8, CAP), jnp.int32)),
        scratch=(((13, 4, CAP), F32),), name="route",
    )
    near_in = to_group(near, ALIGNED)
    far_in = to_group(far, SHIFTED)

    wall = jnp.tile(wall_flag.astype(F32), (1, 16))
    head = jnp.concatenate([geometry, wall, jnp.zeros((2, LANES), F32)], 0)
    below = lax.ppermute(jnp.concatenate([head, forcing[448:512]], 0), "dom", UP)
    above = lax.ppermute(jnp.concatenate([head, forcing[0:64]], 0), "dom", DOWN)
    inverse, free, load = call(
        prep_kernel, (place, geometry, wall, forcing, below, above),
        (FIELD, FIELD, FIELD), scratch=(((64, LANES), F32),), name="prep",
    )
    (fields,) = call(
        split_kernel, (donors,), (((FIELDS, 512, 256), jnp.bfloat16),), smem_first=False,
        name="split",
    )
    near_out, far_out = call(
        eval_kernel, (near_in, far_in, fields),
        (((4, FIELDS, CAP), F32), ((4, FIELDS, CAP), F32)),
        flops=7_000_000_000, smem_first=False, name="evaluate",
    )
    near_back = to_group(near_out, ALIGNED)
    far_back = to_group(far_out, SHIFTED)
    (interface,) = call(
        unpack_kernel, (place, near_back, far_back, moves, owner), (((FIELDS, N_REC), F32),),
        name="unpack",
    )
    received = jnp.broadcast_to(interface[0].reshape(1, 32, 64), (4, 32, 64))
    near_rec = to_group(received, ALIGNED)
    far_rec = to_group(received, SHIFTED)
    w0, u, edge, moments = call(
        first_kernel,
        (place, near_rec, far_rec, geometry, below, above, inverse, free, load, xmat),
        (FIELD, FIELD, ((128, LANES), F32), ((1, LANES), F32)),
        scratch=(FIELD, ((128, LANES), F32)), name="first",
    )

    def halo(u):
        return lax.ppermute(u[448:512], "dom", UP), lax.ppermute(u[0:64], "dom", DOWN)

    ws = [w0]
    for step in (1, 2):
        from_below, from_above = halo(u)
        w, u, moments = call(
            functools.partial(next_kernel, 2 * step, step == 2),
            (place, ws[-1], u, from_below, from_above, geometry, inverse, free, xmat, moments),
            (FIELD, FIELD, ((1 if step == 1 else N_DOM, LANES), F32)),
            scratch=(FIELD,), name=f"next{step}",
        )
        ws.append(w)
    from_below, from_above = halo(u)
    sums = to_all(moments)
    velocity, residual = call(
        last_kernel,
        (*ws, u, from_below, from_above, inverse, free, edge, sums),
        (FIELD, FIELD), smem_first=False, name="last",
    )
    return velocity, residual, interface


def solution(mesh):
    both = ("mesh", "dom")
    in_specs = (
        P(None, None, both), P(None, None, both), P(both, None), P(both), P(None, both),
        P(None, both), P(None, both),
    )
    out_specs = (P(None, both), P(None, both), P(None, both))
    return jax.shard_map(body, mesh=mesh, in_specs=in_specs, out_specs=out_specs, check_vma=False)
```

time: 539 us -> 162 us (0.30); the launches traced: 529 us -> 160 us
  local copies, waits for them, and re-layouts: 189 us -> 13.1 us
  other arithmetic: 141 us -> 1.59 us
  waiting for transfers between devices: 55.5 us -> 10.7 us
  Pallas kernels: 0 us -> 33.4 us
  starting transfers between devices: 62.1 us -> 50.4 us
  between operations: 11.5 us -> 0.82 us
  matrix products: 10.3 us -> 0 us
  blocking collectives: 59.2 us -> 49.5 us
    gather x8 -> x0, local copies, waits for them, and re-layouts: 93.9 us -> none  [the longest x5 68 us: body(): jnp.take(donor_fields, lookups, axis=2).reshape(field_count, 64, 8, count)]
    select_n x24 -> x0, other arithmetic: 80.6 us -> none  [the longest x5 61.5 us: body(): jnp.take(donor_fields, lookups, axis=2).reshape(field_count, 64, 8, count)]
    select_n x6 -> x0, local copies, waits for them, and re-layouts: 75.1 us -> none  [the longest x5 73.3 us: body(): jnp.take(donor_fields, lookups, axis=2).reshape(field_count, 64, 8, count)]
    reduce_sum x22 -> x0, other arithmetic: 44.8 us -> none  [the longest x5 39.1 us: body(): jnp.sum(gathered * piece[0:8][None, None], axis=2)]
    ppermute x20 -> x9, waiting for transfers between devices: 46.8 us -> 8.84 us  [the longest x3 8.46 us: halo(): lax.ppermute(u[0:64], 'dom', DOWN)]
    ppermute x20 -> x9, starting transfers between devices: 49.5 us -> 15.4 us  [the longest x3 6.07 us: halo(): lax.ppermute(u[448:512], 'dom', UP)]
    pallas_call x0 -> x9, Pallas kernels: none -> 33.4 us  [call(): pl.pallas_call(kernel, out_shape=out_shape, in_specs=specs, out_specs=[VM...]
    all_to_all x1 -> x4, starting transfers between devices: 12.6 us -> 35 us  [to_group(): lax.all_to_all(value, 'dom', 0, 0, tiled=True, axis_index_groups=groups)]
  transfers between devices with their start and end apart: 21 -> 13, of which waited for: 15 -> 5; matrix products, arithmetic and copies ran while one was open for 40% -> 2% of each run, Pallas kernels for 0% -> 5%
where the time goes in v1:
time: 162 us; the launch traced here: 160 us
  starting transfers between devices  50.4 us (31%)
  blocking collectives  49.5 us (31%)
  Pallas kernels  33.4 us (21%)
  local copies, waits for them, and re-layouts  13.1 us (8%)
  waiting for transfers between devices  10.7 us (7%)
    all_to_all x4, starting transfers between devices, to_group(): lax.all_to_all(value, 'dom', 0, 0, tiled=True, axis_index_groups=groups)  35 us
    pallas_call x9, Pallas kernels, call(): pl.pallas_call(kernel, out_shape=out_shape, in_specs=specs, out_specs=[VM...  33.4 us
    all_to_all x1, blocking collectives, to_all(): return lax.all_to_all(value, 'dom', 0, 0, tiled=True)  29.1 us
    all_to_all x2, blocking collectives, to_group(): lax.all_to_all(value, 'dom', 0, 0, tiled=True, axis_index_groups=groups)  20.4 us
    ppermute x3, waiting for transfers between devices, halo(): lax.ppermute(u[0:64], 'dom', DOWN)  8.46 us
    unnamed x32, local copies, waits for them, and re-layouts  8.31 us
    ppermute x3, starting transfers between devices, halo(): lax.ppermute(u[448:512], 'dom', UP)  6.07 us
    ppermute x3, starting transfers between devices, halo(): lax.ppermute(u[0:64], 'dom', DOWN)  4.06 us
  transfers between devices with their start and end apart: 13, of which 5 were waited for; matrix products, arithmetic and copies ran while one was open for 2% of the time, Pallas kernels for 5%

profile of v1, /device:TPU:0, one launch (start us, length us, event | category | flops | bytes accessed | tf_op | source)
XLA Modules:
  0.0 159.5 jit_solution(17524589006822323291)
XLA Ops:
  0.7 2.9 %route.1 = (f32[4,4,1024]{2,1,0:T(4,128)}, f32[4,4,1024]{2,1,0:T(4,128)}, s32[8,1024]{1,0:T(8,128)}) custom-call(s32[1]{0:T(128)} %bitcast.place_ref, f32[3,8,2048]{2,1,0:T(8,128)} %weights_ref.1, s32[1,2048]{1,0:T(1,128)} %bitcast.9, s32[1,2048]{1,0:T(1,128)} %bitcast.11), custom_call_target="tpu_custom_call" | custom-call | flops 100000 | bytes 1000000 | tf_op jit(solution)/shard_map/route/pallas_call | solution.py:580
  3.6 10.3 %all_to_all.41.near_ref = f32[4,4,1024]{2,1,0:T(4,128)} all-to-all(f32[4,4,1024]{2,1,0:T(4,128)} %get-tuple-element.23), channel_id=1, replica_groups={{0,1,2,3},{4,5,6,7},{8,9,10,11},{12,13,14,15},{16,17,18,19},{20,21,22,2..., dimensions={0} | all-to-all | bytes 131072 | tf_op jit(solution)/shard_map/all_to_all | solution.py:600
  13.9 9.9 %all-to-all-start.1 = ((f32[4,4,1024]{2,1,0:T(4,128)}), f32[4,4,1024]{2,1,0:T(4,128)S(1)}, u32[]{:S(2)}, u32[]{:S(2)}) async-start(f32[4,4,1024]{2,1,0:T(4,128)} %get-tuple-element.24), calls=%async_computation.1 | async-start | bytes 131072 | tf_op jit(solution)/shard_map/all_to_all | solution.py:600
  24.9 2.7 %split.1.fields_ref = bf16[5,512,256]{2,1,0:T(8,128)(2,1)} custom-call(f32[5,512,128]{2,1,0:T(8,128)} %copy-done), custom_call_target="tpu_custom_call" | custom-call | flops 100000 | bytes 1000000 | tf_op jit(solution)/shard_map/split/pallas_call | solution.py:580
  28.2 9.1 %evaluate.1 = (f32[4,5,1024]{2,1,0:T(8,128)}, f32[4,5,1024]{2,1,0:T(8,128)}) custom-call(f32[4,4,1024]{2,1,0:T(4,128)} %all_to_all.41.near_ref, f32[4,4,1024]{2,1,0:T(4,128)} %copy-done.4, bf16[5,512,256]{2,1,0:T(8,128)(2,1)} %split.1.fields_ref), custom_call_target="tpu_custom_call" | custom-call | flops 7000000000 | bytes 1000000 | tf_op jit(solution)/shard_map/evaluate/pallas_call | solution.py:580
  37.3 10.1 %all_to_all.42.near_ref = f32[4,5,1024]{2,1,0:T(8,128)} all-to-all(f32[4,5,1024]{2,1,0:T(8,128)} %get-tuple-element.25), channel_id=1, replica_groups={{0,1,2,3},{4,5,6,7},{8,9,10,11},{12,13,14,15},{16,17,18,19},{20,21,22,2..., dimensions={0} | all-to-all | bytes 163840 | tf_op jit(solution)/shard_map/all_to_all | solution.py:600
  47.4 9.0 %all-to-all-start.3 = ((f32[4,5,1024]{2,1,0:T(8,128)}), f32[4,5,1024]{2,1,0:T(8,128)S(1)}, u32[]{:S(2)}, u32[]{:S(2)}) async-start(f32[4,5,1024]{2,1,0:T(8,128)} %get-tuple-element.26), calls=%async_computation.3 | async-start | bytes 262144 | tf_op jit(solution)/shard_map/all_to_all | solution.py:600
  57.4 1.8 %all-to-all-done.3.far_ref = f32[4,5,1024]{2,1,0:T(8,128)S(1)} async-done(((f32[4,5,1024]{2,1,0:T(8,128)}), f32[4,5,1024]{2,1,0:T(8,128)S(1)}, u32[]{:S(2)}, u32[]{:S(2)}) %all-to-all-start.3) | async-done | bytes 81952 | tf_op jit(solution)/shard_map/all_to_all | solution.py:600
  59.9 2.5 %unpack.1 = f32[5,2048]{1,0:T(8,128)} custom-call(s32[1]{0:T(128)} %bitcast.place_ref, f32[4,5,1024]{2,1,0:T(8,128)} %all_to_all.42.near_ref, f32[4,5,1024]{2,1,0:T(8,128)} %copy-done.1, s32[8,1024]{1,0:T(8,128)} %get-tuple-element.27.moves_ref, s32[1,2048]{1,0:T(1,128)} %bitcast.10), custom_call_target="tpu_custom_call" | custom-call | flops 100000 | bytes 1000000 | tf_op jit(solution)/shard_map/unpack/pallas_call | solution.py:580
  64.0 3.3 %all-to-all-start.4 = ((f32[4,1,2048]{2,1,0:T(1,128)}), f32[4,1,2048]{2,1,0:T(1,128)S(1)}, u32[]{:S(2)}, u32[]{:S(2)}) async-start(f32[4,1,2048]{2,1,0:T(1,128)} %reshape.32), calls=%async_computation.4 | async-start | bytes 65536 | tf_op jit(solution)/shard_map/all_to_all | solution.py:600
  67.4 3.9 %collective-permute-start.1 = (f32[72,128]{1,0:T(8,128)S(1)}, f32[72,128]{1,0:T(8,128)S(1)}, u32[]{:S(2)}, u32[]{:S(2)}) collective-permute-start(f32[72,128]{1,0:T(8,128)S(1)} %get-tuple-element.52), channel_id=1, source_target_pairs={{0,1},{1,2},{2,3},{3,4},{4,5},{5,6},{6,7},{7,8},{8,9},{9,10},{10,1... | collective-permute-start | bytes 110600 | tf_op jit(solution)/shard_map/ppermute | solution.py:619
  73.3 12.8 %all-to-all-start.5 = ((f32[4,1,2048]{2,1,0:T(1,128)}), f32[4,1,2048]{2,1,0:T(1,128)S(1)}, u32[]{:S(2)}, u32[]{:S(2)}) async-start(f32[4,1,2048]{2,1,0:T(1,128)} %reshape.34), calls=%async_computation.5 | async-start | bytes 65536 | tf_op jit(solution)/shard_map/all_to_all | solution.py:600
  87.3 2.6 %prep.1 = (f32[512,128]{1,0:T(8,128)}, f32[512,128]{1,0:T(8,128)}, f32[512,128]{1,0:T(8,128)}) custom-call(s32[1]{0:T(128)} %bitcast.place_ref, f32[4,128]{1,0:T(4,128)} %geometry_ref.7, f32[2,128]{1,0:T(2,128)} %copy-done.12, f32[512,128]{1,0:T(8,128)} %forcing_ref.1, f32[72,128]{1,0:T(8,128)} %copy-done.2, f32[72,128]{1,0:T(8,128)} %copy-done.3), custom_call_target="tpu_custom_call" | custom-call | flops 100000 | bytes 1000000 | tf_op jit(solution)/shard_map/prep/pallas_call | solution.py:580
  93.5 4.5 %first.1 = (f32[512,128]{1,0:T(8,128)}, f32[512,128]{1,0:T(8,128)}, f32[128,128]{1,0:T(8,128)}, f32[1,128]{1,0:T(1,128)}) custom-call(s32[1]{0:T(128)} %bitcast.place_ref, f32[4,32,64]{2,1,0:T(8,128)} %reshape.33.near_ref, f32[4,32,64]{2,1,0:T(8,128)} %reshape.35.far_ref, f32[4,128]{1,0:T(4,128)} %geometry_ref.7, f32[72,128]{1,0:T(8,128)} %copy-done.2, ...), custom_call_target="tpu_custom_call" | custom-call | flops 100000 | bytes 1000000 | tf_op jit(solution)/shard_map/first/pallas_call | solution.py:580
  98.8 1.9 %collective-permute-start.3 = (f32[64,128]{1,0:T(8,128)S(1)}, f32[64,128]{1,0:T(8,128)S(1)}, u32[]{:S(2)}, u32[]{:S(2)}) collective-permute-start(f32[64,128]{1,0:T(8,128)S(1)} %get-tuple-element.48), channel_id=1, source_target_pairs={{0,1},{1,2},{2,3},{3,4},{4,5},{5,6},{6,7},{7,8},{8,9},{9,10},{10,1... | collective-permute-start | bytes 98312 | tf_op jit(solution)/shard_map/ppermute | solution.py:651
  102.2 4.2 %collective-permute-done.4.above_ref = f32[64,128]{1,0:T(8,128)S(1)} collective-permute-done((f32[64,128]{1,0:T(8,128)S(1)}, f32[64,128]{1,0:T(8,128)S(1)}, u32[]{:S(2)}, u32[]{:S(2)}) %collective-permute-start.4) | collective-permute-done | bytes 32800 | tf_op jit(solution)/shard_map/ppermute | solution.py:651
  107.1 3.1 %next1.1 = (f32[512,128]{1,0:T(8,128)}, f32[512,128]{1,0:T(8,128)}, f32[1,128]{1,0:T(1,128)}) custom-call(s32[1]{0:T(128)} %bitcast.place_ref, f32[512,128]{1,0:T(8,128)} %get-tuple-element.31.w_old_ref.w0_ref, f32[512,128]{1,0:T(8,128)} %get-tuple-element.32.u_old_ref, f32[64,128]{1,0:T(8,128)} %copy-done.9, f32[64,128]{1,0:T(8,128)} %copy-done.11, ...), custom_call_target="tpu_custom_call" | custom-call | flops 100000 | bytes 1000000 | tf_op jit(solution)/shard_map/next1/pallas_call | solution.py:580
  111.0 1.9 %collective-permute-start.5 = (f32[64,128]{1,0:T(8,128)S(1)}, f32[64,128]{1,0:T(8,128)S(1)}, u32[]{:S(2)}, u32[]{:S(2)}) collective-permute-start(f32[64,128]{1,0:T(8,128)S(1)} %get-tuple-element.46), channel_id=1, source_target_pairs={{0,1},{1,2},{2,3},{3,4},{4,5},{5,6},{6,7},{7,8},{8,9},{9,10},{10,1... | collective-permute-start | bytes 98312 | tf_op jit(solution)/shard_map/ppermute | solution.py:651
  112.9 1.5 collective-permute-start.6
  114.5 4.2 %collective-permute-done.6.above_ref = f32[64,128]{1,0:T(8,128)S(1)} collective-permute-done((f32[64,128]{1,0:T(8,128)S(1)}, f32[64,128]{1,0:T(8,128)S(1)}, u32[]{:S(2)}, u32[]{:S(2)}) %collective-permute-start.6) | collective-permute-done | bytes 32800 | tf_op jit(solution)/shard_map/ppermute | solution.py:651
  119.3 3.1 %next2.1 = (f32[512,128]{1,0:T(8,128)}, f32[512,128]{1,0:T(8,128)}, f32[64,128]{1,0:T(8,128)}) custom-call(s32[1]{0:T(128)} %bitcast.place_ref, f32[512,128]{1,0:T(8,128)} %get-tuple-element.34.w_old_ref.w1_ref, f32[512,128]{1,0:T(8,128)} %get-tuple-element.35.u_old_ref, f32[64,128]{1,0:T(8,128)} %copy-done.8, f32[64,128]{1,0:T(8,128)} %copy-done.10, ...), custom_call_target="tpu_custom_call" | custom-call | flops 100000 | bytes 1000000 | tf_op jit(solution)/shard_map/next2/pallas_call | solution.py:580
  123.2 2.3 %collective-permute-start.7 = (f32[64,128]{1,0:T(8,128)S(1)}, f32[64,128]{1,0:T(8,128)S(1)}, u32[]{:S(2)}, u32[]{:S(2)}) collective-permute-start(f32[64,128]{1,0:T(8,128)S(1)} %get-tuple-element.44), channel_id=1, source_target_pairs={{0,1},{1,2},{2,3},{3,4},{4,5},{5,6},{6,7},{7,8},{8,9},{9,10},{10,1... | collective-permute-start | bytes 98312 | tf_op jit(solution)/shard_map/ppermute | solution.py:651
  126.8 29.1 %all_to_all.43 = f32[64,1,128]{2,1,0:T(1,128)} all-to-all(f32[64,1,128]{2,1,0:T(1,128)} %bitcast.8), channel_id=1, replica_groups=mesh['mesh'=2,'dom'=64] {'dom'}, dimensions={0} | all-to-all | bytes 65536 | tf_op jit(solution)/shard_map/all_to_all | solution.py:596
  156.5 3.0 %last.1 = (f32[512,128]{1,0:T(8,128)}, f32[512,128]{1,0:T(8,128)}) custom-call(f32[512,128]{1,0:T(8,128)} %get-tuple-element.31.w_old_ref.w0_ref, f32[512,128]{1,0:T(8,128)} %get-tuple-element.34.w_old_ref.w1_ref, f32[512,128]{1,0:T(8,128)} %get-tuple-element.37.w2_ref, f32[512,128]{1,0:T(8,128)} %get-tuple-element.38.u_ref, f32[64,128]{1,0:T(8,128)} %copy-done.6, ...), custom_call_target="tpu_custom_call" | custom-call | flops 100000 | bytes 1000000 | tf_op jit(solution)/shard_map/last/pallas_call | solution.py:580
  (62 shorter events, 19.1 us)
Async XLA Ops:
  0.6 23.2 %collective-permute-start = (f32[5,512,128]{2,1,0:T(8,128)}, f32[5,512,128]{2,1,0:T(8,128)S(1)}, u32[]{:S(2)}, u32[]{:S(2)}) collective-permute-start(f32[5,512,128]{2,1,0:T(8,128)} %param.8), channel_id=1, source_target_pairs={{0,64},{64,0},{1,65},{65,1},{2,66},{66,2},{3,67},{67,3},{4,68},{68... | collective-permute-start | bytes 3932168 | tf_op jit(solution)/shard_map/ppermute | solution.py:606
  13.9 13.7 %all-to-all-start.1 = ((f32[4,4,1024]{2,1,0:T(4,128)}), f32[4,4,1024]{2,1,0:T(4,128)S(1)}, u32[]{:S(2)}, u32[]{:S(2)}) async-start(f32[4,4,1024]{2,1,0:T(4,128)} %get-tuple-element.24), calls=%async_computation.1 | async-start | bytes 131072 | tf_op jit(solution)/shard_map/all_to_all | solution.py:600
  23.8 1.1 copy-start
  27.6 29.7 %copy-start.13 = (s32[2,8]{1,0:T(2,128)S(1)}, s32[2,8]{1,0:T(2,128)}, u32[]{:S(2)}) copy-start(s32[2,8]{1,0:T(2,128)} %param.13) | copy-start | bytes 196
  27.6 0.6 copy-start.4
  37.3 30.0 %copy-start.5 = (f32[4,128]{1,0:T(4,128)S(1)}, f32[4,128]{1,0:T(4,128)}, u32[]{:S(2)}) copy-start(f32[4,128]{1,0:T(4,128)} %geometry_ref.7) | copy-start | bytes 6148
  47.4 11.8 %all-to-all-start.3 = ((f32[4,5,1024]{2,1,0:T(8,128)}), f32[4,5,1024]{2,1,0:T(8,128)S(1)}, u32[]{:S(2)}, u32[]{:S(2)}) async-start(f32[4,5,1024]{2,1,0:T(8,128)} %get-tuple-element.26), calls=%async_computation.3 | async-start | bytes 262144 | tf_op jit(solution)/shard_map/all_to_all | solution.py:600
  57.3 28.8 %copy-start.12 = (f32[2,128]{1,0:T(2,128)}, f32[2,128]{1,0:T(2,128)S(1)}, u32[]{:S(2)}) copy-start(f32[2,128]{1,0:T(2,128)S(1)} %tile.10.wall_ref) | copy-start | bytes 3076
  59.3 0.7 copy-start.1
  64.0 9.3 %all-to-all-start.4 = ((f32[4,1,2048]{2,1,0:T(1,128)}), f32[4,1,2048]{2,1,0:T(1,128)S(1)}, u32[]{:S(2)}, u32[]{:S(2)}) async-start(f32[4,1,2048]{2,1,0:T(1,128)} %reshape.32), calls=%async_computation.4 | async-start | bytes 65536 | tf_op jit(solution)/shard_map/all_to_all | solution.py:600
  67.4 18.7 %collective-permute-start.1 = (f32[72,128]{1,0:T(8,128)S(1)}, f32[72,128]{1,0:T(8,128)S(1)}, u32[]{:S(2)}, u32[]{:S(2)}) collective-permute-start(f32[72,128]{1,0:T(8,128)S(1)} %get-tuple-element.52), channel_id=1, source_target_pairs={{0,1},{1,2},{2,3},{3,4},{4,5},{5,6},{6,7},{7,8},{8,9},{9,10},{10,1... | collective-permute-start | bytes 110600 | tf_op jit(solution)/shard_map/ppermute | solution.py:619
  71.3 14.8 %collective-permute-start.2 = (f32[72,128]{1,0:T(8,128)S(1)}, f32[72,128]{1,0:T(8,128)S(1)}, u32[]{:S(2)}, u32[]{:S(2)}) collective-permute-start(f32[72,128]{1,0:T(8,128)S(1)} %get-tuple-element.51), channel_id=1, source_target_pairs={{1,0},{2,1},{3,2},{4,3},{5,4},{6,5},{7,6},{8,7},{9,8},{10,9},{11,1... | collective-permute-start | bytes 110600 | tf_op jit(solution)/shard_map/ppermute | solution.py:620
  73.3 18.7 %all-to-all-start.5 = ((f32[4,1,2048]{2,1,0:T(1,128)}), f32[4,1,2048]{2,1,0:T(1,128)S(1)}, u32[]{:S(2)}, u32[]{:S(2)}) async-start(f32[4,1,2048]{2,1,0:T(1,128)} %reshape.34), calls=%async_computation.5 | async-start | bytes 65536 | tf_op jit(solution)/shard_map/all_to_all | solution.py:600
  86.1 0.6 copy-start.2
  98.8 3.4 %collective-permute-start.3 = (f32[64,128]{1,0:T(8,128)S(1)}, f32[64,128]{1,0:T(8,128)S(1)}, u32[]{:S(2)}, u32[]{:S(2)}) collective-permute-start(f32[64,128]{1,0:T(8,128)S(1)} %get-tuple-element.48), channel_id=1, source_target_pairs={{0,1},{1,2},{2,3},{3,4},{4,5},{5,6},{6,7},{7,8},{8,9},{9,10},{10,1... | collective-permute-start | bytes 98312 | tf_op jit(solution)/shard_map/ppermute | solution.py:651
  100.6 5.8 %collective-permute-start.4 = (f32[64,128]{1,0:T(8,128)S(1)}, f32[64,128]{1,0:T(8,128)S(1)}, u32[]{:S(2)}, u32[]{:S(2)}) collective-permute-start(f32[64,128]{1,0:T(8,128)S(1)} %get-tuple-element.47), channel_id=1, source_target_pairs={{1,0},{2,1},{3,2},{4,3},{5,4},{6,5},{7,6},{8,7},{9,8},{10,9},{11,1... | collective-permute-start | bytes 98312 | tf_op jit(solution)/shard_map/ppermute | solution.py:651
  102.2 4.2 %copy-start.9 = (f32[64,128]{1,0:T(8,128)}, f32[64,128]{1,0:T(8,128)S(1)}, u32[]{:S(2)}) copy-start(f32[64,128]{1,0:T(8,128)S(1)} %collective-permute-done.3.below_ref) | copy-start | bytes 98308
  106.5 0.6 copy-start.11
  111.0 3.5 %collective-permute-start.5 = (f32[64,128]{1,0:T(8,128)S(1)}, f32[64,128]{1,0:T(8,128)S(1)}, u32[]{:S(2)}, u32[]{:S(2)}) collective-permute-start(f32[64,128]{1,0:T(8,128)S(1)} %get-tuple-element.46), channel_id=1, source_target_pairs={{0,1},{1,2},{2,3},{3,4},{4,5},{5,6},{6,7},{7,8},{8,9},{9,10},{10,1... | collective-permute-start | bytes 98312 | tf_op jit(solution)/shard_map/ppermute | solution.py:651
  112.9 5.8 %collective-permute-start.6 = (f32[64,128]{1,0:T(8,128)S(1)}, f32[64,128]{1,0:T(8,128)S(1)}, u32[]{:S(2)}, u32[]{:S(2)}) collective-permute-start(f32[64,128]{1,0:T(8,128)S(1)} %get-tuple-element.45), channel_id=1, source_target_pairs={{1,0},{2,1},{3,2},{4,3},{5,4},{6,5},{7,6},{8,7},{9,8},{10,9},{11,1... | collective-permute-start | bytes 98312 | tf_op jit(solution)/shard_map/ppermute | solution.py:651
  114.5 4.2 %copy-start.8 = (f32[64,128]{1,0:T(8,128)}, f32[64,128]{1,0:T(8,128)S(1)}, u32[]{:S(2)}) copy-start(f32[64,128]{1,0:T(8,128)S(1)} %collective-permute-done.5.below_ref) | copy-start | bytes 98308
  123.2 32.7 %collective-permute-start.7 = (f32[64,128]{1,0:T(8,128)S(1)}, f32[64,128]{1,0:T(8,128)S(1)}, u32[]{:S(2)}, u32[]{:S(2)}) collective-permute-start(f32[64,128]{1,0:T(8,128)S(1)} %get-tuple-element.44), channel_id=1, source_target_pairs={{0,1},{1,2},{2,3},{3,4},{4,5},{5,6},{6,7},{7,8},{8,9},{9,10},{10,1... | collective-permute-start | bytes 98312 | tf_op jit(solution)/shard_map/ppermute | solution.py:651
  125.5 30.4 %collective-permute-start.8 = (f32[64,128]{1,0:T(8,128)S(1)}, f32[64,128]{1,0:T(8,128)S(1)}, u32[]{:S(2)}, u32[]{:S(2)}) collective-permute-start(f32[64,128]{1,0:T(8,128)S(1)} %get-tuple-element.43), channel_id=1, source_target_pairs={{1,0},{2,1},{3,2},{4,3},{5,4},{6,5},{7,6},{8,7},{9,8},{10,9},{11,1... | collective-permute-start | bytes 98312 | tf_op jit(solution)/shard_map/ppermute | solution.py:651
  155.9 0.6 copy-start.7
  (3 other events, 1.8 us)

commit v2 on v1

--- a/solution.py
+++ b/solution.py
@@ -14,11 +14,24 @@
 CAP = 1024
 FIELDS = 5
 LANES = 128
-BLOCK = 256
-ALIGNED = [[4 * g + t for t in range(4)] for g in range(16)]
-SHIFTED = [[(4 * g + 2 + t) % N_DOM for t in range(4)] for g in range(16)]
-UP = [(i, i + 1) for i in range(N_DOM - 1)]
-DOWN = [(i + 1, i) for i in range(N_DOM - 1)]
+BLOCK = 512
+CHUNK = 104
+
+
+def both_ways(lows, distance):
+    return [pair for q in lows for pair in ((q, q + distance), (q + distance, q))]
+
+
+CROSS_1 = both_ways(range(1, N_DOM - 1, 2), 1)
+INNER_1 = both_ways(range(0, N_DOM - 1, 2), 1)
+CROSS_2 = both_ways([q for q in range(N_DOM - 2) if q % 4 >= 2], 2)
+INNER_2 = both_ways([q for q in range(N_DOM - 2) if q % 4 < 2], 2)
+
+
+def from_above(q):
+    odd = q % 2 == 1
+    late = q % 4 >= 2
+    return odd, jnp.logical_not(odd), late, jnp.logical_not(late)
 
 
 def legendre_pair(values, degree):
@@ -162,7 +175,18 @@
     return jnp.where(iota((1, LANES), 1) == at, value, 0.0)
 
 
-def route_kernel(place_ref, weights_ref, owner_ref, element_ref, near_ref, far_ref, moves_ref, slots_ref):
+def by_side(q, cross_1, inner_1, cross_2=None, inner_2=None):
+    above = from_above(q)
+    out = (jnp.where(above[0], inner_1, cross_1), jnp.where(above[0], cross_1, inner_1))
+    if cross_2 is not None:
+        out += (jnp.where(above[2], inner_2, cross_2), jnp.where(above[2], cross_2, inner_2))
+    return out
+
+
+def route_kernel(
+    place_ref, weights_ref, owner_ref, element_ref, geometry_ref, wall_ref, forcing_ref,
+    cross_1_ref, inner_1_ref, cross_2_ref, inner_2_ref, own_ref, moves_ref, slots_ref,
+):
     q = place_ref[0]
     width = N_REC
     lane = iota((8, width), 1)
@@ -181,7 +205,7 @@
     for i in range(1, 8):
         node = jnp.where(node_rows == i, float(NODES[i]), node)
     coords = [jnp.sum(weights_ref[d] * node, axis=0, keepdims=True) for d in range(3)]
-    words = element_ref[...].astype(jnp.float32)
+    words = element_ref[...].astype(jnp.float32) + 1.0
     base = jnp.where(row % 4 == 3, words, 0.0)
     for d in range(3):
         base = jnp.where(row % 4 == d, coords[d], base)
@@ -198,20 +222,27 @@
             packs[n] = jnp.where(first == 1, pltpu.roll(packs[n], width - step, 1), packs[n])
         moves = jnp.where(moved == 1, incoming, jnp.where((moves >> b) & 1 == 1, 0, moves))
     moves_ref[...] = moves[:, :CAP]
-    slots_ref[...] = jnp.full(slots_ref.shape, -1.0, jnp.float32)
     lane = iota((4, CAP), 1)
     for s in range(5):
         at = (s % 2) * 4
-        slots_ref[s + 4] = jnp.where(
-            lane < totals[s : s + 1, :], packs[s // 2][at : at + 4, :CAP], -1.0
-        )
-    r = q % 4
-    rs = (q + 2) % 4
-    for t in range(4):
-        near_ref[t] = slots_ref[t - r + 6]
-        off = t - rs
-        inside = (r + off >= 0) & (r + off <= 3)
-        far_ref[t] = slots_ref[jnp.where(inside, 0, off + 6)]
+        slot = jnp.where(lane < totals[s : s + 1, :], packs[s // 2][at : at + 4, :CAP], 0.0)
+        for c in range(8):
+            slots_ref[s, 4 * c : 4 * c + 4, :] = slot[:, c * LANES : (c + 1) * LANES]
+    above = from_above(q)
+    bottom, top = forcing_ref[0:64, :], forcing_ref[448:512, :]
+    spread = jnp.where(iota((8, LANES), 1) % 8 == iota((8, LANES), 0), 1.0, 0.0)
+    wall = lax.dot(
+        wall_ref[...].astype(jnp.float32), spread, preferred_element_type=jnp.float32
+    )
+    for target_ref, up in ((cross_1_ref, above[0]), (inner_1_ref, above[1])):
+        target_ref[0:32, :] = jnp.where(up, slots_ref[3], slots_ref[1])
+        target_ref[32:36, :] = geometry_ref[...]
+        target_ref[36:38, :] = wall
+        target_ref[38:40, :] = jnp.zeros((2, LANES), jnp.float32)
+        target_ref[40:104, :] = jnp.where(up, top, bottom)
+    for target_ref, up in ((cross_2_ref, above[2]), (inner_2_ref, above[3])):
+        target_ref[...] = jnp.where(up, slots_ref[4], slots_ref[0])
+    own_ref[...] = slots_ref[2]
 
 
 def split_kernel(fields_ref, out_ref):
@@ -242,54 +273,57 @@
     return out
 
 
-def eval_kernel(near_ref, far_ref, fields_ref, near_out_ref, far_out_ref):
-    for source, target in ((near_ref, near_out_ref), (far_ref, far_out_ref)):
-        valid = (source[:, 3, :] >= 0.0).astype(jnp.int32)
-        for c in range(4):
-            blocks = (jnp.sum(valid[c : c + 1, :]) + BLOCK - 1) // BLOCK
-
-            def one_block(b, carry, c=c, source=source, target=target):
-                start = pl.multiple_of(b * BLOCK, BLOCK)
-                words = source[c, :, pl.ds(start, BLOCK)]
-                element = words[3:4, :].astype(jnp.int32)
-                hot = (iota((LANES, BLOCK), 0) == element).astype(jnp.float32).astype(jnp.bfloat16)
-                hot = jnp.concatenate([hot, hot], axis=0)
-                along = [basis_rows(words[d : d + 1, :]) for d in range(3)]
-                row = iota((8, BLOCK), 0)
-                wx = jnp.broadcast_to(along[0][0], (8, BLOCK))
-                for i in range(1, 8):
-                    wx = jnp.where(row == i, along[0][i], wx)
-                for f in range(FIELDS):
-                    picked = lax.dot(
-                        fields_ref[f], hot, preferred_element_type=jnp.float32
-                    )
-                    over_k = picked[0:64, :] * along[2][0]
-                    for k in range(1, 8):
-                        over_k = over_k + picked[64 * k : 64 * k + 64, :] * along[2][k]
-                    over_j = over_k[0:8, :] * along[1][0]
-                    for j in range(1, 8):
-                        over_j = over_j + over_k[8 * j : 8 * j + 8, :] * along[1][j]
-                    target[c, f : f + 1, pl.ds(start, BLOCK)] = jnp.sum(
-                        over_j * wx, axis=0, keepdims=True
-                    )
-                return carry
-
-            lax.fori_loop(0, blocks, one_block, 0)
-
-
-def unpack_kernel(place_ref, near_ref, far_ref, moves_ref, owner_ref, out_ref):
+def eval_kernel(*refs):
+    sources, fields_ref, targets = refs[0:5], refs[5], refs[6:11]
+    for source, target in zip(sources, targets):
+        words = source[0:32, :]
+        valid = jnp.where((iota((32, LANES), 0) % 4 == 3) & (words > 0.0), 1, 0)
+        blocks = (jnp.sum(valid) + BLOCK - 1) // BLOCK
+
+        def one_block(b, carry, source=source, target=target):
+            start = pl.multiple_of(b * BLOCK, BLOCK)
+            tiles = source[pl.ds(pl.multiple_of(b * 16, 16), 16), :]
+            words = jnp.concatenate([tiles[4 * n : 4 * n + 4, :] for n in range(4)], axis=1)
+            element = words[3:4, :].astype(jnp.int32) - 1
+            hot = (iota((LANES, BLOCK), 0) == element).astype(jnp.float32).astype(jnp.bfloat16)
+            hot = jnp.concatenate([hot, hot], axis=0)
+            along = [basis_rows(words[d : d + 1, :]) for d in range(3)]
+            row = iota((8, BLOCK), 0)
+            wx = jnp.broadcast_to(along[0][0], (8, BLOCK))
+            for i in range(1, 8):
+                wx = jnp.where(row == i, along[0][i], wx)
+            for f in range(FIELDS):
+                picked = lax.dot(
+                    fields_ref[f], hot, preferred_element_type=jnp.float32
+                )
+                over_k = picked[0:64, :] * along[2][0]
+                for k in range(1, 8):
+                    over_k = over_k + picked[64 * k : 64 * k + 64, :] * along[2][k]
+                over_j = over_k[0:8, :] * along[1][0]
+                for j in range(1, 8):
+                    over_j = over_j + over_k[8 * j : 8 * j + 8, :] * along[1][j]
+                target[f : f + 1, pl.ds(start, BLOCK)] = jnp.sum(
+                    over_j * wx, axis=0, keepdims=True
+                )
+            return carry
+
+        lax.fori_loop(0, blocks, one_block, 0)
+
+
+def unpack_kernel(
+    place_ref, cross_1_ref, inner_1_ref, cross_2_ref, inner_2_ref, own_ref, moves_ref, owner_ref,
+    out_ref, share_ref,
+):
     q = place_ref[0]
-    r = q % 4
-    rs = (q + 2) % 4
     width = N_REC
+    below_1, above_1, below_2, above_2 = by_side(
+        q, cross_1_ref[...], inner_1_ref[...], cross_2_ref[...], inner_2_ref[...]
+    )
     zeros = jnp.zeros((FIELDS, CAP), jnp.float32)
-    values = []
-    for s in range(5):
-        off = s - 2
-        inside = (r + off >= 0) & (r + off <= 3)
-        near = near_ref[jnp.clip(r + off, 0, 3)]
-        far = far_ref[jnp.clip(rs + off, 0, 3)]
-        values.append(jnp.concatenate([jnp.where(inside, near, far), zeros], axis=1))
+    values = [
+        jnp.concatenate([value, zeros], axis=1)
+        for value in (below_2, below_1, own_ref[...], above_1, above_2)
+    ]
     moves = jnp.concatenate([moves_ref[...], jnp.zeros((8, CAP), jnp.int32)], axis=1)
     for b in range(10, -1, -1):
         step = 1 << b
@@ -304,13 +338,18 @@
     for s in range(1, 5):
         out = jnp.where(distance == s, values[s], out)
     out_ref[...] = out
+    for n in range(16):
+        share_ref[n : n + 1, :] = out[0:1, n * LANES : (n + 1) * LANES]
 
 
 def prep_kernel(
-    place_ref, geometry_ref, wall_ref, forcing_ref, below_ref, above_ref,
-    inverse_ref, free_ref, load_ref, plane_ref,
+    place_ref, geometry_ref, wall_ref, forcing_ref, cross_ref, inner_ref,
+    inverse_ref, free_ref, load_ref, beside_ref, plane_ref, below_ref, above_ref,
 ):
     q = place_ref[0]
+    below_ref[...], above_ref[...] = by_side(q, cross_ref[32:104, :], inner_ref[32:104, :])
+    beside_ref[0:8, :] = below_ref[0:8, :]
+    beside_ref[8:16, :] = above_ref[0:8, :]
     wcol = w_column()
     scol = s_column()
 
@@ -339,7 +378,11 @@
         sum_xy(plane_ref, 1)
         return plane_ref[...]
 
-    wall = wall_plane(wall_ref[0:1, :], wall_ref[1:2, :])
+    spread = jnp.where(lane % 8 == row, 1.0, 0.0)
+    flags = lax.dot(
+        wall_ref[...].astype(jnp.float32), spread, preferred_element_type=jnp.float32
+    )
+    wall = wall_plane(flags[0:1, :], flags[1:2, :])
     wall_below = wall_plane(below[4:5, :], below[5:6, :])
     wall_above = wall_plane(above[4:5, :], above[5:6, :])
     mark = jnp.where(
@@ -423,34 +466,39 @@
 
 
 def first_kernel(
-    place_ref, near_ref, far_ref, geometry_ref, below_ref, above_ref, inverse_ref, free_ref,
-    load_ref, xmat_ref, w_ref, u_ref, edge_ref, moments_ref, v_ref, face_ref,
+    place_ref, own_ref, cross_1_ref, inner_1_ref, cross_2_ref, inner_2_ref, geometry_ref,
+    beside_ref, inverse_ref, free_ref, load_ref, xmat_ref, w_ref, u_ref, edge_ref, moments_ref, cross_ref, inner_ref, v_ref, face_ref,
 ):
     q = place_ref[0]
-    r = q % 4
-    rs = (q + 2) % 4
-    pick_row = iota((16, LANES), 0)
-    pick_lane = iota((16, LANES), 1)
+    below_1, above_1, below_2, above_2 = by_side(
+        q, cross_1_ref[...], inner_1_ref[...], cross_2_ref[...], inner_2_ref[...]
+    )
+    pick_row = iota((8, LANES), 0)
+    pick_lane = iota((8, LANES), 1)
     picks = [
-        jnp.where(pick_lane == pick_row * 8 + (0 if s == 0 else 7), 1.0, 0.0) for s in range(2)
+        [
+            jnp.where(pick_lane == pick_row * 16 + (8 * odd + 7 * s), 1.0, 0.0)
+            for odd in range(2)
+        ]
+        for s in range(2)
     ]
 
-    def planes(off):
-        inside = (r + off >= 0) & (r + off <= 3)
-        exists = (q + off >= 0) & (q + off < N_DOM)
-        near = near_ref[jnp.clip(r + off, 0, 3)]
-        far = far_ref[jnp.clip(rs + off, 0, 3)]
-        values = jnp.where(exists, jnp.where(inside, near, far), 0.0)
+    def planes(values):
         out = []
         for s in range(2):
-            plane = lax.dot_general(
-                values[16 * s : 16 * s + 16, :], picks[s], (((0,), (0,)), ((), ())),
-                precision=HIGHEST, preferred_element_type=jnp.float32,
-            )
+            halves = [
+                lax.dot_general(
+                    values[8 * s : 8 * s + 8, :], picks[s][odd], (((0,), (0,)), ((), ())),
+                    precision=HIGHEST, preferred_element_type=jnp.float32,
+                )
+                for odd in range(2)
+            ]
+            plane = halves[0][0:64, :] + halves[1][64:128, :]
             out.append([plane[8 * k : 8 * k + 8, :] for k in range(8)])
         return out
 
-    received = {off: planes(off) for off in range(-2, 3)}
+    layers = (below_2, below_1, own_ref[...], above_1, above_2)
+    received = {off: planes(values) for off, values in zip(range(-2, 3), layers)}
     lane = iota((8, LANES), 1)
     j_row = iota((8, LANES), 0)
     low = (j_row == 0) & (lane >= 8)
@@ -486,7 +534,7 @@
     zero = jnp.zeros((64, LANES), jnp.float32)
     for k in range(8):
         v_ref[64 * k : 64 * k + 64, :] = zero
-    for off, geometry, plane in ((-1, below_ref[0:4, :], 7), (1, above_ref[0:4, :], 0)):
+    for off, geometry, plane in ((-1, beside_ref[0:4, :], 7), (1, beside_ref[8:12, :], 0)):
         sides = boundary(off)
         v_ref[pl.ds(0, 64, stride=8), :] = sides[0]
         v_ref[pl.ds(7, 64, stride=8), :] = sides[1]
@@ -509,31 +557,42 @@
         q, w_ref, inverse_ref, geometry_ref, xmat_ref, v_ref, u_ref, 0,
         jnp.zeros((1, LANES), jnp.float32),
     )
+    send_faces(q, u_ref, cross_ref, inner_ref)
+
+
+def send_faces(q, u_ref, cross_ref, inner_ref):
+    up = from_above(q)[0]
+    bottom, top = u_ref[0:64, :], u_ref[448:512, :]
+    cross_ref[...] = jnp.where(up, top, bottom)
+    inner_ref[...] = jnp.where(up, bottom, top)
 
 
 def next_kernel(
-    at, last, place_ref, w_old_ref, u_old_ref, below_ref, above_ref, geometry_ref, inverse_ref,
-    free_ref, xmat_ref, moments_old_ref, w_ref, u_ref, moments_ref, v_ref,
+    at, place_ref, w_old_ref, u_old_ref, cross_in_ref, inner_in_ref, geometry_ref, inverse_ref,
+    free_ref, xmat_ref, moments_old_ref, w_ref, u_ref, moments_ref, cross_ref, inner_ref, v_ref,
 ):
     q = place_ref[0]
+    below, above = by_side(q, cross_in_ref[...], inner_in_ref[...])
     for k in range(8):
         rows = slice(64 * k, 64 * k + 64)
         image = u_old_ref[rows, :]
         if k == 0:
-            image = image + below_ref[...]
+            image = image + below
         if k == 7:
-            image = image + above_ref[...]
+            image = image + above
         w_ref[rows, :] = free_ref[rows, :] * image - w_old_ref[rows, :]
     row = krylov_step(
         q, w_ref, inverse_ref, geometry_ref, xmat_ref, v_ref, u_ref, at, moments_old_ref[...]
     )
     moments_ref[...] = jnp.broadcast_to(row, moments_ref.shape)
+    send_faces(q, u_ref, cross_ref, inner_ref)
 
 
 def last_kernel(
-    w0_ref, w1_ref, w2_ref, u_ref, below_ref, above_ref, inverse_ref, free_ref, edge_ref,
-    moments_ref, velocity_ref, residual_ref,
+    place_ref, w0_ref, w1_ref, w2_ref, u_ref, cross_in_ref, inner_in_ref, inverse_ref, free_ref,
+    edge_ref, moments_ref, velocity_ref, residual_ref,
 ):
+    below, above = by_side(place_ref[0], cross_in_ref[...], inner_in_ref[...])
     sums = jnp.sum(moments_ref[...], axis=0, keepdims=True)
     h0, a0, h2, a1, h4, a2 = [sums[:, m : m + 1] for m in range(6)]
     h1, h3 = a0 - h0, a1 - h2
@@ -555,9 +614,9 @@
         rows = slice(64 * k, 64 * k + 64)
         image = u_ref[rows, :]
         if k == 0:
-            image = image + below_ref[...]
+            image = image + below
         if k == 7:
-            image = image + above_ref[...]
+            image = image + above
         w0, w1, w2 = w0_ref[rows, :], w1_ref[rows, :], w2_ref[rows, :]
         velocity_ref[rows, :] = inverse_ref[rows, :] * (c0 * w0 + c1 * w1 + c2 * w2)
         residual_ref[rows, :] = (
@@ -572,7 +631,7 @@
 SMEM = pl.BlockSpec(memory_space=pltpu.SMEM)
 
 
-def call(kernel, operands, outs, scratch=(), flops=100_000, smem_first=True, name=None):
+def call(kernel, operands, outs, scratch=(), flops=100_000, smem_first=True, name=None, mib=12):
     specs = [VMEM] * len(operands)
     if smem_first:
         specs[0] = SMEM
@@ -584,6 +643,7 @@
         out_specs=[VMEM] * len(outs),
         scratch_shapes=[pltpu.VMEM(shape, dtype) for shape, dtype in scratch],
         cost_estimate=pl.CostEstimate(flops=flops, bytes_accessed=1_000_000, transcendentals=0),
+        compiler_params=pltpu.CompilerParams(vmem_limit_bytes=mib * 1024 * 1024),
         name=name,
     )(*operands)
 
@@ -596,8 +656,10 @@
     return lax.all_to_all(value, "dom", 0, 0, tiled=True)
 
 
-def to_group(value, groups):
-    return lax.all_to_all(value, "dom", 0, 0, tiled=True, axis_index_groups=groups)
+def to_neighbours(cross_1, inner_1, cross_2=None, inner_2=None):
+    lists = ((cross_1, CROSS_1), (cross_2, CROSS_2), (inner_1, INNER_1), (inner_2, INNER_2))
+    moved = [None if value is None else lax.ppermute(value, "dom", pairs) for value, pairs in lists]
+    return [moved[n] for n in (0, 2, 1, 3) if moved[n] is not None]
 
 
 def body(donor_fields, interp_weights, donor_owner, donor_element, geometry, wall_flag, forcing):
@@ -606,66 +668,54 @@
     donors = lax.ppermute(donor_fields, "mesh", [(0, 1), (1, 0)])
     owner = donor_owner.reshape(1, N_REC)
     element = donor_element.reshape(1, N_REC)
-    near, far, moves = call(
-        route_kernel, (place, interp_weights, owner, element),
-        (((4, 4, CAP), F32), ((4, 4, CAP), F32), ((8, CAP), jnp.int32)),
-        scratch=(((13, 4, CAP), F32),), name="route",
-    )
-    near_in = to_group(near, ALIGNED)
-    far_in = to_group(far, SHIFTED)
-
-    wall = jnp.tile(wall_flag.astype(F32), (1, 16))
-    head = jnp.concatenate([geometry, wall, jnp.zeros((2, LANES), F32)], 0)
-    below = lax.ppermute(jnp.concatenate([head, forcing[448:512]], 0), "dom", UP)
-    above = lax.ppermute(jnp.concatenate([head, forcing[0:64]], 0), "dom", DOWN)
-    inverse, free, load = call(
-        prep_kernel, (place, geometry, wall, forcing, below, above),
-        (FIELD, FIELD, FIELD), scratch=(((64, LANES), F32),), name="prep",
-    )
+    asked = ((32, LANES), F32)
+    with_head = ((CHUNK, LANES), F32)
+    *requests, own, moves = call(
+        route_kernel, (place, interp_weights, owner, element, geometry, wall_flag, forcing),
+        (with_head, with_head, asked, asked, asked, ((8, CAP), jnp.int32)),
+        scratch=(((5, 32, LANES), F32),), name="route", mib=60,
+    )
+    requests = to_neighbours(*requests)
     (fields,) = call(
         split_kernel, (donors,), (((FIELDS, 512, 256), jnp.bfloat16),), smem_first=False,
         name="split",
     )
-    near_out, far_out = call(
-        eval_kernel, (near_in, far_in, fields),
-        (((4, FIELDS, CAP), F32), ((4, FIELDS, CAP), F32)),
-        flops=7_000_000_000, smem_first=False, name="evaluate",
-    )
-    near_back = to_group(near_out, ALIGNED)
-    far_back = to_group(far_out, SHIFTED)
-    (interface,) = call(
-        unpack_kernel, (place, near_back, far_back, moves, owner), (((FIELDS, N_REC), F32),),
-        name="unpack",
-    )
-    received = jnp.broadcast_to(interface[0].reshape(1, 32, 64), (4, 32, 64))
-    near_rec = to_group(received, ALIGNED)
-    far_rec = to_group(received, SHIFTED)
-    w0, u, edge, moments = call(
+    answers = call(
+        eval_kernel, (*requests, own, fields), (((FIELDS, CAP), F32),) * 5,
+        flops=7_000_000_000, smem_first=False, name="evaluate", mib=24,
+    )
+    answered = to_neighbours(*answers[0:4])
+    inverse, free, load, beside = call(
+        prep_kernel, (place, geometry, wall_flag, forcing, requests[0], requests[1]),
+        (FIELD, FIELD, FIELD, ((16, LANES), F32)),
+        scratch=(((64, LANES), F32), ((72, LANES), F32), ((72, LANES), F32)), name="prep",
+    )
+    interface, share = call(
+        unpack_kernel, (place, *answered, answers[4], moves, owner),
+        (((FIELDS, N_REC), F32), ((16, LANES), F32)), name="unpack",
+    )
+    face = ((64, LANES), F32)
+    w0, u, edge, moments, *faces = call(
         first_kernel,
-        (place, near_rec, far_rec, geometry, below, above, inverse, free, load, xmat),
-        (FIELD, FIELD, ((128, LANES), F32), ((1, LANES), F32)),
+        (place, share, *to_neighbours(share, share, share, share), geometry, beside, inverse, free,
+         load, xmat),
+        (FIELD, FIELD, ((128, LANES), F32), ((1, LANES), F32), face, face),
         scratch=(FIELD, ((128, LANES), F32)), name="first",
     )
-
-    def halo(u):
-        return lax.ppermute(u[448:512], "dom", UP), lax.ppermute(u[0:64], "dom", DOWN)
-
     ws = [w0]
     for step in (1, 2):
-        from_below, from_above = halo(u)
-        w, u, moments = call(
-            functools.partial(next_kernel, 2 * step, step == 2),
-            (place, ws[-1], u, from_below, from_above, geometry, inverse, free, xmat, moments),
-            (FIELD, FIELD, ((1 if step == 1 else N_DOM, LANES), F32)),
+        w, u, moments, *faces = call(
+            functools.partial(next_kernel, 2 * step),
+            (place, ws[-1], u, *to_neighbours(*faces), geometry, inverse, free, xmat, moments),
+            (FIELD, FIELD, ((1 if step == 1 else N_DOM, LANES), F32), face, face),
             scratch=(FIELD,), name=f"next{step}",
         )
         ws.append(w)
-    from_below, from_above = halo(u)
+    faces = to_neighbours(*faces)
     sums = to_all(moments)
     velocity, residual = call(
-        last_kernel,
-        (*ws, u, from_below, from_above, inverse, free, edge, sums),
-        (FIELD, FIELD), smem_first=False, name="last",
+        last_kernel, (place, *ws, u, *faces, inverse, free, edge, sums),
+        (FIELD, FIELD), name="last",
     )
     return velocity, residual, interface
 

time: 162 us -> 116 us (0.72)
  blocking collectives: 49.5 us -> 30.9 us
  Pallas kernels: 33.4 us -> 15.9 us
  local copies, waits for them, and re-layouts: 13.1 us -> 0.04 us
  starting transfers between devices: 50.4 us -> 59.6 us
  waiting for transfers between devices: 10.7 us -> 7.45 us
    ppermute x8 -> x18, starting transfers between devices: 15.3 us -> 59.5 us  [to_neighbours(): lax.ppermute(value, 'dom', pairs)]
    all_to_all x4 -> x0, starting transfers between devices: 35 us -> none  [to_group(): lax.all_to_all(value, 'dom', 0, 0, tiled=True, axis_index_groups=groups)]
    all_to_all x2 -> x0, blocking collectives: 20.4 us -> none  [to_group(): lax.all_to_all(value, 'dom', 0, 0, tiled=True, axis_index_groups=groups)]
    pallas_call x9, Pallas kernels: 33.4 us -> 15.9 us  [call(): pl.pallas_call(kernel, out_shape=out_shape, in_specs=specs, out_specs=[VM...]
    unnamed x32 -> x14, local copies, waits for them, and re-layouts: 8.31 us -> 0.04 us
    slice x5 -> x0, local copies, waits for them, and re-layouts: 3.98 us -> none  [the longest x3 2.34 us: halo(): u[0:64]]
    all_to_all x1, blocking collectives: 29.1 us -> 30.9 us  [to_all(): return lax.all_to_all(value, 'dom', 0, 0, tiled=True)]
    all_to_all x4 -> x0, waiting for transfers between devices: 1.83 us -> none  [to_group(): lax.all_to_all(value, 'dom', 0, 0, tiled=True, axis_index_groups=groups)]
  transfers between devices with their start and end apart: 13 -> 19, of which waited for: 5 -> 4; matrix products, arithmetic and copies ran while one was open for 2% -> 0% of each run, Pallas kernels for 5% -> 4%
where the time goes in v2:
time: 116 us; the launch traced here: 115 us
  starting transfers between devices  59.6 us (51%)
  blocking collectives  30.9 us (27%)
  Pallas kernels  15.9 us (14%)
  waiting for transfers between devices  7.45 us (6%)
    ppermute x18, starting transfers between devices, to_neighbours(): lax.ppermute(value, 'dom', pairs)  59.5 us
    all_to_all x1, blocking collectives, to_all(): return lax.all_to_all(value, 'dom', 0, 0, tiled=True)  30.9 us
    pallas_call x9, Pallas kernels, call(): pl.pallas_call(kernel, out_shape=out_shape, in_specs=specs, out_specs=[VM...  15.9 us
    ppermute x18, waiting for transfers between devices, to_neighbours(): lax.ppermute(value, 'dom', pairs)  7.44 us
  transfers between devices with their start and end apart: 19, of which 4 were waited for; matrix products, arithmetic and copies ran while one was open for 0% of the time, Pallas kernels for 4%

profile of v2, /device:TPU:0, one launch (start us, length us, event | category | flops | bytes accessed | tf_op | source)
XLA Modules:
  0.0 114.8 jit_solution(11839045256186586128)
XLA Ops:
  0.7 3.0 %route.1 = (f32[104,128]{1,0:T(8,128)}, f32[104,128]{1,0:T(8,128)}, f32[32,128]{1,0:T(8,128)}, f32[32,128]{1,0:T(8,128)}, f32[32,128]{1,0:T(8,128)}, /*index=5*/s32[8,1024]{1,0:T(8,128)}) custom-call(s32[1]{0:T(128)} %bitcast.place_ref, f32[3,8,2048]{2,1,0:T(8,128)} %weights_ref.1, s32[1,2048]{1,0:T(1,128)} %bitcast.8, s32[1,2048]{1,0:T(1,128)} %bitcast.11, ...), custom_call_target="tpu_custom_call" | custom-call | flops 100000 | bytes 1000000 | tf_op jit(solution)/shard_map/route/pallas_call | solution.py:639
  4.4 4.6 %collective-permute-start.1 = (f32[104,128]{1,0:T(8,128)}, f32[104,128]{1,0:T(8,128)S(1)}, u32[]{:S(2)}, u32[]{:S(2)}) collective-permute-start(f32[104,128]{1,0:T(8,128)} %get-tuple-element.39), channel_id=1, source_target_pairs={{0,1},{1,0},{2,3},{3,2},{4,5},{5,4},{6,7},{7,6},{8,9},{9,8},{10,11... | collective-permute-start | bytes 159752 | tf_op jit(solution)/shard_map/ppermute | solution.py:661
  9.7 5.8 %collective-permute-start.3 = (f32[32,128]{1,0:T(8,128)}, f32[32,128]{1,0:T(8,128)S(1)}, u32[]{:S(2)}, u32[]{:S(2)}) collective-permute-start(f32[32,128]{1,0:T(8,128)} %get-tuple-element.41), channel_id=1, source_target_pairs={{0,2},{2,0},{1,3},{3,1},{4,6},{6,4},{5,7},{7,5},{8,10},{10,8},{9,1... | collective-permute-start | bytes 49160 | tf_op jit(solution)/shard_map/ppermute | solution.py:661
  15.7 1.6 %collective-permute-done.3.refs_3_ = f32[32,128]{1,0:T(8,128)S(1)} collective-permute-done((f32[32,128]{1,0:T(8,128)}, f32[32,128]{1,0:T(8,128)S(1)}, u32[]{:S(2)}, u32[]{:S(2)}) %collective-permute-start.3) | collective-permute-done | bytes 16416 | tf_op jit(solution)/shard_map/ppermute | solution.py:661
  17.5 3.3 %evaluate.1 = (f32[5,1024]{1,0:T(8,128)S(1)}, f32[5,1024]{1,0:T(8,128)S(1)}, f32[5,1024]{1,0:T(8,128)S(1)}, f32[5,1024]{1,0:T(8,128)S(1)}, f32[5,1024]{1,0:T(8,128)S(1)}) custom-call(f32[104,128]{1,0:T(8,128)S(1)} %collective-permute-done.refs_0_.cross_ref, f32[104,128]{1,0:T(8,128)S(1)} %collective-permute-done.1.refs_1_.inner_ref, ...), custom_call_target="tpu_custom_call" | custom-call | flops 7000000000 | bytes 1000000 | tf_op jit(solution)/shard_map/evaluate/pallas_call | solution.py:639
  20.8 0.7 collective-permute-start.5
  21.5 8.4 %collective-permute-start.6 = (f32[5,1024]{1,0:T(8,128)S(1)}, f32[5,1024]{1,0:T(8,128)S(1)}, u32[]{:S(2)}, u32[]{:S(2)}) collective-permute-start(f32[5,1024]{1,0:T(8,128)S(1)} %get-tuple-element.44), channel_id=1, source_target_pairs={{0,1},{1,0},{2,3},{3,2},{4,5},{5,4},{6,7},{7,6},{8,9},{9,8},{10,11... | collective-permute-start | bytes 61448 | tf_op jit(solution)/shard_map/ppermute | solution.py:661
  30.5 5.0 %collective-permute-start.8 = (f32[5,1024]{1,0:T(8,128)S(1)}, f32[5,1024]{1,0:T(8,128)S(1)}, u32[]{:S(2)}, u32[]{:S(2)}) collective-permute-start(f32[5,1024]{1,0:T(8,128)S(1)} %get-tuple-element.46), channel_id=1, source_target_pairs={{0,2},{2,0},{1,3},{3,1},{4,6},{6,4},{5,7},{7,5},{8,10},{10,8},{9,1... | collective-permute-start | bytes 61448 | tf_op jit(solution)/shard_map/ppermute | solution.py:661
  35.6 1.9 %collective-permute-done.8.inner_2_ref = f32[5,1024]{1,0:T(8,128)S(1)} collective-permute-done((f32[5,1024]{1,0:T(8,128)S(1)}, f32[5,1024]{1,0:T(8,128)S(1)}, u32[]{:S(2)}, u32[]{:S(2)}) %collective-permute-start.8) | collective-permute-done | bytes 20512 | tf_op jit(solution)/shard_map/ppermute | solution.py:661
  37.4 1.5 %unpack.1 = (f32[5,2048]{1,0:T(8,128)}, f32[16,128]{1,0:T(8,128)S(1)}) custom-call(s32[1]{0:T(128)} %bitcast.place_ref, f32[5,1024]{1,0:T(8,128)S(1)} %collective-permute-done.5.cross_1_ref, f32[5,1024]{1,0:T(8,128)S(1)} %collective-permute-done.6.inner_1_ref, f32[5,1024]{1,0:T(8,128)S(1)} %collective-permute-done.7.cross_2_ref, ...), custom_call_target="tpu_custom_call" | custom-call | flops 100000 | bytes 1000000 | tf_op jit(solution)/shard_map/unpack/pallas_call | solution.py:639
  38.9 2.0 %collective-permute-start.10 = (f32[16,128]{1,0:T(8,128)S(1)}, f32[16,128]{1,0:T(8,128)S(1)}, u32[]{:S(2)}, u32[]{:S(2)}) collective-permute-start(f32[16,128]{1,0:T(8,128)S(1)} %get-tuple-element.49.own_ref), channel_id=1, source_target_pairs={{0,1},{1,0},{2,3},{3,2},{4,5},{5,4},{6,7},{7,6},{8,9},{9,8},{10,11... | collective-permute-start | bytes 24584 | tf_op jit(solution)/shard_map/ppermute | solution.py:661
  41.6 8.5 %collective-permute-start.12 = (f32[16,128]{1,0:T(8,128)S(1)}, f32[16,128]{1,0:T(8,128)S(1)}, u32[]{:S(2)}, u32[]{:S(2)}) collective-permute-start(f32[16,128]{1,0:T(8,128)S(1)} %get-tuple-element.49.own_ref), channel_id=1, source_target_pairs={{0,2},{2,0},{1,3},{3,1},{4,6},{6,4},{5,7},{7,5},{8,10},{10,8},{9,1... | collective-permute-start | bytes 24584 | tf_op jit(solution)/shard_map/ppermute | solution.py:661
  50.1 0.8 collective-permute-start.9
  51.0 0.9 prep.1
  52.0 3.1 %first.1 = (f32[512,128]{1,0:T(8,128)S(1)}, f32[512,128]{1,0:T(8,128)S(1)}, f32[128,128]{1,0:T(8,128)S(1)}, f32[1,128]{1,0:T(1,128)S(1)}, f32[64,128]{1,0:T(8,128)S(1)}, /*index=5*/f32[64,128]{1,0:T(8,128)S(1)}) custom-call(s32[1]{0:T(128)} %bitcast.place_ref, f32[16,128]{1,0:T(8,128)S(1)} %get-tuple-element.49.own_ref, ...), custom_call_target="tpu_custom_call" | custom-call | flops 100000 | bytes 1000000 | tf_op jit(solution)/shard_map/first/pallas_call | solution.py:639
  55.8 5.7 %collective-permute-start.14 = (f32[64,128]{1,0:T(8,128)S(1)}, f32[64,128]{1,0:T(8,128)S(1)}, u32[]{:S(2)}, u32[]{:S(2)}) collective-permute-start(f32[64,128]{1,0:T(8,128)S(1)} %get-tuple-element.57), channel_id=1, source_target_pairs={{0,1},{1,0},{2,3},{3,2},{4,5},{5,4},{6,7},{7,6},{8,9},{9,8},{10,11... | collective-permute-start | bytes 98312 | tf_op jit(solution)/shard_map/ppermute | solution.py:661
  61.5 1.9 %collective-permute-done.14.inner_in_ref = f32[64,128]{1,0:T(8,128)S(1)} collective-permute-done((f32[64,128]{1,0:T(8,128)S(1)}, f32[64,128]{1,0:T(8,128)S(1)}, u32[]{:S(2)}, u32[]{:S(2)}) %collective-permute-start.14) | collective-permute-done | bytes 32800 | tf_op jit(solution)/shard_map/ppermute | solution.py:661
  63.4 1.0 next1.1
  65.1 8.1 %collective-permute-start.16 = (f32[64,128]{1,0:T(8,128)S(1)}, f32[64,128]{1,0:T(8,128)S(1)}, u32[]{:S(2)}, u32[]{:S(2)}) collective-permute-start(f32[64,128]{1,0:T(8,128)S(1)} %get-tuple-element.62), channel_id=1, source_target_pairs={{0,1},{1,0},{2,3},{3,2},{4,5},{5,4},{6,7},{7,6},{8,9},{9,8},{10,11... | collective-permute-start | bytes 98312 | tf_op jit(solution)/shard_map/ppermute | solution.py:661
  73.2 2.0 %collective-permute-done.16.inner_in_ref = f32[64,128]{1,0:T(8,128)S(1)} collective-permute-done((f32[64,128]{1,0:T(8,128)S(1)}, f32[64,128]{1,0:T(8,128)S(1)}, u32[]{:S(2)}, u32[]{:S(2)}) %collective-permute-start.16) | collective-permute-done | bytes 32800 | tf_op jit(solution)/shard_map/ppermute | solution.py:661
  75.2 1.0 next2.1
  76.9 5.4 %collective-permute-start.18 = (f32[64,128]{1,0:T(8,128)S(1)}, f32[64,128]{1,0:T(8,128)S(1)}, u32[]{:S(2)}, u32[]{:S(2)}) collective-permute-start(f32[64,128]{1,0:T(8,128)S(1)} %get-tuple-element.67), channel_id=1, source_target_pairs={{0,1},{1,0},{2,3},{3,2},{4,5},{5,4},{6,7},{7,6},{8,9},{9,8},{10,11... | collective-permute-start | bytes 98312 | tf_op jit(solution)/shard_map/ppermute | solution.py:661
  82.3 30.9 %all_to_all.11 = f32[64,1,128]{2,1,0:T(1,128)S(1)} all-to-all(f32[64,1,128]{2,1,0:T(1,128)S(1)} %bitcast.10), channel_id=1, replica_groups=mesh['mesh'=2,'dom'=64] {'dom'}, dimensions={0} | all-to-all | bytes 65536 | tf_op jit(solution)/shard_map/all_to_all | solution.py:656
  113.2 1.6 %last.1 = (f32[512,128]{1,0:T(8,128)}, f32[512,128]{1,0:T(8,128)}) custom-call(s32[1]{0:T(128)} %bitcast.place_ref, f32[512,128]{1,0:T(8,128)S(1)} %get-tuple-element.54.w_old_ref.w0_ref, f32[512,128]{1,0:T(8,128)S(1)} %get-tuple-element.59.w_old_ref.w1_ref, f32[512,128]{1,0:T(8,128)S(1)} %get-tuple-element.64.w2_ref, ...), custom_call_target="tpu_custom_call" | custom-call | flops 100000 | bytes 1000000 | tf_op jit(solution)/shard_map/last/pallas_call | solution.py:639
  (38 shorter events, 5.0 us)
Async XLA Ops:
  0.6 14.8 %collective-permute-start.4 = (f32[5,512,128]{2,1,0:T(8,128)}, f32[5,512,128]{2,1,0:T(8,128)S(1)}, u32[]{:S(2)}, u32[]{:S(2)}) collective-permute-start(f32[5,512,128]{2,1,0:T(8,128)} %param.8), channel_id=1, source_target_pairs={{0,64},{64,0},{1,65},{65,1},{2,66},{66,2},{3,67},{67,3},{4,68},{68... | collective-permute-start | bytes 3932168 | tf_op jit(solution)/shard_map/ppermute | solution.py:668
  3.7 13.6 %collective-permute-start = (f32[104,128]{1,0:T(8,128)}, f32[104,128]{1,0:T(8,128)S(1)}, u32[]{:S(2)}, u32[]{:S(2)}) collective-permute-start(f32[104,128]{1,0:T(8,128)} %get-tuple-element.38), channel_id=1, source_target_pairs={{1,2},{2,1},{3,4},{4,3},{5,6},{6,5},{7,8},{8,7},{9,10},{10,9},{11,... | collective-permute-start | bytes 159752 | tf_op jit(solution)/shard_map/ppermute | solution.py:661
  4.4 13.0 %collective-permute-start.1 = (f32[104,128]{1,0:T(8,128)}, f32[104,128]{1,0:T(8,128)S(1)}, u32[]{:S(2)}, u32[]{:S(2)}) collective-permute-start(f32[104,128]{1,0:T(8,128)} %get-tuple-element.39), channel_id=1, source_target_pairs={{0,1},{1,0},{2,3},{3,2},{4,5},{5,4},{6,7},{7,6},{8,9},{9,8},{10,11... | collective-permute-start | bytes 159752 | tf_op jit(solution)/shard_map/ppermute | solution.py:661
  9.0 6.7 %collective-permute-start.2 = (f32[32,128]{1,0:T(8,128)}, f32[32,128]{1,0:T(8,128)S(1)}, u32[]{:S(2)}, u32[]{:S(2)}) collective-permute-start(f32[32,128]{1,0:T(8,128)} %get-tuple-element.40), channel_id=1, source_target_pairs={{2,4},{4,2},{3,5},{5,3},{6,8},{8,6},{7,9},{9,7},{10,12},{12,10},{1... | collective-permute-start | bytes 49160 | tf_op jit(solution)/shard_map/ppermute | solution.py:661
  9.7 7.7 %collective-permute-start.3 = (f32[32,128]{1,0:T(8,128)}, f32[32,128]{1,0:T(8,128)S(1)}, u32[]{:S(2)}, u32[]{:S(2)}) collective-permute-start(f32[32,128]{1,0:T(8,128)} %get-tuple-element.41), channel_id=1, source_target_pairs={{0,2},{2,0},{1,3},{3,1},{4,6},{6,4},{5,7},{7,5},{8,10},{10,8},{9,1... | collective-permute-start | bytes 49160 | tf_op jit(solution)/shard_map/ppermute | solution.py:661
  17.4 20.1 %copy-start.3 = (s32[2048,1]{0,1:T(1,128)S(1)}, s32[2048,1]{0,1:T(1,128)}, u32[]{:S(2)}) copy-start(s32[2048,1]{0,1:T(1,128)} %param.10) | copy-start | bytes 24580
  17.4 33.6 %copy-start.1 = (f32[512,128]{1,0:T(8,128)S(1)}, f32[512,128]{1,0:T(8,128)}, u32[]{:S(2)}) copy-start(f32[512,128]{1,0:T(8,128)} %forcing_ref.3) | copy-start | bytes 786436
  17.4 33.6 %copy-start.2 = (f32[4,128]{1,0:T(4,128)S(1)}, f32[4,128]{1,0:T(4,128)}, u32[]{:S(2)}) copy-start(f32[4,128]{1,0:T(4,128)} %geometry_ref.9) | copy-start | bytes 6148
  17.4 33.6 %copy-start.5 = (s32[2,8]{1,0:T(2,128)S(1)}, s32[2,8]{1,0:T(2,128)}, u32[]{:S(2)}) copy-start(s32[2,8]{1,0:T(2,128)} %wall_ref.3) | copy-start | bytes 196
  17.4 34.5 %copy-start = (f32[512,256]{1,0:T(8,128)S(1)}, f32[512,256]{1,0:T(8,128)}, u32[]{:S(2)}) copy-start(f32[512,256]{1,0:T(8,128)} %constant.6.clone.xmat_ref) | copy-start | bytes 1572868
  20.8 14.7 %collective-permute-start.5 = (f32[5,1024]{1,0:T(8,128)S(1)}, f32[5,1024]{1,0:T(8,128)S(1)}, u32[]{:S(2)}, u32[]{:S(2)}) collective-permute-start(f32[5,1024]{1,0:T(8,128)S(1)} %get-tuple-element.43), channel_id=1, source_target_pairs={{1,2},{2,1},{3,4},{4,3},{5,6},{6,5},{7,8},{8,7},{9,10},{10,9},{11,... | collective-permute-start | bytes 61448 | tf_op jit(solution)/shard_map/ppermute | solution.py:661
  21.5 14.1 %collective-permute-start.6 = (f32[5,1024]{1,0:T(8,128)S(1)}, f32[5,1024]{1,0:T(8,128)S(1)}, u32[]{:S(2)}, u32[]{:S(2)}) collective-permute-start(f32[5,1024]{1,0:T(8,128)S(1)} %get-tuple-element.44), channel_id=1, source_target_pairs={{0,1},{1,0},{2,3},{3,2},{4,5},{5,4},{6,7},{7,6},{8,9},{9,8},{10,11... | collective-permute-start | bytes 61448 | tf_op jit(solution)/shard_map/ppermute | solution.py:661
  29.8 5.7 %collective-permute-start.7 = (f32[5,1024]{1,0:T(8,128)S(1)}, f32[5,1024]{1,0:T(8,128)S(1)}, u32[]{:S(2)}, u32[]{:S(2)}) collective-permute-start(f32[5,1024]{1,0:T(8,128)S(1)} %get-tuple-element.45), channel_id=1, source_target_pairs={{2,4},{4,2},{3,5},{5,3},{6,8},{8,6},{7,9},{9,7},{10,12},{12,10},{1... | collective-permute-start | bytes 61448 | tf_op jit(solution)/shard_map/ppermute | solution.py:661
  30.5 6.9 %collective-permute-start.8 = (f32[5,1024]{1,0:T(8,128)S(1)}, f32[5,1024]{1,0:T(8,128)S(1)}, u32[]{:S(2)}, u32[]{:S(2)}) collective-permute-start(f32[5,1024]{1,0:T(8,128)S(1)} %get-tuple-element.46), channel_id=1, source_target_pairs={{0,2},{2,0},{1,3},{3,1},{4,6},{6,4},{5,7},{7,5},{8,10},{10,8},{9,1... | collective-permute-start | bytes 61448 | tf_op jit(solution)/shard_map/ppermute | solution.py:661
  38.9 13.0 %collective-permute-start.10 = (f32[16,128]{1,0:T(8,128)S(1)}, f32[16,128]{1,0:T(8,128)S(1)}, u32[]{:S(2)}, u32[]{:S(2)}) collective-permute-start(f32[16,128]{1,0:T(8,128)S(1)} %get-tuple-element.49.own_ref), channel_id=1, source_target_pairs={{0,1},{1,0},{2,3},{3,2},{4,5},{5,4},{6,7},{7,6},{8,9},{9,8},{10,11... | collective-permute-start | bytes 24584 | tf_op jit(solution)/shard_map/ppermute | solution.py:661
  40.9 11.0 %collective-permute-start.11 = (f32[16,128]{1,0:T(8,128)S(1)}, f32[16,128]{1,0:T(8,128)S(1)}, u32[]{:S(2)}, u32[]{:S(2)}) collective-permute-start(f32[16,128]{1,0:T(8,128)S(1)} %get-tuple-element.49.own_ref), channel_id=1, source_target_pairs={{2,4},{4,2},{3,5},{5,3},{6,8},{8,6},{7,9},{9,7},{10,12},{12,10},{1... | collective-permute-start | bytes 24584 | tf_op jit(solution)/shard_map/ppermute | solution.py:661
  41.6 10.4 %collective-permute-start.12 = (f32[16,128]{1,0:T(8,128)S(1)}, f32[16,128]{1,0:T(8,128)S(1)}, u32[]{:S(2)}, u32[]{:S(2)}) collective-permute-start(f32[16,128]{1,0:T(8,128)S(1)} %get-tuple-element.49.own_ref), channel_id=1, source_target_pairs={{0,2},{2,0},{1,3},{3,1},{4,6},{6,4},{5,7},{7,5},{8,10},{10,8},{9,1... | collective-permute-start | bytes 24584 | tf_op jit(solution)/shard_map/ppermute | solution.py:661
  50.1 1.8 %collective-permute-start.9 = (f32[16,128]{1,0:T(8,128)S(1)}, f32[16,128]{1,0:T(8,128)S(1)}, u32[]{:S(2)}, u32[]{:S(2)}) collective-permute-start(f32[16,128]{1,0:T(8,128)S(1)} %get-tuple-element.49.own_ref), channel_id=1, source_target_pairs={{1,2},{2,1},{3,4},{4,3},{5,6},{6,5},{7,8},{8,7},{9,10},{10,9},{11,... | collective-permute-start | bytes 24584 | tf_op jit(solution)/shard_map/ppermute | solution.py:661
  55.1 6.4 %collective-permute-start.13 = (f32[64,128]{1,0:T(8,128)S(1)}, f32[64,128]{1,0:T(8,128)S(1)}, u32[]{:S(2)}, u32[]{:S(2)}) collective-permute-start(f32[64,128]{1,0:T(8,128)S(1)} %get-tuple-element.56), channel_id=1, source_target_pairs={{1,2},{2,1},{3,4},{4,3},{5,6},{6,5},{7,8},{8,7},{9,10},{10,9},{11,... | collective-permute-start | bytes 98312 | tf_op jit(solution)/shard_map/ppermute | solution.py:661
  55.8 7.6 %collective-permute-start.14 = (f32[64,128]{1,0:T(8,128)S(1)}, f32[64,128]{1,0:T(8,128)S(1)}, u32[]{:S(2)}, u32[]{:S(2)}) collective-permute-start(f32[64,128]{1,0:T(8,128)S(1)} %get-tuple-element.57), channel_id=1, source_target_pairs={{0,1},{1,0},{2,3},{3,2},{4,5},{5,4},{6,7},{7,6},{8,9},{9,8},{10,11... | collective-permute-start | bytes 98312 | tf_op jit(solution)/shard_map/ppermute | solution.py:661
  64.4 8.8 %collective-permute-start.15 = (f32[64,128]{1,0:T(8,128)S(1)}, f32[64,128]{1,0:T(8,128)S(1)}, u32[]{:S(2)}, u32[]{:S(2)}) collective-permute-start(f32[64,128]{1,0:T(8,128)S(1)} %get-tuple-element.61), channel_id=1, source_target_pairs={{1,2},{2,1},{3,4},{4,3},{5,6},{6,5},{7,8},{8,7},{9,10},{10,9},{11,... | collective-permute-start | bytes 98312 | tf_op jit(solution)/shard_map/ppermute | solution.py:661
  65.1 10.1 %collective-permute-start.16 = (f32[64,128]{1,0:T(8,128)S(1)}, f32[64,128]{1,0:T(8,128)S(1)}, u32[]{:S(2)}, u32[]{:S(2)}) collective-permute-start(f32[64,128]{1,0:T(8,128)S(1)} %get-tuple-element.62), channel_id=1, source_target_pairs={{0,1},{1,0},{2,3},{3,2},{4,5},{5,4},{6,7},{7,6},{8,9},{9,8},{10,11... | collective-permute-start | bytes 98312 | tf_op jit(solution)/shard_map/ppermute | solution.py:661
  76.2 37.0 %collective-permute-start.17 = (f32[64,128]{1,0:T(8,128)S(1)}, f32[64,128]{1,0:T(8,128)S(1)}, u32[]{:S(2)}, u32[]{:S(2)}) collective-permute-start(f32[64,128]{1,0:T(8,128)S(1)} %get-tuple-element.66), channel_id=1, source_target_pairs={{1,2},{2,1},{3,4},{4,3},{5,6},{6,5},{7,8},{8,7},{9,10},{10,9},{11,... | collective-permute-start | bytes 98312 | tf_op jit(solution)/shard_map/ppermute | solution.py:661
  76.9 36.3 %collective-permute-start.18 = (f32[64,128]{1,0:T(8,128)S(1)}, f32[64,128]{1,0:T(8,128)S(1)}, u32[]{:S(2)}, u32[]{:S(2)}) collective-permute-start(f32[64,128]{1,0:T(8,128)S(1)} %get-tuple-element.67), channel_id=1, source_target_pairs={{0,1},{1,0},{2,3},{3,2},{4,5},{5,4},{6,7},{7,6},{8,9},{9,8},{10,11... | collective-permute-start | bytes 98312 | tf_op jit(solution)/shard_map/ppermute | solution.py:661
  (2 other events, 27.8 us)

commit v3 on v2

--- a/solution.py
+++ b/solution.py
@@ -7,6 +7,7 @@
 from jax.experimental import pallas as pl
 from jax.experimental.pallas import tpu as pltpu
 from jax.sharding import PartitionSpec as P
+
 
 HIGHEST = lax.Precision.HIGHEST
 N_DOM = 64
@@ -588,11 +589,17 @@
     send_faces(q, u_ref, cross_ref, inner_ref)
 
 
+def image_kernel(place_ref, u_ref, cross_in_ref, inner_in_ref, free_ref, image_ref):
+    below, above = by_side(place_ref[0], cross_in_ref[...], inner_in_ref[...])
+    image_ref[...] = free_ref[...] * u_ref[...]
+    image_ref[0:64, :] = image_ref[0:64, :] + free_ref[0:64, :] * below
+    image_ref[448:512, :] = image_ref[448:512, :] + free_ref[448:512, :] * above
+
+
 def last_kernel(
-    place_ref, w0_ref, w1_ref, w2_ref, u_ref, cross_in_ref, inner_in_ref, inverse_ref, free_ref,
-    edge_ref, moments_ref, velocity_ref, residual_ref,
+    w0_ref, w1_ref, w2_ref, image_ref, inverse_ref, edge_ref, moments_ref, velocity_ref,
+    residual_ref,
 ):
-    below, above = by_side(place_ref[0], cross_in_ref[...], inner_in_ref[...])
     sums = jnp.sum(moments_ref[...], axis=0, keepdims=True)
     h0, a0, h2, a1, h4, a2 = [sums[:, m : m + 1] for m in range(6)]
     h1, h3 = a0 - h0, a1 - h2
@@ -612,15 +619,10 @@
     c0, c1, c2 = [jnp.broadcast_to(c, (64, LANES)) for c in (c0, c1, c2)]
     for k in range(8):
         rows = slice(64 * k, 64 * k + 64)
-        image = u_ref[rows, :]
-        if k == 0:
-            image = image + below
-        if k == 7:
-            image = image + above
         w0, w1, w2 = w0_ref[rows, :], w1_ref[rows, :], w2_ref[rows, :]
         velocity_ref[rows, :] = inverse_ref[rows, :] * (c0 * w0 + c1 * w1 + c2 * w2)
         residual_ref[rows, :] = (
-            w0 - c0 * (w1 + w0) - c1 * (w2 + w1) - c2 * (free_ref[rows, :] * image)
+            w0 - c0 * (w1 + w0) - c1 * (w2 + w1) - c2 * image_ref[rows, :]
         )
     for s in range(2):
         rows = pl.ds(7 * s, 64, stride=8)
@@ -631,7 +633,7 @@
 SMEM = pl.BlockSpec(memory_space=pltpu.SMEM)
 
 
-def call(kernel, operands, outs, scratch=(), flops=100_000, smem_first=True, name=None, mib=12):
+def call(kernel, operands, outs, scratch=(), flops=100_000, smem_first=True, mib=12):
     specs = [VMEM] * len(operands)
     if smem_first:
         specs[0] = SMEM
@@ -644,7 +646,6 @@
         scratch_shapes=[pltpu.VMEM(shape, dtype) for shape, dtype in scratch],
         cost_estimate=pl.CostEstimate(flops=flops, bytes_accessed=1_000_000, transcendentals=0),
         compiler_params=pltpu.CompilerParams(vmem_limit_bytes=mib * 1024 * 1024),
-        name=name,
     )(*operands)
 
 
@@ -658,7 +659,9 @@
 
 def to_neighbours(cross_1, inner_1, cross_2=None, inner_2=None):
     lists = ((cross_1, CROSS_1), (cross_2, CROSS_2), (inner_1, INNER_1), (inner_2, INNER_2))
-    moved = [None if value is None else lax.ppermute(value, "dom", pairs) for value, pairs in lists]
+    moved = []
+    for value, pairs in lists:
+        moved.append(None if value is None else lax.ppermute(value, "dom", pairs))
     return [moved[n] for n in (0, 2, 1, 3) if moved[n] is not None]
 
 
@@ -673,26 +676,25 @@
     *requests, own, moves = call(
         route_kernel, (place, interp_weights, owner, element, geometry, wall_flag, forcing),
         (with_head, with_head, asked, asked, asked, ((8, CAP), jnp.int32)),
-        scratch=(((5, 32, LANES), F32),), name="route", mib=60,
+        scratch=(((5, 32, LANES), F32),), mib=60,
     )
     requests = to_neighbours(*requests)
     (fields,) = call(
         split_kernel, (donors,), (((FIELDS, 512, 256), jnp.bfloat16),), smem_first=False,
-        name="split",
     )
     answers = call(
         eval_kernel, (*requests, own, fields), (((FIELDS, CAP), F32),) * 5,
-        flops=7_000_000_000, smem_first=False, name="evaluate", mib=24,
+        flops=7_000_000_000, smem_first=False, mib=24,
     )
     answered = to_neighbours(*answers[0:4])
     inverse, free, load, beside = call(
         prep_kernel, (place, geometry, wall_flag, forcing, requests[0], requests[1]),
         (FIELD, FIELD, FIELD, ((16, LANES), F32)),
-        scratch=(((64, LANES), F32), ((72, LANES), F32), ((72, LANES), F32)), name="prep",
+        scratch=(((64, LANES), F32), ((72, LANES), F32), ((72, LANES), F32)),
     )
     interface, share = call(
         unpack_kernel, (place, *answered, answers[4], moves, owner),
-        (((FIELDS, N_REC), F32), ((16, LANES), F32)), name="unpack",
+        (((FIELDS, N_REC), F32), ((16, LANES), F32)),
     )
     face = ((64, LANES), F32)
     w0, u, edge, moments, *faces = call(
@@ -700,7 +702,7 @@
         (place, share, *to_neighbours(share, share, share, share), geometry, beside, inverse, free,
          load, xmat),
         (FIELD, FIELD, ((128, LANES), F32), ((1, LANES), F32), face, face),
-        scratch=(FIELD, ((128, LANES), F32)), name="first",
+        scratch=(FIELD, ((128, LANES), F32)),
     )
     ws = [w0]
     for step in (1, 2):
@@ -708,14 +710,13 @@
             functools.partial(next_kernel, 2 * step),
             (place, ws[-1], u, *to_neighbours(*faces), geometry, inverse, free, xmat, moments),
             (FIELD, FIELD, ((1 if step == 1 else N_DOM, LANES), F32), face, face),
-            scratch=(FIELD,), name=f"next{step}",
+            scratch=(FIELD,),
         )
         ws.append(w)
-    faces = to_neighbours(*faces)
     sums = to_all(moments)
+    (image,) = call(image_kernel, (place, u, *to_neighbours(*faces), free), (FIELD,))
     velocity, residual = call(
-        last_kernel, (place, *ws, u, *faces, inverse, free, edge, sums),
-        (FIELD, FIELD), name="last",
+        last_kernel, (*ws, image, inverse, edge, sums), (FIELD, FIELD), smem_first=False,
     )
     return velocity, residual, interface
 
@@ -727,4 +728,5 @@
         P(None, both), P(None, both),
     )
     out_specs = (P(None, both), P(None, both), P(None, both))
+
     return jax.shard_map(body, mesh=mesh, in_specs=in_specs, out_specs=out_specs, check_vma=False)

time: 116 us -> 116 us (level)
  blocking collectives: 30.9 us -> 0 us
  starting transfers between devices: 59.6 us -> 80.5 us
  waiting for transfers between devices: 7.45 us -> 16.8 us
  Pallas kernels: 15.9 us -> 17.4 us
    all_to_all x1 -> x0, blocking collectives: 30.9 us -> none  [to_all(): return lax.all_to_all(value, 'dom', 0, 0, tiled=True)]
    all_to_all x0 -> x1, starting transfers between devices: none -> 23.5 us  [to_all(): return lax.all_to_all(value, 'dom', 0, 0, tiled=True)]
    all_to_all x0 -> x1, waiting for transfers between devices: none -> 9.44 us  [to_all(): return lax.all_to_all(value, 'dom', 0, 0, tiled=True)]
    ppermute x18, starting transfers between devices: 59.5 us -> 56.9 us  [to_neighbours(): moved.append(None if value is None else lax.ppermute(value, 'dom', pairs))]
    pallas_call x9 -> x10, Pallas kernels: 15.9 us -> 17.4 us  [call(): pl.pallas_call(kernel, out_shape=out_shape, in_specs=specs, out_specs=[VM...]
  transfers between devices with their start and end apart: 19 -> 20, of which waited for: 4 -> 5; matrix products, arithmetic and copies ran while one was open for 0% -> 0% of each run, Pallas kernels for 4% -> 4%
where the time goes in v3:
time: 116 us
  starting transfers between devices  80.5 us (69%)
  Pallas kernels  17.4 us (15%)
  waiting for transfers between devices  16.8 us (14%)
    ppermute x18, starting transfers between devices, to_neighbours(): moved.append(None if value is None else lax.ppermute(value, 'dom', pairs))  56.9 us
    all_to_all x1, starting transfers between devices, to_all(): return lax.all_to_all(value, 'dom', 0, 0, tiled=True)  23.5 us
    pallas_call x10, Pallas kernels, call(): pl.pallas_call(kernel, out_shape=out_shape, in_specs=specs, out_specs=[VM...  17.4 us
    all_to_all x1, waiting for transfers between devices, to_all(): return lax.all_to_all(value, 'dom', 0, 0, tiled=True)  9.44 us
    ppermute x18, waiting for transfers between devices, to_neighbours(): moved.append(None if value is None else lax.ppermute(value, 'dom', pairs))  7.34 us
  transfers between devices with their start and end apart: 20, of which 5 were waited for; matrix products, arithmetic and copies ran while one was open for 0% of the time, Pallas kernels for 4%

profile of v3, /device:TPU:0, one launch (start us, length us, event | category | flops | bytes accessed | tf_op | source)
XLA Modules:
  0.0 115.6 jit_solution(3645385018838956242)
XLA Ops:
  0.7 3.0 %shard_map.103 = (f32[104,128]{1,0:T(8,128)}, f32[104,128]{1,0:T(8,128)}, f32[32,128]{1,0:T(8,128)}, f32[32,128]{1,0:T(8,128)}, f32[32,128]{1,0:T(8,128)}, /*index=5*/s32[8,1024]{1,0:T(8,128)}) custom-call(s32[1]{0:T(128)} %bitcast.place_ref, f32[3,8,2048]{2,1,0:T(8,128)} %weights_ref.1, s32[1,2048]{1,0:T(1,128)} %bitcast.8, s32[1,2048]{1,0:T(1,128)} %bitcast.10, ...), custom_call_target="tpu_custom_call" | custom-call | flops 100000 | bytes 1000000 | tf_op jit(solution)/shard_map/pallas_call | solution.py:641
  4.4 4.6 %collective-permute-start.1 = (f32[104,128]{1,0:T(8,128)}, f32[104,128]{1,0:T(8,128)S(1)}, u32[]{:S(2)}, u32[]{:S(2)}) collective-permute-start(f32[104,128]{1,0:T(8,128)} %get-tuple-element.39), channel_id=1, source_target_pairs={{0,1},{1,0},{2,3},{3,2},{4,5},{5,4},{6,7},{7,6},{8,9},{9,8},{10,11... | collective-permute-start | bytes 159752 | tf_op jit(solution)/shard_map/ppermute | solution.py:664
  9.7 5.8 %collective-permute-start.3 = (f32[32,128]{1,0:T(8,128)}, f32[32,128]{1,0:T(8,128)S(1)}, u32[]{:S(2)}, u32[]{:S(2)}) collective-permute-start(f32[32,128]{1,0:T(8,128)} %get-tuple-element.41), channel_id=1, source_target_pairs={{0,2},{2,0},{1,3},{3,1},{4,6},{6,4},{5,7},{7,5},{8,10},{10,8},{9,1... | collective-permute-start | bytes 49160 | tf_op jit(solution)/shard_map/ppermute | solution.py:664
  15.7 1.6 %collective-permute-done.3.refs_3_ = f32[32,128]{1,0:T(8,128)S(1)} collective-permute-done((f32[32,128]{1,0:T(8,128)}, f32[32,128]{1,0:T(8,128)S(1)}, u32[]{:S(2)}, u32[]{:S(2)}) %collective-permute-start.3) | collective-permute-done | bytes 16416 | tf_op jit(solution)/shard_map/ppermute | solution.py:664
  17.5 4.2 %shard_map.105 = (f32[5,1024]{1,0:T(8,128)S(1)}, f32[5,1024]{1,0:T(8,128)S(1)}, f32[5,1024]{1,0:T(8,128)S(1)}, f32[5,1024]{1,0:T(8,128)S(1)}, f32[5,1024]{1,0:T(8,128)S(1)}) custom-call(f32[104,128]{1,0:T(8,128)S(1)} %collective-permute-done.refs_0_.cross_ref, f32[104,128]{1,0:T(8,128)S(1)} %collective-permute-done.1.refs_1_.inner_ref, ...), custom_call_target="tpu_custom_call" | custom-call | flops 7000000000 | bytes 1000000 | tf_op jit(solution)/shard_map/pallas_call | solution.py:641
  22.4 7.5 %collective-permute-start.6 = (f32[5,1024]{1,0:T(8,128)S(1)}, f32[5,1024]{1,0:T(8,128)S(1)}, u32[]{:S(2)}, u32[]{:S(2)}) collective-permute-start(f32[5,1024]{1,0:T(8,128)S(1)} %get-tuple-element.44), channel_id=1, source_target_pairs={{0,1},{1,0},{2,3},{3,2},{4,5},{5,4},{6,7},{7,6},{8,9},{9,8},{10,11... | collective-permute-start | bytes 61448 | tf_op jit(solution)/shard_map/ppermute | solution.py:664
  30.5 5.0 %collective-permute-start.8 = (f32[5,1024]{1,0:T(8,128)S(1)}, f32[5,1024]{1,0:T(8,128)S(1)}, u32[]{:S(2)}, u32[]{:S(2)}) collective-permute-start(f32[5,1024]{1,0:T(8,128)S(1)} %get-tuple-element.46), channel_id=1, source_target_pairs={{0,2},{2,0},{1,3},{3,1},{4,6},{6,4},{5,7},{7,5},{8,10},{10,8},{9,1... | collective-permute-start | bytes 61448 | tf_op jit(solution)/shard_map/ppermute | solution.py:664
  35.5 1.9 %collective-permute-done.8.inner_2_ref = f32[5,1024]{1,0:T(8,128)S(1)} collective-permute-done((f32[5,1024]{1,0:T(8,128)S(1)}, f32[5,1024]{1,0:T(8,128)S(1)}, u32[]{:S(2)}, u32[]{:S(2)}) %collective-permute-start.8) | collective-permute-done | bytes 20512 | tf_op jit(solution)/shard_map/ppermute | solution.py:664
  37.4 1.5 %shard_map.106 = (f32[5,2048]{1,0:T(8,128)}, f32[16,128]{1,0:T(8,128)S(1)}) custom-call(s32[1]{0:T(128)} %bitcast.place_ref, f32[5,1024]{1,0:T(8,128)S(1)} %collective-permute-done.5.cross_1_ref, f32[5,1024]{1,0:T(8,128)S(1)} %collective-permute-done.6.inner_1_ref, f32[5,1024]{1,0:T(8,128)S(1)} %collective-permute-done.7.cross_2_ref, ...), custom_call_target="tpu_custom_call" | custom-call | flops 100000 | bytes 1000000 | tf_op jit(solution)/shard_map/pallas_call | solution.py:641
  38.9 2.0 %collective-permute-start.10 = (f32[16,128]{1,0:T(8,128)S(1)}, f32[16,128]{1,0:T(8,128)S(1)}, u32[]{:S(2)}, u32[]{:S(2)}) collective-permute-start(f32[16,128]{1,0:T(8,128)S(1)} %get-tuple-element.49.own_ref), channel_id=1, source_target_pairs={{0,1},{1,0},{2,3},{3,2},{4,5},{5,4},{6,7},{7,6},{8,9},{9,8},{10,11... | collective-permute-start | bytes 24584 | tf_op jit(solution)/shard_map/ppermute | solution.py:664
  41.6 6.7 %collective-permute-start.12 = (f32[16,128]{1,0:T(8,128)S(1)}, f32[16,128]{1,0:T(8,128)S(1)}, u32[]{:S(2)}, u32[]{:S(2)}) collective-permute-start(f32[16,128]{1,0:T(8,128)S(1)} %get-tuple-element.49.own_ref), channel_id=1, source_target_pairs={{0,2},{2,0},{1,3},{3,1},{4,6},{6,4},{5,7},{7,5},{8,10},{10,8},{9,1... | collective-permute-start | bytes 24584 | tf_op jit(solution)/shard_map/ppermute | solution.py:664
  48.3 0.8 collective-permute-start.9
  49.1 0.9 shard_map.107
  50.1 3.1 %shard_map.108 = (f32[512,128]{1,0:T(8,128)S(1)}, f32[512,128]{1,0:T(8,128)S(1)}, f32[128,128]{1,0:T(8,128)S(1)}, f32[1,128]{1,0:T(1,128)S(1)}, f32[64,128]{1,0:T(8,128)S(1)}, /*index=5*/f32[64,128]{1,0:T(8,128)S(1)}) custom-call(s32[1]{0:T(128)} %bitcast.place_ref, f32[16,128]{1,0:T(8,128)S(1)} %get-tuple-element.49.own_ref, ...), custom_call_target="tpu_custom_call" | custom-call | flops 100000 | bytes 1000000 | tf_op jit(solution)/shard_map/pallas_call | solution.py:641
  53.9 5.8 %collective-permute-start.14 = (f32[64,128]{1,0:T(8,128)S(1)}, f32[64,128]{1,0:T(8,128)S(1)}, u32[]{:S(2)}, u32[]{:S(2)}) collective-permute-start(f32[64,128]{1,0:T(8,128)S(1)} %get-tuple-element.57), channel_id=1, source_target_pairs={{0,1},{1,0},{2,3},{3,2},{4,5},{5,4},{6,7},{7,6},{8,9},{9,8},{10,11... | collective-permute-start | bytes 98312 | tf_op jit(solution)/shard_map/ppermute | solution.py:664
  59.7 1.9 %collective-permute-done.14.inner_in_ref = f32[64,128]{1,0:T(8,128)S(1)} collective-permute-done((f32[64,128]{1,0:T(8,128)S(1)}, f32[64,128]{1,0:T(8,128)S(1)}, u32[]{:S(2)}, u32[]{:S(2)}) %collective-permute-start.14) | collective-permute-done | bytes 32800 | tf_op jit(solution)/shard_map/ppermute | solution.py:664
  61.6 1.0 shard_map.109
  63.3 8.1 %collective-permute-start.16 = (f32[64,128]{1,0:T(8,128)S(1)}, f32[64,128]{1,0:T(8,128)S(1)}, u32[]{:S(2)}, u32[]{:S(2)}) collective-permute-start(f32[64,128]{1,0:T(8,128)S(1)} %get-tuple-element.62), channel_id=1, source_target_pairs={{0,1},{1,0},{2,3},{3,2},{4,5},{5,4},{6,7},{7,6},{8,9},{9,8},{10,11... | collective-permute-start | bytes 98312 | tf_op jit(solution)/shard_map/ppermute | solution.py:664
  71.4 1.9 %collective-permute-done.16.inner_in_ref = f32[64,128]{1,0:T(8,128)S(1)} collective-permute-done((f32[64,128]{1,0:T(8,128)S(1)}, f32[64,128]{1,0:T(8,128)S(1)}, u32[]{:S(2)}, u32[]{:S(2)}) %collective-permute-start.16) | collective-permute-done | bytes 32800 | tf_op jit(solution)/shard_map/ppermute | solution.py:664
  73.3 1.6 %shard_map.110 = (f32[512,128]{1,0:T(8,128)S(1)}, f32[512,128]{1,0:T(8,128)S(1)}, f32[64,128]{1,0:T(8,128)}, f32[64,128]{1,0:T(8,128)S(1)}, f32[64,128]{1,0:T(8,128)S(1)}) custom-call(s32[1]{0:T(128)} %bitcast.place_ref, f32[512,128]{1,0:T(8,128)S(1)} %get-tuple-element.59.w_old_ref.w1_ref, f32[512,128]{1,0:T(8,128)S(1)} %get-tuple-element.60.u_old_ref, ...), custom_call_target="tpu_custom_call" | custom-call | flops 100000 | bytes 1000000 | tf_op jit(solution)/shard_map/pallas_call | solution.py:641
  75.6 5.4 %collective-permute-start.18 = (f32[64,128]{1,0:T(8,128)S(1)}, f32[64,128]{1,0:T(8,128)S(1)}, u32[]{:S(2)}, u32[]{:S(2)}) collective-permute-start(f32[64,128]{1,0:T(8,128)S(1)} %get-tuple-element.67), channel_id=1, source_target_pairs={{0,1},{1,0},{2,3},{3,2},{4,5},{5,4},{6,7},{7,6},{8,9},{9,8},{10,11... | collective-permute-start | bytes 98312 | tf_op jit(solution)/shard_map/ppermute | solution.py:664
  81.0 23.5 %all-to-all-start = ((f32[64,1,128]{2,1,0:T(1,128)}), f32[64,1,128]{2,1,0:T(1,128)S(1)}, u32[]{:S(2)}, u32[]{:S(2)}) async-start(f32[64,1,128]{2,1,0:T(1,128)} %bitcast.4), calls=%async_computation | async-start | bytes 65536 | tf_op jit(solution)/shard_map/all_to_all | solution.py:657
  104.6 9.4 %all-to-all-done = f32[64,1,128]{2,1,0:T(1,128)S(1)} async-done(((f32[64,1,128]{2,1,0:T(1,128)}), f32[64,1,128]{2,1,0:T(1,128)S(1)}, u32[]{:S(2)}, u32[]{:S(2)}) %all-to-all-start) | async-done | bytes 32800 | tf_op jit(solution)/shard_map/all_to_all | solution.py:657
  114.0 1.6 %shard_map.112 = (f32[512,128]{1,0:T(8,128)}, f32[512,128]{1,0:T(8,128)}) custom-call(f32[512,128]{1,0:T(8,128)S(1)} %get-tuple-element.54.w_old_ref.w0_ref, f32[512,128]{1,0:T(8,128)S(1)} %get-tuple-element.59.w_old_ref.w1_ref, f32[512,128]{1,0:T(8,128)S(1)} %get-tuple-element.64.w2_ref, f32[512,128]{1,0:T(8,128)S(1)} %shard_map.111.image_ref, ...), custom_call_target="tpu_custom_call" | custom-call | flops 100000 | bytes 1000000 | tf_op jit(solution)/shard_map/pallas_call | solution.py:641
  (40 shorter events, 5.7 us)
Async XLA Ops:
  0.6 14.8 %collective-permute-start.4 = (f32[5,512,128]{2,1,0:T(8,128)}, f32[5,512,128]{2,1,0:T(8,128)S(1)}, u32[]{:S(2)}, u32[]{:S(2)}) collective-permute-start(f32[5,512,128]{2,1,0:T(8,128)} %param.8), channel_id=1, source_target_pairs={{0,64},{64,0},{1,65},{65,1},{2,66},{66,2},{3,67},{67,3},{4,68},{68... | collective-permute-start | bytes 3932168 | tf_op jit(solution)/shard_map/ppermute | solution.py:671
  3.7 13.6 %collective-permute-start = (f32[104,128]{1,0:T(8,128)}, f32[104,128]{1,0:T(8,128)S(1)}, u32[]{:S(2)}, u32[]{:S(2)}) collective-permute-start(f32[104,128]{1,0:T(8,128)} %get-tuple-element.38), channel_id=1, source_target_pairs={{1,2},{2,1},{3,4},{4,3},{5,6},{6,5},{7,8},{8,7},{9,10},{10,9},{11,... | collective-permute-start | bytes 159752 | tf_op jit(solution)/shard_map/ppermute | solution.py:664
  4.4 13.0 %collective-permute-start.1 = (f32[104,128]{1,0:T(8,128)}, f32[104,128]{1,0:T(8,128)S(1)}, u32[]{:S(2)}, u32[]{:S(2)}) collective-permute-start(f32[104,128]{1,0:T(8,128)} %get-tuple-element.39), channel_id=1, source_target_pairs={{0,1},{1,0},{2,3},{3,2},{4,5},{5,4},{6,7},{7,6},{8,9},{9,8},{10,11... | collective-permute-start | bytes 159752 | tf_op jit(solution)/shard_map/ppermute | solution.py:664
  9.0 6.7 %collective-permute-start.2 = (f32[32,128]{1,0:T(8,128)}, f32[32,128]{1,0:T(8,128)S(1)}, u32[]{:S(2)}, u32[]{:S(2)}) collective-permute-start(f32[32,128]{1,0:T(8,128)} %get-tuple-element.40), channel_id=1, source_target_pairs={{2,4},{4,2},{3,5},{5,3},{6,8},{8,6},{7,9},{9,7},{10,12},{12,10},{1... | collective-permute-start | bytes 49160 | tf_op jit(solution)/shard_map/ppermute | solution.py:664
  9.7 7.7 %collective-permute-start.3 = (f32[32,128]{1,0:T(8,128)}, f32[32,128]{1,0:T(8,128)S(1)}, u32[]{:S(2)}, u32[]{:S(2)}) collective-permute-start(f32[32,128]{1,0:T(8,128)} %get-tuple-element.41), channel_id=1, source_target_pairs={{0,2},{2,0},{1,3},{3,1},{4,6},{6,4},{5,7},{7,5},{8,10},{10,8},{9,1... | collective-permute-start | bytes 49160 | tf_op jit(solution)/shard_map/ppermute | solution.py:664
  17.4 31.7 %copy-start.1 = (f32[512,128]{1,0:T(8,128)S(1)}, f32[512,128]{1,0:T(8,128)}, u32[]{:S(2)}) copy-start(f32[512,128]{1,0:T(8,128)} %forcing_ref.3) | copy-start | bytes 786436
  17.4 31.7 %copy-start.2 = (f32[4,128]{1,0:T(4,128)S(1)}, f32[4,128]{1,0:T(4,128)}, u32[]{:S(2)}) copy-start(f32[4,128]{1,0:T(4,128)} %geometry_ref.9) | copy-start | bytes 6148
  17.4 31.7 %copy-start.5 = (s32[2,8]{1,0:T(2,128)S(1)}, s32[2,8]{1,0:T(2,128)}, u32[]{:S(2)}) copy-start(s32[2,8]{1,0:T(2,128)} %wall_ref.3) | copy-start | bytes 196
  17.4 32.7 %copy-start = (f32[512,256]{1,0:T(8,128)S(1)}, f32[512,256]{1,0:T(8,128)}, u32[]{:S(2)}) copy-start(f32[512,256]{1,0:T(8,128)} %constant.6.clone.xmat_ref) | copy-start | bytes 1572868
  21.7 13.8 %collective-permute-start.5 = (f32[5,1024]{1,0:T(8,128)S(1)}, f32[5,1024]{1,0:T(8,128)S(1)}, u32[]{:S(2)}, u32[]{:S(2)}) collective-permute-start(f32[5,1024]{1,0:T(8,128)S(1)} %get-tuple-element.43), channel_id=1, source_target_pairs={{1,2},{2,1},{3,4},{4,3},{5,6},{6,5},{7,8},{8,7},{9,10},{10,9},{11,... | collective-permute-start | bytes 61448 | tf_op jit(solution)/shard_map/ppermute | solution.py:664
  22.4 13.2 %collective-permute-start.6 = (f32[5,1024]{1,0:T(8,128)S(1)}, f32[5,1024]{1,0:T(8,128)S(1)}, u32[]{:S(2)}, u32[]{:S(2)}) collective-permute-start(f32[5,1024]{1,0:T(8,128)S(1)} %get-tuple-element.44), channel_id=1, source_target_pairs={{0,1},{1,0},{2,3},{3,2},{4,5},{5,4},{6,7},{7,6},{8,9},{9,8},{10,11... | collective-permute-start | bytes 61448 | tf_op jit(solution)/shard_map/ppermute | solution.py:664
  29.8 5.7 %collective-permute-start.7 = (f32[5,1024]{1,0:T(8,128)S(1)}, f32[5,1024]{1,0:T(8,128)S(1)}, u32[]{:S(2)}, u32[]{:S(2)}) collective-permute-start(f32[5,1024]{1,0:T(8,128)S(1)} %get-tuple-element.45), channel_id=1, source_target_pairs={{2,4},{4,2},{3,5},{5,3},{6,8},{8,6},{7,9},{9,7},{10,12},{12,10},{1... | collective-permute-start | bytes 61448 | tf_op jit(solution)/shard_map/ppermute | solution.py:664
  30.5 6.9 %collective-permute-start.8 = (f32[5,1024]{1,0:T(8,128)S(1)}, f32[5,1024]{1,0:T(8,128)S(1)}, u32[]{:S(2)}, u32[]{:S(2)}) collective-permute-start(f32[5,1024]{1,0:T(8,128)S(1)} %get-tuple-element.46), channel_id=1, source_target_pairs={{0,2},{2,0},{1,3},{3,1},{4,6},{6,4},{5,7},{7,5},{8,10},{10,8},{9,1... | collective-permute-start | bytes 61448 | tf_op jit(solution)/shard_map/ppermute | solution.py:664
  38.9 11.1 %collective-permute-start.10 = (f32[16,128]{1,0:T(8,128)S(1)}, f32[16,128]{1,0:T(8,128)S(1)}, u32[]{:S(2)}, u32[]{:S(2)}) collective-permute-start(f32[16,128]{1,0:T(8,128)S(1)} %get-tuple-element.49.own_ref), channel_id=1, source_target_pairs={{0,1},{1,0},{2,3},{3,2},{4,5},{5,4},{6,7},{7,6},{8,9},{9,8},{10,11... | collective-permute-start | bytes 24584 | tf_op jit(solution)/shard_map/ppermute | solution.py:664
  40.9 9.1 %collective-permute-start.11 = (f32[16,128]{1,0:T(8,128)S(1)}, f32[16,128]{1,0:T(8,128)S(1)}, u32[]{:S(2)}, u32[]{:S(2)}) collective-permute-start(f32[16,128]{1,0:T(8,128)S(1)} %get-tuple-element.49.own_ref), channel_id=1, source_target_pairs={{2,4},{4,2},{3,5},{5,3},{6,8},{8,6},{7,9},{9,7},{10,12},{12,10},{1... | collective-permute-start | bytes 24584 | tf_op jit(solution)/shard_map/ppermute | solution.py:664
  41.6 8.5 %collective-permute-start.12 = (f32[16,128]{1,0:T(8,128)S(1)}, f32[16,128]{1,0:T(8,128)S(1)}, u32[]{:S(2)}, u32[]{:S(2)}) collective-permute-start(f32[16,128]{1,0:T(8,128)S(1)} %get-tuple-element.49.own_ref), channel_id=1, source_target_pairs={{0,2},{2,0},{1,3},{3,1},{4,6},{6,4},{5,7},{7,5},{8,10},{10,8},{9,1... | collective-permute-start | bytes 24584 | tf_op jit(solution)/shard_map/ppermute | solution.py:664
  48.3 1.8 %collective-permute-start.9 = (f32[16,128]{1,0:T(8,128)S(1)}, f32[16,128]{1,0:T(8,128)S(1)}, u32[]{:S(2)}, u32[]{:S(2)}) collective-permute-start(f32[16,128]{1,0:T(8,128)S(1)} %get-tuple-element.49.own_ref), channel_id=1, source_target_pairs={{1,2},{2,1},{3,4},{4,3},{5,6},{6,5},{7,8},{8,7},{9,10},{10,9},{11,... | collective-permute-start | bytes 24584 | tf_op jit(solution)/shard_map/ppermute | solution.py:664
  53.2 6.5 %collective-permute-start.13 = (f32[64,128]{1,0:T(8,128)S(1)}, f32[64,128]{1,0:T(8,128)S(1)}, u32[]{:S(2)}, u32[]{:S(2)}) collective-permute-start(f32[64,128]{1,0:T(8,128)S(1)} %get-tuple-element.56), channel_id=1, source_target_pairs={{1,2},{2,1},{3,4},{4,3},{5,6},{6,5},{7,8},{8,7},{9,10},{10,9},{11,... | collective-permute-start | bytes 98312 | tf_op jit(solution)/shard_map/ppermute | solution.py:664
  53.9 7.7 %collective-permute-start.14 = (f32[64,128]{1,0:T(8,128)S(1)}, f32[64,128]{1,0:T(8,128)S(1)}, u32[]{:S(2)}, u32[]{:S(2)}) collective-permute-start(f32[64,128]{1,0:T(8,128)S(1)} %get-tuple-element.57), channel_id=1, source_target_pairs={{0,1},{1,0},{2,3},{3,2},{4,5},{5,4},{6,7},{7,6},{8,9},{9,8},{10,11... | collective-permute-start | bytes 98312 | tf_op jit(solution)/shard_map/ppermute | solution.py:664
  62.7 8.8 %collective-permute-start.15 = (f32[64,128]{1,0:T(8,128)S(1)}, f32[64,128]{1,0:T(8,128)S(1)}, u32[]{:S(2)}, u32[]{:S(2)}) collective-permute-start(f32[64,128]{1,0:T(8,128)S(1)} %get-tuple-element.61), channel_id=1, source_target_pairs={{1,2},{2,1},{3,4},{4,3},{5,6},{6,5},{7,8},{8,7},{9,10},{10,9},{11,... | collective-permute-start | bytes 98312 | tf_op jit(solution)/shard_map/ppermute | solution.py:664
  63.3 10.0 %collective-permute-start.16 = (f32[64,128]{1,0:T(8,128)S(1)}, f32[64,128]{1,0:T(8,128)S(1)}, u32[]{:S(2)}, u32[]{:S(2)}) collective-permute-start(f32[64,128]{1,0:T(8,128)S(1)} %get-tuple-element.62), channel_id=1, source_target_pairs={{0,1},{1,0},{2,3},{3,2},{4,5},{5,4},{6,7},{7,6},{8,9},{9,8},{10,11... | collective-permute-start | bytes 98312 | tf_op jit(solution)/shard_map/ppermute | solution.py:664
  74.9 29.5 %collective-permute-start.17 = (f32[64,128]{1,0:T(8,128)S(1)}, f32[64,128]{1,0:T(8,128)S(1)}, u32[]{:S(2)}, u32[]{:S(2)}) collective-permute-start(f32[64,128]{1,0:T(8,128)S(1)} %get-tuple-element.66), channel_id=1, source_target_pairs={{1,2},{2,1},{3,4},{4,3},{5,6},{6,5},{7,8},{8,7},{9,10},{10,9},{11,... | collective-permute-start | bytes 98312 | tf_op jit(solution)/shard_map/ppermute | solution.py:664
  75.6 28.9 %collective-permute-start.18 = (f32[64,128]{1,0:T(8,128)S(1)}, f32[64,128]{1,0:T(8,128)S(1)}, u32[]{:S(2)}, u32[]{:S(2)}) collective-permute-start(f32[64,128]{1,0:T(8,128)S(1)} %get-tuple-element.67), channel_id=1, source_target_pairs={{0,1},{1,0},{2,3},{3,2},{4,5},{5,4},{6,7},{7,6},{8,9},{9,8},{10,11... | collective-permute-start | bytes 98312 | tf_op jit(solution)/shard_map/ppermute | solution.py:664
  81.0 33.0 %all-to-all-start = ((f32[64,1,128]{2,1,0:T(1,128)}), f32[64,1,128]{2,1,0:T(1,128)S(1)}, u32[]{:S(2)}, u32[]{:S(2)}) async-start(f32[64,1,128]{2,1,0:T(1,128)} %bitcast.4), calls=%async_computation | async-start | bytes 65536 | tf_op jit(solution)/shard_map/all_to_all | solution.py:657
  (3 other events, 47.8 us)

commit v4 on v3

--- a/solution.py
+++ b/solution.py
@@ -313,7 +313,7 @@
 
 def unpack_kernel(
     place_ref, cross_1_ref, inner_1_ref, cross_2_ref, inner_2_ref, own_ref, moves_ref, owner_ref,
-    out_ref, share_ref,
+    out_ref,
 ):
     q = place_ref[0]
     width = N_REC
@@ -339,8 +339,33 @@
     for s in range(1, 5):
         out = jnp.where(distance == s, values[s], out)
     out_ref[...] = out
+
+
+def share_kernel(
+    place_ref, cross_1_ref, inner_1_ref, cross_2_ref, inner_2_ref, own_ref, moves_ref, owner_ref,
+    share_ref,
+):
+    q = place_ref[0]
+    width = N_REC
+    below_1, above_1, below_2, above_2 = by_side(
+        q, *(ref[0:1, :] for ref in (cross_1_ref, inner_1_ref, cross_2_ref, inner_2_ref))
+    )
+    row = iota((8, CAP), 0)
+    values = jnp.broadcast_to(below_2, (8, CAP))
+    for s, value in ((1, below_1), (2, own_ref[0:1, :]), (3, above_1), (4, above_2)):
+        values = jnp.where(row == s, value, values)
+    values = jnp.concatenate([values, jnp.zeros((8, CAP), jnp.float32)], axis=1)
+    moves = jnp.concatenate([moves_ref[...], jnp.zeros((8, CAP), jnp.int32)], axis=1)
+    for b in range(10, -1, -1):
+        step = 1 << b
+        incoming = pltpu.roll(moves, step, 1)
+        moved = (incoming >> b) & 1
+        values = jnp.where(moved == 1, pltpu.roll(values, step, 1), values)
+        moves = jnp.where(moved == 1, incoming, jnp.where((moves >> b) & 1 == 1, 0, moves))
+    mine = iota((8, width), 0) == owner_ref[...] - q + 2
+    out = jnp.sum(jnp.where(mine, values, 0.0), axis=0, keepdims=True)
     for n in range(16):
-        share_ref[n : n + 1, :] = out[0:1, n * LANES : (n + 1) * LANES]
+        share_ref[n : n + 1, :] = out[:, n * LANES : (n + 1) * LANES]
 
 
 def prep_kernel(
@@ -467,13 +492,12 @@
 
 
 def first_kernel(
-    place_ref, own_ref, cross_1_ref, inner_1_ref, cross_2_ref, inner_2_ref, geometry_ref,
-    beside_ref, inverse_ref, free_ref, load_ref, xmat_ref, w_ref, u_ref, edge_ref, moments_ref, cross_ref, inner_ref, v_ref, face_ref,
+    place_ref, own_ref, cross_in_ref, inner_in_ref, geometry_ref,
+    beside_ref, inverse_ref, free_ref, load_ref, xmat_ref, w_ref, u_ref, edge_ref, lift_ref, moments_ref, cross_ref,
+    inner_ref, v_ref, face_ref,
 ):
     q = place_ref[0]
-    below_1, above_1, below_2, above_2 = by_side(
-        q, cross_1_ref[...], inner_1_ref[...], cross_2_ref[...], inner_2_ref[...]
-    )
+    below, above = by_side(q, cross_in_ref[...], inner_in_ref[...])
     pick_row = iota((8, LANES), 0)
     pick_lane = iota((8, LANES), 1)
     picks = [
@@ -498,8 +522,7 @@
             out.append([plane[8 * k : 8 * k + 8, :] for k in range(8)])
         return out
 
-    layers = (below_2, below_1, own_ref[...], above_1, above_2)
-    received = {off: planes(values) for off, values in zip(range(-2, 3), layers)}
+    received = {off: planes(values) for off, values in ((-1, below), (0, own_ref[...]), (1, above))}
     lane = iota((8, LANES), 1)
     j_row = iota((8, LANES), 0)
     low = (j_row == 0) & (lane >= 8)
@@ -523,10 +546,12 @@
                 total = received[off][s][k]
                 count = count_y * on_side[s]
                 if k == 0:
-                    total = total + received[off - 1][s][7]
+                    if off >= 0:
+                        total = total + received[off - 1][s][7]
                     count = count + count * has_below
                 if k == 7:
-                    total = total + received[off + 1][s][0]
+                    if off <= 0:
+                        total = total + received[off + 1][s][0]
                     count = count + count * has_above
                 side.append(sum_y(total) / jnp.maximum(count, 1.0))
             out.append(jnp.concatenate(side, axis=0))
@@ -549,6 +574,8 @@
     edge_ref[64:128, :] = sides[1]
     apply_local(v_ref, geometry_ref[...], xmat_ref, u_ref, tuple(range(8)))
     sum_xy(u_ref, 8)
+    lift_ref[0:64, :] = u_ref[0:64, :]
+    lift_ref[64:128, :] = u_ref[448:512, :]
     u_ref[0:64, :] = u_ref[0:64, :] + face_ref[0:64, :]
     u_ref[448:512, :] = u_ref[448:512, :] + face_ref[64:128, :]
     for k in range(8):
@@ -559,29 +586,43 @@
         jnp.zeros((1, LANES), jnp.float32),
     )
     send_faces(q, u_ref, cross_ref, inner_ref)
+    up = from_above(q)[0]
+    bottom, top = lift_ref[0:64, :], lift_ref[64:128, :]
+    cross_ref[64:128, :] = jnp.where(up, top, bottom)
+    inner_ref[64:128, :] = jnp.where(up, bottom, top)
 
 
 def send_faces(q, u_ref, cross_ref, inner_ref):
     up = from_above(q)[0]
     bottom, top = u_ref[0:64, :], u_ref[448:512, :]
-    cross_ref[...] = jnp.where(up, top, bottom)
-    inner_ref[...] = jnp.where(up, bottom, top)
+    cross_ref[0:64, :] = jnp.where(up, top, bottom)
+    inner_ref[0:64, :] = jnp.where(up, bottom, top)
 
 
 def next_kernel(
     at, place_ref, w_old_ref, u_old_ref, cross_in_ref, inner_in_ref, geometry_ref, inverse_ref,
-    free_ref, xmat_ref, moments_old_ref, w_ref, u_ref, moments_ref, cross_ref, inner_ref, v_ref,
+    free_ref, xmat_ref, moments_old_ref, *refs,
 ):
     q = place_ref[0]
+    if at == 2:
+        load_ref, lift_ref, *refs = refs
+    w_ref, u_ref, moments_ref, cross_ref, inner_ref, *refs = refs
+    v_ref = refs[-1]
     below, above = by_side(q, cross_in_ref[...], inner_in_ref[...])
     for k in range(8):
         rows = slice(64 * k, 64 * k + 64)
         image = u_old_ref[rows, :]
-        if k == 0:
-            image = image + below
-        if k == 7:
-            image = image + above
-        w_ref[rows, :] = free_ref[rows, :] * image - w_old_ref[rows, :]
+        w_old = w_old_ref[rows, :]
+        if k in (0, 7):
+            other = below if k == 0 else above
+            image = image + other[0:64, :]
+            face = slice(0, 64) if k == 0 else slice(64, 128)
+            if at == 2:
+                w_old = free_ref[rows, :] * (
+                    load_ref[rows, :] - (lift_ref[face, :] + other[64:128, :])
+                )
+                refs[0][face, :] = w_old
+        w_ref[rows, :] = free_ref[rows, :] * image - w_old
     row = krylov_step(
         q, w_ref, inverse_ref, geometry_ref, xmat_ref, v_ref, u_ref, at, moments_old_ref[...]
     )
@@ -597,8 +638,8 @@
 
 
 def last_kernel(
-    w0_ref, w1_ref, w2_ref, image_ref, inverse_ref, edge_ref, moments_ref, velocity_ref,
-    residual_ref,
+    w0_ref, face_ref, w1_ref, w2_ref, image_ref, inverse_ref, edge_ref, moments_ref,
+    velocity_ref, residual_ref,
 ):
     sums = jnp.sum(moments_ref[...], axis=0, keepdims=True)
     h0, a0, h2, a1, h4, a2 = [sums[:, m : m + 1] for m in range(6)]
@@ -620,6 +661,8 @@
     for k in range(8):
         rows = slice(64 * k, 64 * k + 64)
         w0, w1, w2 = w0_ref[rows, :], w1_ref[rows, :], w2_ref[rows, :]
+        if k in (0, 7):
+            w0 = face_ref[0:64, :] if k == 0 else face_ref[64:128, :]
         velocity_ref[rows, :] = inverse_ref[rows, :] * (c0 * w0 + c1 * w1 + c2 * w2)
         residual_ref[rows, :] = (
             w0 - c0 * (w1 + w0) - c1 * (w2 + w1) - c2 * image_ref[rows, :]
@@ -692,31 +735,33 @@
         (FIELD, FIELD, FIELD, ((16, LANES), F32)),
         scratch=(((64, LANES), F32), ((72, LANES), F32), ((72, LANES), F32)),
     )
-    interface, share = call(
-        unpack_kernel, (place, *answered, answers[4], moves, owner),
-        (((FIELDS, N_REC), F32), ((16, LANES), F32)),
-    )
+    unpacked = (place, *answered, answers[4], moves, owner)
+    (share,) = call(share_kernel, unpacked, (((16, LANES), F32),))
+    (interface,) = call(unpack_kernel, unpacked, (((FIELDS, N_REC), F32),))
     face = ((64, LANES), F32)
-    w0, u, edge, moments, *faces = call(
+    two_faces = ((128, LANES), F32)
+    w0, u, edge, lift, moments, *faces = call(
         first_kernel,
-        (place, share, *to_neighbours(share, share, share, share), geometry, beside, inverse, free,
+        (place, share, *to_neighbours(share, share), geometry, beside, inverse, free,
          load, xmat),
-        (FIELD, FIELD, ((128, LANES), F32), ((1, LANES), F32), face, face),
-        scratch=(FIELD, ((128, LANES), F32)),
-    )
-    ws = [w0]
-    for step in (1, 2):
-        w, u, moments, *faces = call(
-            functools.partial(next_kernel, 2 * step),
-            (place, ws[-1], u, *to_neighbours(*faces), geometry, inverse, free, xmat, moments),
-            (FIELD, FIELD, ((1 if step == 1 else N_DOM, LANES), F32), face, face),
-            scratch=(FIELD,),
-        )
-        ws.append(w)
+        (FIELD, FIELD, two_faces, two_faces, ((1, LANES), F32), two_faces, two_faces),
+        scratch=(FIELD, two_faces),
+    )
+    fixed = (geometry, inverse, free, xmat)
+    w1, u, moments, *faces, w0_faces = call(
+        functools.partial(next_kernel, 2),
+        (place, w0, u, *to_neighbours(*faces), *fixed, moments, load, lift),
+        (FIELD, FIELD, ((1, LANES), F32), face, face, two_faces), scratch=(FIELD,),
+    )
+    w2, u, moments, *faces = call(
+        functools.partial(next_kernel, 4),
+        (place, w1, u, *to_neighbours(*faces), *fixed, moments),
+        (FIELD, FIELD, ((N_DOM, LANES), F32), face, face), scratch=(FIELD,),
+    )
     sums = to_all(moments)
     (image,) = call(image_kernel, (place, u, *to_neighbours(*faces), free), (FIELD,))
     velocity, residual = call(
-        last_kernel, (*ws, image, inverse, edge, sums), (FIELD, FIELD), smem_first=False,
+        last_kernel, (w0, w0_faces, w1, w2, image, inverse, edge, sums), (FIELD, FIELD), smem_first=False,
     )
     return velocity, residual, interface
 

time: 116 us -> 109 us (0.940)
  starting transfers between devices: 80.5 us -> 74.3 us
    ppermute x18 -> x16, starting transfers between devices: 56.9 us -> 50.7 us  [to_neighbours(): moved.append(None if value is None else lax.ppermute(value, 'dom', pairs))]
    all_to_all x1, waiting for transfers between devices: 9.44 us -> 7.97 us  [to_all(): return lax.all_to_all(value, 'dom', 0, 0, tiled=True)]
    ppermute x18 -> x16, waiting for transfers between devices: 7.34 us -> 7.72 us  [to_neighbours(): moved.append(None if value is None else lax.ppermute(value, 'dom', pairs))]
    pallas_call x10 -> x11, Pallas kernels: 17.4 us -> 17.7 us  [call(): pl.pallas_call(kernel, out_shape=out_shape, in_specs=specs, out_specs=[VM...]
  transfers between devices with their start and end apart: 20 -> 18, of which waited for: 5 -> 5; matrix products, arithmetic and copies ran while one was open for 0% -> 0% of each run, Pallas kernels for 4% -> 5%
where the time goes in v4:
time: 109 us
  starting transfers between devices  74.3 us (68%)
  Pallas kernels  17.7 us (16%)
  waiting for transfers between devices  15.7 us (14%)
    ppermute x16, starting transfers between devices, to_neighbours(): moved.append(None if value is None else lax.ppermute(value, 'dom', pairs))  50.7 us
    all_to_all x1, starting transfers between devices, to_all(): return lax.all_to_all(value, 'dom', 0, 0, tiled=True)  23.5 us
    pallas_call x11, Pallas kernels, call(): pl.pallas_call(kernel, out_shape=out_shape, in_specs=specs, out_specs=[VM...  17.7 us
    all_to_all x1, waiting for transfers between devices, to_all(): return lax.all_to_all(value, 'dom', 0, 0, tiled=True)  7.97 us
    ppermute x16, waiting for transfers between devices, to_neighbours(): moved.append(None if value is None else lax.ppermute(value, 'dom', pairs))  7.72 us
  transfers between devices with their start and end apart: 18, of which 5 were waited for; matrix products, arithmetic and copies ran while one was open for 0% of the time, Pallas kernels for 5%

profile of v4, /device:TPU:0, one launch (start us, length us, event | category | flops | bytes accessed | tf_op | source)
XLA Modules:
  0.0 108.6 jit_solution(15861095863744371354)
XLA Ops:
  0.7 3.0 %shard_map.103 = (f32[104,128]{1,0:T(8,128)}, f32[104,128]{1,0:T(8,128)}, f32[32,128]{1,0:T(8,128)}, f32[32,128]{1,0:T(8,128)}, f32[32,128]{1,0:T(8,128)}, /*index=5*/s32[8,1024]{1,0:T(8,128)}) custom-call(s32[1]{0:T(128)} %bitcast.place_ref, f32[3,8,2048]{2,1,0:T(8,128)} %weights_ref.1, s32[1,2048]{1,0:T(1,128)} %bitcast.8, s32[1,2048]{1,0:T(1,128)} %bitcast.11, ...), custom_call_target="tpu_custom_call" | custom-call | flops 100000 | bytes 1000000 | tf_op jit(solution)/shard_map/pallas_call | solution.py:684
  4.4 4.6 %collective-permute-start.1 = (f32[104,128]{1,0:T(8,128)}, f32[104,128]{1,0:T(8,128)S(1)}, u32[]{:S(2)}, u32[]{:S(2)}) collective-permute-start(f32[104,128]{1,0:T(8,128)} %get-tuple-element.39), channel_id=1, source_target_pairs={{0,1},{1,0},{2,3},{3,2},{4,5},{5,4},{6,7},{7,6},{8,9},{9,8},{10,11... | collective-permute-start | bytes 159752 | tf_op jit(solution)/shard_map/ppermute | solution.py:707
  9.7 5.8 %collective-permute-start.3 = (f32[32,128]{1,0:T(8,128)}, f32[32,128]{1,0:T(8,128)S(1)}, u32[]{:S(2)}, u32[]{:S(2)}) collective-permute-start(f32[32,128]{1,0:T(8,128)} %get-tuple-element.41), channel_id=1, source_target_pairs={{0,2},{2,0},{1,3},{3,1},{4,6},{6,4},{5,7},{7,5},{8,10},{10,8},{9,1... | collective-permute-start | bytes 49160 | tf_op jit(solution)/shard_map/ppermute | solution.py:707
  15.7 1.6 %collective-permute-done.3.refs_3_ = f32[32,128]{1,0:T(8,128)S(1)} collective-permute-done((f32[32,128]{1,0:T(8,128)}, f32[32,128]{1,0:T(8,128)S(1)}, u32[]{:S(2)}, u32[]{:S(2)}) %collective-permute-start.3) | collective-permute-done | bytes 16416 | tf_op jit(solution)/shard_map/ppermute | solution.py:707
  17.5 4.2 %shard_map.105 = (f32[5,1024]{1,0:T(8,128)S(1)}, f32[5,1024]{1,0:T(8,128)S(1)}, f32[5,1024]{1,0:T(8,128)S(1)}, f32[5,1024]{1,0:T(8,128)S(1)}, f32[5,1024]{1,0:T(8,128)S(1)}) custom-call(f32[104,128]{1,0:T(8,128)S(1)} %collective-permute-done.refs_0_.cross_ref, f32[104,128]{1,0:T(8,128)S(1)} %collective-permute-done.1.refs_1_.inner_ref, ...), custom_call_target="tpu_custom_call" | custom-call | flops 7000000000 | bytes 1000000 | tf_op jit(solution)/shard_map/pallas_call | solution.py:684
  21.7 0.7 collective-permute-start.5
  22.4 7.5 %collective-permute-start.6 = (f32[5,1024]{1,0:T(8,128)S(1)}, f32[5,1024]{1,0:T(8,128)S(1)}, u32[]{:S(2)}, u32[]{:S(2)}) collective-permute-start(f32[5,1024]{1,0:T(8,128)S(1)} %get-tuple-element.44), channel_id=1, source_target_pairs={{0,1},{1,0},{2,3},{3,2},{4,5},{5,4},{6,7},{7,6},{8,9},{9,8},{10,11... | collective-permute-start | bytes 61448 | tf_op jit(solution)/shard_map/ppermute | solution.py:707
  30.5 5.0 %collective-permute-start.8 = (f32[5,1024]{1,0:T(8,128)S(1)}, f32[5,1024]{1,0:T(8,128)S(1)}, u32[]{:S(2)}, u32[]{:S(2)}) collective-permute-start(f32[5,1024]{1,0:T(8,128)S(1)} %get-tuple-element.46), channel_id=1, source_target_pairs={{0,2},{2,0},{1,3},{3,1},{4,6},{6,4},{5,7},{7,5},{8,10},{10,8},{9,1... | collective-permute-start | bytes 61448 | tf_op jit(solution)/shard_map/ppermute | solution.py:707
  35.5 1.9 %collective-permute-done.8.inner_2_ref = f32[5,1024]{1,0:T(8,128)S(1)} collective-permute-done((f32[5,1024]{1,0:T(8,128)S(1)}, f32[5,1024]{1,0:T(8,128)S(1)}, u32[]{:S(2)}, u32[]{:S(2)}) %collective-permute-start.8) | collective-permute-done | bytes 20512 | tf_op jit(solution)/shard_map/ppermute | solution.py:707
  38.1 2.1 %collective-permute-start.10 = (f32[16,128]{1,0:T(8,128)S(1)}, f32[16,128]{1,0:T(8,128)S(1)}, u32[]{:S(2)}, u32[]{:S(2)}) collective-permute-start(f32[16,128]{1,0:T(8,128)S(1)} %shard_map.106.own_ref), channel_id=1, source_target_pairs={{0,1},{1,0},{2,3},{3,2},{4,5},{5,4},{6,7},{7,6},{8,9},{9,8},{10,11... | collective-permute-start | bytes 24584 | tf_op jit(solution)/shard_map/ppermute | solution.py:707
  40.8 0.9 shard_map.107
  41.8 2.9 %shard_map.108 = (f32[512,128]{1,0:T(8,128)S(1)}, f32[512,128]{1,0:T(8,128)S(1)}, f32[128,128]{1,0:T(8,128)S(1)}, f32[128,128]{1,0:T(8,128)S(1)}, f32[1,128]{1,0...) custom-call(s32[1]{0:T(128)} %bitcast.place_ref, f32[16,128]{1,0:T(8,128)S(1)} %shard_map.106.own_ref, ...), custom_call_target="tpu_custom_call" | custom-call | flops 100000 | bytes 1000000 | tf_op jit(solution)/shard_map/pallas_call | solution.py:684
  44.6 0.7 collective-permute-start.11
  45.3 9.5 %collective-permute-start.12 = (f32[128,128]{1,0:T(8,128)S(1)}, f32[128,128]{1,0:T(8,128)S(1)}, u32[]{:S(2)}, u32[]{:S(2)}) collective-permute-start(f32[128,128]{1,0:T(8,128)S(1)} %get-tuple-element.56), channel_id=1, source_target_pairs={{0,1},{1,0},{2,3},{3,2},{4,5},{5,4},{6,7},{7,6},{8,9},{9,8},{10,11... | collective-permute-start | bytes 196616 | tf_op jit(solution)/shard_map/ppermute | solution.py:707
  54.8 2.2 %collective-permute-done.12.inner_in_ref = f32[128,128]{1,0:T(8,128)S(1)} collective-permute-done((f32[128,128]{1,0:T(8,128)S(1)}, f32[128,128]{1,0:T(8,128)S(1)}, u32[]{:S(2)}, u32[]{:S(2)}) %collective-permute-start.12) | collective-permute-done | bytes 65568 | tf_op jit(solution)/shard_map/ppermute | solution.py:707
  57.0 1.0 shard_map.109
  58.7 5.8 %collective-permute-start.14 = (f32[64,128]{1,0:T(8,128)S(1)}, f32[64,128]{1,0:T(8,128)S(1)}, u32[]{:S(2)}, u32[]{:S(2)}) collective-permute-start(f32[64,128]{1,0:T(8,128)S(1)} %get-tuple-element.63), channel_id=1, source_target_pairs={{0,1},{1,0},{2,3},{3,2},{4,5},{5,4},{6,7},{7,6},{8,9},{9,8},{10,11... | collective-permute-start | bytes 98312 | tf_op jit(solution)/shard_map/ppermute | solution.py:707
  64.6 1.9 %collective-permute-done.14.inner_in_ref = f32[64,128]{1,0:T(8,128)S(1)} collective-permute-done((f32[64,128]{1,0:T(8,128)S(1)}, f32[64,128]{1,0:T(8,128)S(1)}, u32[]{:S(2)}, u32[]{:S(2)}) %collective-permute-start.14) | collective-permute-done | bytes 32800 | tf_op jit(solution)/shard_map/ppermute | solution.py:707
  66.5 1.7 %shard_map.110 = (f32[512,128]{1,0:T(8,128)S(1)}, f32[512,128]{1,0:T(8,128)S(1)}, f32[64,128]{1,0:T(8,128)}, f32[64,128]{1,0:T(8,128)S(1)}, f32[64,128]{1,0:T(8,128)S(1)}) custom-call(s32[1]{0:T(128)} %bitcast.place_ref, f32[512,128]{1,0:T(8,128)S(1)} %get-tuple-element.60.w_old_ref.w1_ref, f32[512,128]{1,0:T(8,128)S(1)} %get-tuple-element.61.u_old_ref, ...), custom_call_target="tpu_custom_call" | custom-call | flops 100000 | bytes 1000000 | tf_op jit(solution)/shard_map/pallas_call | solution.py:684
  68.8 5.2 %collective-permute-start.16 = (f32[64,128]{1,0:T(8,128)S(1)}, f32[64,128]{1,0:T(8,128)S(1)}, u32[]{:S(2)}, u32[]{:S(2)}) collective-permute-start(f32[64,128]{1,0:T(8,128)S(1)} %get-tuple-element.68), channel_id=1, source_target_pairs={{0,1},{1,0},{2,3},{3,2},{4,5},{5,4},{6,7},{7,6},{8,9},{9,8},{10,11... | collective-permute-start | bytes 98312 | tf_op jit(solution)/shard_map/ppermute | solution.py:707
  73.9 23.5 %all-to-all-start = ((f32[64,1,128]{2,1,0:T(1,128)}), f32[64,1,128]{2,1,0:T(1,128)S(1)}, u32[]{:S(2)}, u32[]{:S(2)}) async-start(f32[64,1,128]{2,1,0:T(1,128)} %bitcast.4), calls=%async_computation | async-start | bytes 65536 | tf_op jit(solution)/shard_map/all_to_all | solution.py:700
  97.5 1.5 %shard_map.113 = f32[5,2048]{1,0:T(8,128)} custom-call(s32[1]{0:T(128)} %bitcast.place_ref, f32[5,1024]{1,0:T(8,128)S(1)} %collective-permute-done.5.cross_1_ref, f32[5,1024]{1,0:T(8,128)S(1)} %collective-permute-done.6.inner_1_ref, f32[5,1024]{1,0:T(8,128)S(1)} %collective-permute-done.7.cross_2_ref, f32[5,1024]{1,0:T(8,128)S(1)} %collective-permute-done.8.inner_2_ref, ...), custom_call_target="tpu_custom_call" | custom-call | flops 100000 | bytes 1000000 | tf_op jit(solution)/shard_map/pallas_call | solution.py:684
  99.0 8.0 %all-to-all-done = f32[64,1,128]{2,1,0:T(1,128)S(1)} async-done(((f32[64,1,128]{2,1,0:T(1,128)}), f32[64,1,128]{2,1,0:T(1,128)S(1)}, u32[]{:S(2)}, u32[]{:S(2)}) %all-to-all-start) | async-done | bytes 32800 | tf_op jit(solution)/shard_map/all_to_all | solution.py:700
  107.0 1.6 %shard_map.112 = (f32[512,128]{1,0:T(8,128)}, f32[512,128]{1,0:T(8,128)}) custom-call(f32[512,128]{1,0:T(8,128)S(1)} %get-tuple-element.53.w_old_ref.w0_ref, f32[128,128]{1,0:T(8,128)S(1)} %get-tuple-element.59.face_ref, f32[512,128]{1,0:T(8,128)S(1)} %get-tuple-element.60.w_old_ref.w1_ref, f32[512,128]{1,0:T(8,128)S(1)} %get-tuple-element.65.w2_ref, ...), custom_call_target="tpu_custom_call" | custom-call | flops 100000 | bytes 1000000 | tf_op jit(solution)/shard_map/pallas_call | solution.py:684
  (37 shorter events, 5.0 us)
Async XLA Ops:
  0.6 14.8 %collective-permute-start.4 = (f32[5,512,128]{2,1,0:T(8,128)}, f32[5,512,128]{2,1,0:T(8,128)S(1)}, u32[]{:S(2)}, u32[]{:S(2)}) collective-permute-start(f32[5,512,128]{2,1,0:T(8,128)} %param.8), channel_id=1, source_target_pairs={{0,64},{64,0},{1,65},{65,1},{2,66},{66,2},{3,67},{67,3},{4,68},{68... | collective-permute-start | bytes 3932168 | tf_op jit(solution)/shard_map/ppermute | solution.py:714
  3.7 13.6 %collective-permute-start = (f32[104,128]{1,0:T(8,128)}, f32[104,128]{1,0:T(8,128)S(1)}, u32[]{:S(2)}, u32[]{:S(2)}) collective-permute-start(f32[104,128]{1,0:T(8,128)} %get-tuple-element.38), channel_id=1, source_target_pairs={{1,2},{2,1},{3,4},{4,3},{5,6},{6,5},{7,8},{8,7},{9,10},{10,9},{11,... | collective-permute-start | bytes 159752 | tf_op jit(solution)/shard_map/ppermute | solution.py:707
  4.4 13.0 %collective-permute-start.1 = (f32[104,128]{1,0:T(8,128)}, f32[104,128]{1,0:T(8,128)S(1)}, u32[]{:S(2)}, u32[]{:S(2)}) collective-permute-start(f32[104,128]{1,0:T(8,128)} %get-tuple-element.39), channel_id=1, source_target_pairs={{0,1},{1,0},{2,3},{3,2},{4,5},{5,4},{6,7},{7,6},{8,9},{9,8},{10,11... | collective-permute-start | bytes 159752 | tf_op jit(solution)/shard_map/ppermute | solution.py:707
  9.0 6.7 %collective-permute-start.2 = (f32[32,128]{1,0:T(8,128)}, f32[32,128]{1,0:T(8,128)S(1)}, u32[]{:S(2)}, u32[]{:S(2)}) collective-permute-start(f32[32,128]{1,0:T(8,128)} %get-tuple-element.40), channel_id=1, source_target_pairs={{2,4},{4,2},{3,5},{5,3},{6,8},{8,6},{7,9},{9,7},{10,12},{12,10},{1... | collective-permute-start | bytes 49160 | tf_op jit(solution)/shard_map/ppermute | solution.py:707
  9.7 7.7 %collective-permute-start.3 = (f32[32,128]{1,0:T(8,128)}, f32[32,128]{1,0:T(8,128)S(1)}, u32[]{:S(2)}, u32[]{:S(2)}) collective-permute-start(f32[32,128]{1,0:T(8,128)} %get-tuple-element.41), channel_id=1, source_target_pairs={{0,2},{2,0},{1,3},{3,1},{4,6},{6,4},{5,7},{7,5},{8,10},{10,8},{9,1... | collective-permute-start | bytes 49160 | tf_op jit(solution)/shard_map/ppermute | solution.py:707
  17.4 20.1 %copy-start.2 = (s32[8,1024]{1,0:T(8,128)S(1)}, s32[8,1024]{1,0:T(8,128)}, u32[]{:S(2)}) copy-start(s32[8,1024]{1,0:T(8,128)} %get-tuple-element.48.moves_ref) | copy-start | bytes 98308
  17.4 20.0 %copy-start.3 = (s32[2048,1]{0,1:T(1,128)S(1)}, s32[2048,1]{0,1:T(1,128)}, u32[]{:S(2)}) copy-start(s32[2048,1]{0,1:T(1,128)} %param.10) | copy-start | bytes 24580
  17.4 23.4 %copy-start.1 = (f32[512,128]{1,0:T(8,128)S(1)}, f32[512,128]{1,0:T(8,128)}, u32[]{:S(2)}) copy-start(f32[512,128]{1,0:T(8,128)} %forcing_ref.3) | copy-start | bytes 786436
  17.4 23.4 %copy-start.4 = (f32[4,128]{1,0:T(4,128)S(1)}, f32[4,128]{1,0:T(4,128)}, u32[]{:S(2)}) copy-start(f32[4,128]{1,0:T(4,128)} %geometry_ref.9) | copy-start | bytes 6148
  17.4 23.4 %copy-start.5 = (s32[2,8]{1,0:T(2,128)S(1)}, s32[2,8]{1,0:T(2,128)}, u32[]{:S(2)}) copy-start(s32[2,8]{1,0:T(2,128)} %wall_ref.3) | copy-start | bytes 196
  17.4 24.4 %copy-start = (f32[512,256]{1,0:T(8,128)S(1)}, f32[512,256]{1,0:T(8,128)}, u32[]{:S(2)}) copy-start(f32[512,256]{1,0:T(8,128)} %constant.6.clone.xmat_ref) | copy-start | bytes 1572868
  21.7 13.8 %collective-permute-start.5 = (f32[5,1024]{1,0:T(8,128)S(1)}, f32[5,1024]{1,0:T(8,128)S(1)}, u32[]{:S(2)}, u32[]{:S(2)}) collective-permute-start(f32[5,1024]{1,0:T(8,128)S(1)} %get-tuple-element.43), channel_id=1, source_target_pairs={{1,2},{2,1},{3,4},{4,3},{5,6},{6,5},{7,8},{8,7},{9,10},{10,9},{11,... | collective-permute-start | bytes 61448 | tf_op jit(solution)/shard_map/ppermute | solution.py:707
  22.4 13.2 %collective-permute-start.6 = (f32[5,1024]{1,0:T(8,128)S(1)}, f32[5,1024]{1,0:T(8,128)S(1)}, u32[]{:S(2)}, u32[]{:S(2)}) collective-permute-start(f32[5,1024]{1,0:T(8,128)S(1)} %get-tuple-element.44), channel_id=1, source_target_pairs={{0,1},{1,0},{2,3},{3,2},{4,5},{5,4},{6,7},{7,6},{8,9},{9,8},{10,11... | collective-permute-start | bytes 61448 | tf_op jit(solution)/shard_map/ppermute | solution.py:707
  29.8 5.7 %collective-permute-start.7 = (f32[5,1024]{1,0:T(8,128)S(1)}, f32[5,1024]{1,0:T(8,128)S(1)}, u32[]{:S(2)}, u32[]{:S(2)}) collective-permute-start(f32[5,1024]{1,0:T(8,128)S(1)} %get-tuple-element.45), channel_id=1, source_target_pairs={{2,4},{4,2},{3,5},{5,3},{6,8},{8,6},{7,9},{9,7},{10,12},{12,10},{1... | collective-permute-start | bytes 61448 | tf_op jit(solution)/shard_map/ppermute | solution.py:707
  30.5 6.9 %collective-permute-start.8 = (f32[5,1024]{1,0:T(8,128)S(1)}, f32[5,1024]{1,0:T(8,128)S(1)}, u32[]{:S(2)}, u32[]{:S(2)}) collective-permute-start(f32[5,1024]{1,0:T(8,128)S(1)} %get-tuple-element.46), channel_id=1, source_target_pairs={{0,2},{2,0},{1,3},{3,1},{4,6},{6,4},{5,7},{7,5},{8,10},{10,8},{9,1... | collective-permute-start | bytes 61448 | tf_op jit(solution)/shard_map/ppermute | solution.py:707
  38.1 3.7 %collective-permute-start.10 = (f32[16,128]{1,0:T(8,128)S(1)}, f32[16,128]{1,0:T(8,128)S(1)}, u32[]{:S(2)}, u32[]{:S(2)}) collective-permute-start(f32[16,128]{1,0:T(8,128)S(1)} %shard_map.106.own_ref), channel_id=1, source_target_pairs={{0,1},{1,0},{2,3},{3,2},{4,5},{5,4},{6,7},{7,6},{8,9},{9,8},{10,11... | collective-permute-start | bytes 24584 | tf_op jit(solution)/shard_map/ppermute | solution.py:707
  40.1 1.7 %collective-permute-start.9 = (f32[16,128]{1,0:T(8,128)S(1)}, f32[16,128]{1,0:T(8,128)S(1)}, u32[]{:S(2)}, u32[]{:S(2)}) collective-permute-start(f32[16,128]{1,0:T(8,128)S(1)} %shard_map.106.own_ref), channel_id=1, source_target_pairs={{1,2},{2,1},{3,4},{4,3},{5,6},{6,5},{7,8},{8,7},{9,10},{10,9},{11,... | collective-permute-start | bytes 24584 | tf_op jit(solution)/shard_map/ppermute | solution.py:707
  44.6 10.1 %collective-permute-start.11 = (f32[128,128]{1,0:T(8,128)S(1)}, f32[128,128]{1,0:T(8,128)S(1)}, u32[]{:S(2)}, u32[]{:S(2)}) collective-permute-start(f32[128,128]{1,0:T(8,128)S(1)} %get-tuple-element.55), channel_id=1, source_target_pairs={{1,2},{2,1},{3,4},{4,3},{5,6},{6,5},{7,8},{8,7},{9,10},{10,9},{11,... | collective-permute-start | bytes 196616 | tf_op jit(solution)/shard_map/ppermute | solution.py:707
  45.3 11.7 %collective-permute-start.12 = (f32[128,128]{1,0:T(8,128)S(1)}, f32[128,128]{1,0:T(8,128)S(1)}, u32[]{:S(2)}, u32[]{:S(2)}) collective-permute-start(f32[128,128]{1,0:T(8,128)S(1)} %get-tuple-element.56), channel_id=1, source_target_pairs={{0,1},{1,0},{2,3},{3,2},{4,5},{5,4},{6,7},{7,6},{8,9},{9,8},{10,11... | collective-permute-start | bytes 196616 | tf_op jit(solution)/shard_map/ppermute | solution.py:707
  58.1 6.5 %collective-permute-start.13 = (f32[64,128]{1,0:T(8,128)S(1)}, f32[64,128]{1,0:T(8,128)S(1)}, u32[]{:S(2)}, u32[]{:S(2)}) collective-permute-start(f32[64,128]{1,0:T(8,128)S(1)} %get-tuple-element.62), channel_id=1, source_target_pairs={{1,2},{2,1},{3,4},{4,3},{5,6},{6,5},{7,8},{8,7},{9,10},{10,9},{11,... | collective-permute-start | bytes 98312 | tf_op jit(solution)/shard_map/ppermute | solution.py:707
  58.7 7.7 %collective-permute-start.14 = (f32[64,128]{1,0:T(8,128)S(1)}, f32[64,128]{1,0:T(8,128)S(1)}, u32[]{:S(2)}, u32[]{:S(2)}) collective-permute-start(f32[64,128]{1,0:T(8,128)S(1)} %get-tuple-element.63), channel_id=1, source_target_pairs={{0,1},{1,0},{2,3},{3,2},{4,5},{5,4},{6,7},{7,6},{8,9},{9,8},{10,11... | collective-permute-start | bytes 98312 | tf_op jit(solution)/shard_map/ppermute | solution.py:707
  68.1 30.8 %collective-permute-start.15 = (f32[64,128]{1,0:T(8,128)S(1)}, f32[64,128]{1,0:T(8,128)S(1)}, u32[]{:S(2)}, u32[]{:S(2)}) collective-permute-start(f32[64,128]{1,0:T(8,128)S(1)} %get-tuple-element.67), channel_id=1, source_target_pairs={{1,2},{2,1},{3,4},{4,3},{5,6},{6,5},{7,8},{8,7},{9,10},{10,9},{11,... | collective-permute-start | bytes 98312 | tf_op jit(solution)/shard_map/ppermute | solution.py:707
  68.8 30.2 %collective-permute-start.16 = (f32[64,128]{1,0:T(8,128)S(1)}, f32[64,128]{1,0:T(8,128)S(1)}, u32[]{:S(2)}, u32[]{:S(2)}) collective-permute-start(f32[64,128]{1,0:T(8,128)S(1)} %get-tuple-element.68), channel_id=1, source_target_pairs={{0,1},{1,0},{2,3},{3,2},{4,5},{5,4},{6,7},{7,6},{8,9},{9,8},{10,11... | collective-permute-start | bytes 98312 | tf_op jit(solution)/shard_map/ppermute | solution.py:707
  73.9 33.0 %all-to-all-start = ((f32[64,1,128]{2,1,0:T(1,128)}), f32[64,1,128]{2,1,0:T(1,128)S(1)}, u32[]{:S(2)}, u32[]{:S(2)}) async-start(f32[64,1,128]{2,1,0:T(1,128)} %bitcast.4), calls=%async_computation | async-start | bytes 65536 | tf_op jit(solution)/shard_map/all_to_all | solution.py:700
  (1 other events, 7.7 us)

commit v5 on v4

--- a/solution.py
+++ b/solution.py
@@ -14,6 +14,7 @@
 N_REC = 2048
 CAP = 1024
 FIELDS = 5
+BY_DOT = 3
 LANES = 128
 BLOCK = 512
 CHUNK = 104
@@ -71,13 +72,10 @@
 
 
 def x_matrix():
-    out = np.zeros((512, 256))
-    for k in range(8):
-        for j in range(8):
-            row = (k * 8 + j) * 8
-            col = row % 256
-            out[row : row + 8, col : col + 8] = WEIGHTS[k] * WEIGHTS[j] * STIFF
-    return out.astype(np.float32)
+    full = np.kron(np.diag(WEIGHTS), STIFF).astype(np.float32)
+    high = jnp.asarray(full).astype(jnp.bfloat16)
+    low = (jnp.asarray(full) - high.astype(jnp.float32)).astype(jnp.bfloat16)
+    return jnp.concatenate([high, high, low], axis=1)
 
 
 def iota(shape, dim):
@@ -126,27 +124,18 @@
     gzw = geometry[2:3, :] * wcol
     gmw = geometry[3:4, :] * wcol
     total = jnp.zeros((8, LANES), jnp.float32)
-    if len(planes) == 8:
-        along_x = [
-            lax.dot(
-                xmat_ref[256 * h : 256 * h + 256, :],
-                v_ref[256 * h : 256 * h + 256, :],
-                precision=HIGHEST,
-                preferred_element_type=jnp.float32,
-            )
-            for h in range(2)
-        ]
-        for h in range(2):
-            out_ref[256 * h : 256 * h + 256, :] = along_x[h]
-    else:
-        for at, k in enumerate(planes):
-            h = k // 4
-            out_ref[at * 64 : at * 64 + 64, :] = lax.dot(
-                xmat_ref[k * 64 : k * 64 + 64, :],
-                v_ref[256 * h : 256 * h + 256, :],
-                precision=HIGHEST,
-                preferred_element_type=jnp.float32,
-            )
+    for at in range(0, len(planes), 2):
+        pair = range(at, min(at + 2, len(planes)))
+        value = [v_ref[planes[n] * 64 : planes[n] * 64 + 64, :] for n in pair]
+        value = jnp.concatenate(value, axis=1) if len(value) > 1 else value[0]
+        high = value.astype(jnp.bfloat16)
+        low = (value - high.astype(jnp.float32)).astype(jnp.bfloat16)
+        along_x = lax.dot(
+            xmat_ref[...], jnp.concatenate([high, low, high], axis=0),
+            preferred_element_type=jnp.float32,
+        )
+        for n in pair:
+            out_ref[n * 64 : n * 64 + 64, :] = along_x[:, (n - at) * LANES : (n - at + 1) * LANES]
     for at, k in enumerate(planes):
         plane = [v_ref[(k * 8 + j) * 8 : (k * 8 + j) * 8 + 8, :] for j in range(8)]
         for j in range(8):
@@ -161,7 +150,7 @@
                 zsum = term if zsum is None else zsum + term
             row = (at * 8 + j) * 8
             value = (
-                out_ref[row : row + 8, :] * gx
+                out_ref[row : row + 8, :] * (gx * float(WEIGHTS[k]))
                 + gyw * ysum
                 + gzw * zsum
                 + gmw * (plane[j] * float(WEIGHTS[k] * WEIGHTS[j]))
@@ -247,7 +236,7 @@
 
 
 def split_kernel(fields_ref, out_ref):
-    for f in range(FIELDS):
+    for f in range(BY_DOT):
         value = fields_ref[f]
         high = value.astype(jnp.bfloat16)
         out_ref[f, :, 0:LANES] = high
@@ -275,8 +264,9 @@
 
 
 def eval_kernel(*refs):
-    sources, fields_ref, targets = refs[0:5], refs[5], refs[6:11]
-    for source, target in zip(sources, targets):
+    fields_ref, donors_ref, *refs = refs
+    half = len(refs) // 2
+    for source, target in zip(refs[:half], refs[half:]):
         words = source[0:32, :]
         valid = jnp.where((iota((32, LANES), 0) % 4 == 3) & (words > 0.0), 1, 0)
         blocks = (jnp.sum(valid) + BLOCK - 1) // BLOCK
@@ -286,17 +276,43 @@
             tiles = source[pl.ds(pl.multiple_of(b * 16, 16), 16), :]
             words = jnp.concatenate([tiles[4 * n : 4 * n + 4, :] for n in range(4)], axis=1)
             element = words[3:4, :].astype(jnp.int32) - 1
-            hot = (iota((LANES, BLOCK), 0) == element).astype(jnp.float32).astype(jnp.bfloat16)
+            hot_rows = iota((LANES, BLOCK), 0)
+            hot = (hot_rows == element).astype(jnp.float32).astype(jnp.bfloat16)
             hot = jnp.concatenate([hot, hot], axis=0)
+            element = jnp.maximum(element, 0)
             along = [basis_rows(words[d : d + 1, :]) for d in range(3)]
             row = iota((8, BLOCK), 0)
             wx = jnp.broadcast_to(along[0][0], (8, BLOCK))
             for i in range(1, 8):
                 wx = jnp.where(row == i, along[0][i], wx)
-            for f in range(FIELDS):
-                picked = lax.dot(
-                    fields_ref[f], hot, preferred_element_type=jnp.float32
+
+            def by_gather(f, h):
+                part = slice(h * LANES, h * LANES + LANES)
+                index = jnp.broadcast_to(element[:, part], (8, LANES))
+                wz = [jnp.broadcast_to(w[:, part], (8, LANES)) for w in along[2]]
+                over_j = None
+                for j in range(8):
+                    over_k = None
+                    for k in range(8):
+                        row = 64 * k + 8 * j
+                        term = wz[k] * jnp.take_along_axis(
+                            donors_ref[f, row : row + 8, :], index, axis=1,
+                            mode="promise_in_bounds",
+                        )
+                        over_k = term if over_k is None else over_k + term
+                    term = over_k * along[1][j][:, part]
+                    over_j = term if over_j is None else over_j + term
+                target[f : f + 1, pl.ds(start + h * LANES, LANES)] = jnp.sum(
+                    over_j * wx[:, part], axis=0, keepdims=True
                 )
+
+            gathers = [(f, h) for f in range(BY_DOT, FIELDS) for h in range(BLOCK // LANES)]
+            for f in range(BY_DOT):
+                picked = lax.dot(fields_ref[f], hot, preferred_element_type=jnp.float32)
+                share = -(-len(gathers) // (BY_DOT - f))
+                for work in gathers[:share]:
+                    by_gather(*work)
+                gathers = gathers[share:]
                 over_k = picked[0:64, :] * along[2][0]
                 for k in range(1, 8):
                     over_k = over_k + picked[64 * k : 64 * k + 64, :] * along[2][k]
@@ -508,21 +524,21 @@
         for s in range(2)
     ]
 
-    def planes(values):
-        out = []
-        for s in range(2):
-            halves = [
-                lax.dot_general(
-                    values[8 * s : 8 * s + 8, :], picks[s][odd], (((0,), (0,)), ((), ())),
-                    precision=HIGHEST, preferred_element_type=jnp.float32,
-                )
-                for odd in range(2)
-            ]
-            plane = halves[0][0:64, :] + halves[1][64:128, :]
-            out.append([plane[8 * k : 8 * k + 8, :] for k in range(8)])
-        return out
-
-    received = {off: planes(values) for off, values in ((-1, below), (0, own_ref[...]), (1, above))}
+    layers = (below, own_ref[...], above)
+    received = {off: [] for off in range(-1, 2)}
+    for s in range(2):
+        values = jnp.concatenate([layer[8 * s : 8 * s + 8, :] for layer in layers], axis=1)
+        halves = [
+            lax.dot_general(
+                values, picks[s][odd], (((0,), (0,)), ((), ())),
+                precision=HIGHEST, preferred_element_type=jnp.float32,
+            )
+            for odd in range(2)
+        ]
+        for n in range(3):
+            at = n * LANES
+            plane = halves[0][at : at + 64, :] + halves[1][at + 64 : at + 128, :]
+            received[n - 1].append([plane[8 * k : 8 * k + 8, :] for k in range(8)])
     lane = iota((8, LANES), 1)
     j_row = iota((8, LANES), 0)
     low = (j_row == 0) & (lane >= 8)
@@ -710,32 +726,44 @@
 
 def body(donor_fields, interp_weights, donor_owner, donor_element, geometry, wall_flag, forcing):
     place = lax.axis_index("dom").astype(jnp.int32).reshape(1)
-    xmat = jnp.asarray(x_matrix())
+    xmat = x_matrix()
     donors = lax.ppermute(donor_fields, "mesh", [(0, 1), (1, 0)])
     owner = donor_owner.reshape(1, N_REC)
     element = donor_element.reshape(1, N_REC)
     asked = ((32, LANES), F32)
     with_head = ((CHUNK, LANES), F32)
     *requests, own, moves = call(
-        route_kernel, (place, interp_weights, owner, element, geometry, wall_flag, forcing),
+        route_kernel,
+        (
+            place,
+            *(
+                pltpu.with_memory_space_constraint(value, pltpu.HBM)
+                for value in (interp_weights, owner, element, geometry, wall_flag, forcing)
+            ),
+        ),
         (with_head, with_head, asked, asked, asked, ((8, CAP), jnp.int32)),
-        scratch=(((5, 32, LANES), F32),), mib=60,
+        scratch=(((5, 32, LANES), F32),),
     )
     requests = to_neighbours(*requests)
     (fields,) = call(
-        split_kernel, (donors,), (((FIELDS, 512, 256), jnp.bfloat16),), smem_first=False,
-    )
-    answers = call(
-        eval_kernel, (*requests, own, fields), (((FIELDS, CAP), F32),) * 5,
-        flops=7_000_000_000, smem_first=False, mib=24,
-    )
-    answered = to_neighbours(*answers[0:4])
+        split_kernel, (donors,), (((BY_DOT, 512, 256), jnp.bfloat16),), smem_first=False,
+    )
+    answer = ((FIELDS, CAP), F32)
+    own_answer, inner_1 = call(
+        eval_kernel, (fields, donors, own, requests[1]), (answer,) * 2,
+        flops=3_000_000_000, smem_first=False, mib=24,
+    )
+    cross_1, cross_2, inner_2 = call(
+        eval_kernel, (fields, donors, requests[0], requests[2], requests[3]), (answer,) * 3,
+        flops=4_000_000_000, smem_first=False, mib=24,
+    )
+    answered = to_neighbours(cross_1, inner_1, cross_2, inner_2)
     inverse, free, load, beside = call(
         prep_kernel, (place, geometry, wall_flag, forcing, requests[0], requests[1]),
         (FIELD, FIELD, FIELD, ((16, LANES), F32)),
         scratch=(((64, LANES), F32), ((72, LANES), F32), ((72, LANES), F32)),
     )
-    unpacked = (place, *answered, answers[4], moves, owner)
+    unpacked = (place, *answered, own_answer, moves, owner)
     (share,) = call(share_kernel, unpacked, (((16, LANES), F32),))
     (interface,) = call(unpack_kernel, unpacked, (((FIELDS, N_REC), F32),))
     face = ((64, LANES), F32)

time: 109 us -> 103 us (0.945)
  starting transfers between devices: 74.3 us -> 69.7 us
  Pallas kernels: 17.7 us -> 14.9 us
  waiting for transfers between devices: 15.7 us -> 16.8 us
    pallas_call x11 -> x12, Pallas kernels: 17.7 us -> 14.9 us  [call(): pl.pallas_call(kernel, out_shape=out_shape, in_specs=specs, out_specs=[VM...]
    all_to_all x1, starting transfers between devices: 23.5 us -> 20.9 us  [to_all(): return lax.all_to_all(value, 'dom', 0, 0, tiled=True)]
    ppermute x16, starting transfers between devices: 50.7 us -> 48.8 us  [to_neighbours(): moved.append(None if value is None else lax.ppermute(value, 'dom', pairs))]
  transfers between devices with their start and end apart: 18 -> 18, of which waited for: 5 -> 6; matrix products, arithmetic and copies ran while one was open for 0% -> 0% of each run, Pallas kernels for 5% -> 8%
where the time goes in v5:
time: 103 us; the launch traced here: 102 us
  starting transfers between devices  69.7 us (68%)
  waiting for transfers between devices  16.8 us (16%)
  Pallas kernels  14.9 us (14%)
    ppermute x16, starting transfers between devices, to_neighbours(): moved.append(None if value is None else lax.ppermute(value, 'dom', pairs))  48.8 us
    all_to_all x1, starting transfers between devices, to_all(): return lax.all_to_all(value, 'dom', 0, 0, tiled=True)  20.9 us
    pallas_call x12, Pallas kernels, call(): pl.pallas_call(kernel, out_shape=out_shape, in_specs=specs, out_specs=[VM...  14.9 us
    ppermute x16, waiting for transfers between devices, to_neighbours(): moved.append(None if value is None else lax.ppermute(value, 'dom', pairs))  8.79 us
    all_to_all x1, waiting for transfers between devices, to_all(): return lax.all_to_all(value, 'dom', 0, 0, tiled=True)  7.97 us
  transfers between devices with their start and end apart: 18, of which 6 were waited for; matrix products, arithmetic and copies ran while one was open for 0% of the time, Pallas kernels for 8%

profile of v5, /device:TPU:0, one launch (start us, length us, event | category | flops | bytes accessed | tf_op | source)
XLA Modules:
  0.0 102.2 jit_solution(7629876667384980502)
XLA Ops:
  0.7 2.4 %shard_map.104 = (f32[104,128]{1,0:T(8,128)S(1)}, f32[104,128]{1,0:T(8,128)S(1)}, f32[32,128]{1,0:T(8,128)S(1)}, f32[32,128]{1,0:T(8,128)S(1)}, f32[32,128]{1,0:T(8,128)S(1)}, /*index=5*/s32[8,1024]{1,0:T(8,128)S(1)}) custom-call(s32[1]{0:T(128)} %bitcast.place_ref, f32[3,8,2048]{2,1,0:T(8,128)} %weights_ref.1, s32[1,2048]{1,0:T(1,128)} %bitcast.8, ...), custom_call_target="tpu_custom_call" | custom-call | flops 100000 | bytes 1000000 | tf_op jit(solution)/shard_map/pallas_call | solution.py:700
  3.1 0.7 collective-permute-start.1
  4.4 10.1 %collective-permute-start.3 = (f32[32,128]{1,0:T(8,128)S(1)}, f32[32,128]{1,0:T(8,128)S(1)}, u32[]{:S(2)}, u32[]{:S(2)}) collective-permute-start(f32[32,128]{1,0:T(8,128)S(1)} %get-tuple-element.40), channel_id=1, source_target_pairs={{0,2},{2,0},{1,3},{3,1},{4,6},{6,4},{5,7},{7,5},{8,10},{10,8},{9,1... | collective-permute-start | bytes 49160 | tf_op jit(solution)/shard_map/ppermute | solution.py:723
  14.9 1.5 %collective-permute-done.3.refs_4_ = f32[32,128]{1,0:T(8,128)S(1)} collective-permute-done((f32[32,128]{1,0:T(8,128)S(1)}, f32[32,128]{1,0:T(8,128)S(1)}, u32[]{:S(2)}, u32[]{:S(2)}) %collective-permute-start.3) | collective-permute-done | bytes 16416 | tf_op jit(solution)/shard_map/ppermute | solution.py:723
  16.5 1.1 %shard_map.105 = (f32[5,1024]{1,0:T(8,128)S(1)}, f32[5,1024]{1,0:T(8,128)S(1)}, f32[5,1024]{1,0:T(8,128)S(1)}) custom-call(bf16[3,512,256]{2,1,0:T(8,128)(2,1)S(1)} %shard_map.103.refs_0_, f32[5,512,128]{2,1,0:T(8,128)S(1)} %collective-permute-done.fields_ref.refs_1_, f32[104,128]{1,0:T(8,128)S(1)} %collective-permute-done.1.refs_2_.cross_ref, ...), custom_call_target="tpu_custom_call" | custom-call | flops 4000000000 | bytes 1000000 | tf_op jit(solution)/shard_map/pallas_call | solution.py:700
  17.6 0.7 collective-permute-start.4
  19.0 11.1 %collective-permute-start.8 = (f32[5,1024]{1,0:T(8,128)S(1)}, f32[5,1024]{1,0:T(8,128)S(1)}, u32[]{:S(2)}, u32[]{:S(2)}) collective-permute-start(f32[5,1024]{1,0:T(8,128)S(1)} %get-tuple-element.46), channel_id=1, source_target_pairs={{0,2},{2,0},{1,3},{3,1},{4,6},{6,4},{5,7},{7,5},{8,10},{10,8},{9,1... | collective-permute-start | bytes 61448 | tf_op jit(solution)/shard_map/ppermute | solution.py:723
  30.1 2.5 %shard_map.106 = (f32[5,1024]{1,0:T(8,128)S(1)}, f32[5,1024]{1,0:T(8,128)S(1)}) custom-call(bf16[3,512,256]{2,1,0:T(8,128)(2,1)S(1)} %shard_map.103.refs_0_, f32[5,512,128]{2,1,0:T(8,128)S(1)} %collective-permute-done.fields_ref.refs_1_, f32[32,128]{1,0:T(8,128)S(1)} %get-tuple-element.42.refs_2_, f32[104,128]{1,0:T(8,128)S(1)} %collective-permute-done.5.refs_3_.inner_ref), custom_call_target="tpu_custom_call" | custom-call | flops 3000000000 | bytes 1000000 | tf_op jit(solution)/shard_map/pallas_call | solution.py:700
  32.6 1.5 %collective-permute-start.6 = (f32[5,1024]{1,0:T(8,128)S(1)}, f32[5,1024]{1,0:T(8,128)S(1)}, u32[]{:S(2)}, u32[]{:S(2)}) collective-permute-start(f32[5,1024]{1,0:T(8,128)S(1)} %get-tuple-element.44), channel_id=1, source_target_pairs={{0,1},{1,0},{2,3},{3,2},{4,5},{5,4},{6,7},{7,6},{8,9},{9,8},{10,11... | collective-permute-start | bytes 61448 | tf_op jit(solution)/shard_map/ppermute | solution.py:723
  34.1 2.5 %collective-permute-done.6.inner_1_ref = f32[5,1024]{1,0:T(8,128)S(1)} collective-permute-done((f32[5,1024]{1,0:T(8,128)S(1)}, f32[5,1024]{1,0:T(8,128)S(1)}, u32[]{:S(2)}, u32[]{:S(2)}) %collective-permute-start.6) | collective-permute-done | bytes 20512 | tf_op jit(solution)/shard_map/ppermute | solution.py:723
  37.2 1.5 %collective-permute-start.10 = (f32[16,128]{1,0:T(8,128)S(1)}, f32[16,128]{1,0:T(8,128)S(1)}, u32[]{:S(2)}, u32[]{:S(2)}) collective-permute-start(f32[16,128]{1,0:T(8,128)S(1)} %shard_map.107.own_ref), channel_id=1, source_target_pairs={{0,1},{1,0},{2,3},{3,2},{4,5},{5,4},{6,7},{7,6},{8,9},{9,8},{10,11... | collective-permute-start | bytes 24584 | tf_op jit(solution)/shard_map/ppermute | solution.py:723
  39.4 0.9 shard_map.108
  40.9 2.2 %shard_map.109 = (f32[512,128]{1,0:T(8,128)S(1)}, f32[512,128]{1,0:T(8,128)S(1)}, f32[128,128]{1,0:T(8,128)S(1)}, f32[128,128]{1,0:T(8,128)S(1)}, f32[1,128]{1,0...) custom-call(s32[1]{0:T(128)} %bitcast.place_ref, f32[16,128]{1,0:T(8,128)S(1)} %shard_map.107.own_ref, ...), custom_call_target="tpu_custom_call" | custom-call | flops 100000 | bytes 1000000 | tf_op jit(solution)/shard_map/pallas_call | solution.py:700
  43.8 5.2 %collective-permute-start.12 = (f32[128,128]{1,0:T(8,128)S(1)}, f32[128,128]{1,0:T(8,128)S(1)}, u32[]{:S(2)}, u32[]{:S(2)}) collective-permute-start(f32[128,128]{1,0:T(8,128)S(1)} %get-tuple-element.56), channel_id=1, source_target_pairs={{0,1},{1,0},{2,3},{3,2},{4,5},{5,4},{6,7},{7,6},{8,9},{9,8},{10,11... | collective-permute-start | bytes 196616 | tf_op jit(solution)/shard_map/ppermute | solution.py:723
  49.1 2.2 %collective-permute-done.12.inner_in_ref = f32[128,128]{1,0:T(8,128)S(1)} collective-permute-done((f32[128,128]{1,0:T(8,128)S(1)}, f32[128,128]{1,0:T(8,128)S(1)}, u32[]{:S(2)}, u32[]{:S(2)}) %collective-permute-start.12) | collective-permute-done | bytes 65568 | tf_op jit(solution)/shard_map/ppermute | solution.py:723
  51.9 0.7 collective-permute-start.13
  52.6 8.5 %collective-permute-start.14 = (f32[64,128]{1,0:T(8,128)S(1)}, f32[64,128]{1,0:T(8,128)S(1)}, u32[]{:S(2)}, u32[]{:S(2)}) collective-permute-start(f32[64,128]{1,0:T(8,128)S(1)} %get-tuple-element.63), channel_id=1, source_target_pairs={{0,1},{1,0},{2,3},{3,2},{4,5},{5,4},{6,7},{7,6},{8,9},{9,8},{10,11... | collective-permute-start | bytes 98312 | tf_op jit(solution)/shard_map/ppermute | solution.py:723
  61.1 1.9 %collective-permute-done.14.inner_in_ref = f32[64,128]{1,0:T(8,128)S(1)} collective-permute-done((f32[64,128]{1,0:T(8,128)S(1)}, f32[64,128]{1,0:T(8,128)S(1)}, u32[]{:S(2)}, u32[]{:S(2)}) %collective-permute-start.14) | collective-permute-done | bytes 32800 | tf_op jit(solution)/shard_map/ppermute | solution.py:723
  63.0 1.2 %shard_map.111 = (f32[512,128]{1,0:T(8,128)S(1)}, f32[512,128]{1,0:T(8,128)S(1)}, f32[64,128]{1,0:T(8,128)}, f32[64,128]{1,0:T(8,128)S(1)}, f32[64,128]{1,0:T(8,128)S(1)}) custom-call(s32[1]{0:T(128)} %bitcast.place_ref, f32[512,128]{1,0:T(8,128)S(1)} %get-tuple-element.60.w_old_ref.w1_ref, f32[512,128]{1,0:T(8,128)S(1)} %get-tuple-element.61.u_old_ref, ...), custom_call_target="tpu_custom_call" | custom-call | flops 100000 | bytes 1000000 | tf_op jit(solution)/shard_map/pallas_call | solution.py:700
  64.9 5.4 %collective-permute-start.16 = (f32[64,128]{1,0:T(8,128)S(1)}, f32[64,128]{1,0:T(8,128)S(1)}, u32[]{:S(2)}, u32[]{:S(2)}) collective-permute-start(f32[64,128]{1,0:T(8,128)S(1)} %get-tuple-element.68), channel_id=1, source_target_pairs={{0,1},{1,0},{2,3},{3,2},{4,5},{5,4},{6,7},{7,6},{8,9},{9,8},{10,11... | collective-permute-start | bytes 98312 | tf_op jit(solution)/shard_map/ppermute | solution.py:723
  70.2 20.9 %all-to-all-start = ((f32[64,1,128]{2,1,0:T(1,128)}), f32[64,1,128]{2,1,0:T(1,128)S(1)}, u32[]{:S(2)}, u32[]{:S(2)}) async-start(f32[64,1,128]{2,1,0:T(1,128)} %bitcast.4), calls=%async_computation | async-start | bytes 65536 | tf_op jit(solution)/shard_map/all_to_all | solution.py:716
  91.1 1.5 %shard_map.114 = f32[5,2048]{1,0:T(8,128)} custom-call(s32[1]{0:T(128)} %bitcast.place_ref, f32[5,1024]{1,0:T(8,128)S(1)} %collective-permute-done.4.cross_1_ref, f32[5,1024]{1,0:T(8,128)S(1)} %collective-permute-done.6.inner_1_ref, f32[5,1024]{1,0:T(8,128)S(1)} %collective-permute-done.7.cross_2_ref, f32[5,1024]{1,0:T(8,128)S(1)} %collective-permute-done.8.inner_2_ref, ...), custom_call_target="tpu_custom_call" | custom-call | flops 100000 | bytes 1000000 | tf_op jit(solution)/shard_map/pallas_call | solution.py:700
  92.6 8.0 %all-to-all-done = f32[64,1,128]{2,1,0:T(1,128)S(1)} async-done(((f32[64,1,128]{2,1,0:T(1,128)}), f32[64,1,128]{2,1,0:T(1,128)S(1)}, u32[]{:S(2)}, u32[]{:S(2)}) %all-to-all-start) | async-done | bytes 32800 | tf_op jit(solution)/shard_map/all_to_all | solution.py:716
  100.6 1.6 %shard_map.113 = (f32[512,128]{1,0:T(8,128)}, f32[512,128]{1,0:T(8,128)}) custom-call(f32[512,128]{1,0:T(8,128)S(1)} %get-tuple-element.53.w_old_ref.w0_ref, f32[128,128]{1,0:T(8,128)S(1)} %get-tuple-element.59.face_ref, f32[512,128]{1,0:T(8,128)S(1)} %get-tuple-element.60.w_old_ref.w1_ref, f32[512,128]{1,0:T(8,128)S(1)} %get-tuple-element.65.w2_ref, ...), custom_call_target="tpu_custom_call" | custom-call | flops 100000 | bytes 1000000 | tf_op jit(solution)/shard_map/pallas_call | solution.py:700
  (34 shorter events, 5.6 us)
Async XLA Ops:
  0.6 14.1 %collective-permute-start = (f32[5,512,128]{2,1,0:T(8,128)}, f32[5,512,128]{2,1,0:T(8,128)S(1)}, u32[]{:S(2)}, u32[]{:S(2)}) collective-permute-start(f32[5,512,128]{2,1,0:T(8,128)} %param.8), channel_id=1, source_target_pairs={{0,64},{64,0},{1,65},{65,1},{2,66},{66,2},{3,67},{67,3},{4,68},{68... | collective-permute-start | bytes 3932168 | tf_op jit(solution)/shard_map/ppermute | solution.py:730
  3.1 13.4 %collective-permute-start.1 = (f32[104,128]{1,0:T(8,128)S(1)}, f32[104,128]{1,0:T(8,128)S(1)}, u32[]{:S(2)}, u32[]{:S(2)}) collective-permute-start(f32[104,128]{1,0:T(8,128)S(1)} %get-tuple-element.38), channel_id=1, source_target_pairs={{1,2},{2,1},{3,4},{4,3},{5,6},{6,5},{7,8},{8,7},{9,10},{10,9},{11,... | collective-permute-start | bytes 159752 | tf_op jit(solution)/shard_map/ppermute | solution.py:723
  3.8 11.1 %collective-permute-start.2 = (f32[32,128]{1,0:T(8,128)S(1)}, f32[32,128]{1,0:T(8,128)S(1)}, u32[]{:S(2)}, u32[]{:S(2)}) collective-permute-start(f32[32,128]{1,0:T(8,128)S(1)} %get-tuple-element.39), channel_id=1, source_target_pairs={{2,4},{4,2},{3,5},{5,3},{6,8},{8,6},{7,9},{9,7},{10,12},{12,10},{1... | collective-permute-start | bytes 49160 | tf_op jit(solution)/shard_map/ppermute | solution.py:723
  4.4 12.0 %collective-permute-start.3 = (f32[32,128]{1,0:T(8,128)S(1)}, f32[32,128]{1,0:T(8,128)S(1)}, u32[]{:S(2)}, u32[]{:S(2)}) collective-permute-start(f32[32,128]{1,0:T(8,128)S(1)} %get-tuple-element.40), channel_id=1, source_target_pairs={{0,2},{2,0},{1,3},{3,1},{4,6},{6,4},{5,7},{7,5},{8,10},{10,8},{9,1... | collective-permute-start | bytes 49160 | tf_op jit(solution)/shard_map/ppermute | solution.py:723
  14.6 15.5 %collective-permute-start.5 = (f32[104,128]{1,0:T(8,128)S(1)}, f32[104,128]{1,0:T(8,128)S(1)}, u32[]{:S(2)}, u32[]{:S(2)}) collective-permute-start(f32[104,128]{1,0:T(8,128)S(1)} %get-tuple-element.43), channel_id=1, source_target_pairs={{0,1},{1,0},{2,3},{3,2},{4,5},{5,4},{6,7},{7,6},{8,9},{9,8},{10,11... | collective-permute-start | bytes 159752 | tf_op jit(solution)/shard_map/ppermute | solution.py:723
  17.6 16.5 %collective-permute-start.4 = (f32[5,1024]{1,0:T(8,128)S(1)}, f32[5,1024]{1,0:T(8,128)S(1)}, u32[]{:S(2)}, u32[]{:S(2)}) collective-permute-start(f32[5,1024]{1,0:T(8,128)S(1)} %get-tuple-element.41), channel_id=1, source_target_pairs={{1,2},{2,1},{3,4},{4,3},{5,6},{6,5},{7,8},{8,7},{9,10},{10,9},{11,... | collective-permute-start | bytes 61448 | tf_op jit(solution)/shard_map/ppermute | solution.py:723
  18.3 15.8 %collective-permute-start.7 = (f32[5,1024]{1,0:T(8,128)S(1)}, f32[5,1024]{1,0:T(8,128)S(1)}, u32[]{:S(2)}, u32[]{:S(2)}) collective-permute-start(f32[5,1024]{1,0:T(8,128)S(1)} %get-tuple-element.45), channel_id=1, source_target_pairs={{2,4},{4,2},{3,5},{5,3},{6,8},{8,6},{7,9},{9,7},{10,12},{12,10},{1... | collective-permute-start | bytes 61448 | tf_op jit(solution)/shard_map/ppermute | solution.py:723
  19.0 15.2 %collective-permute-start.8 = (f32[5,1024]{1,0:T(8,128)S(1)}, f32[5,1024]{1,0:T(8,128)S(1)}, u32[]{:S(2)}, u32[]{:S(2)}) collective-permute-start(f32[5,1024]{1,0:T(8,128)S(1)} %get-tuple-element.46), channel_id=1, source_target_pairs={{0,2},{2,0},{1,3},{3,1},{4,6},{6,4},{5,7},{7,5},{8,10},{10,8},{9,1... | collective-permute-start | bytes 61448 | tf_op jit(solution)/shard_map/ppermute | solution.py:723
  30.1 6.5 %copy-start.2 = (s32[2048,1]{0,1:T(1,128)S(1)}, s32[2048,1]{0,1:T(1,128)}, u32[]{:S(2)}) copy-start(s32[2048,1]{0,1:T(1,128)} %param.10) | copy-start | bytes 24580
  30.1 9.3 %copy-start = (f32[512,128]{1,0:T(8,128)S(1)}, f32[512,128]{1,0:T(8,128)}, u32[]{:S(2)}) copy-start(f32[512,128]{1,0:T(8,128)} %forcing_ref.3) | copy-start | bytes 786436
  30.1 9.3 %copy-start.3 = (f32[4,128]{1,0:T(4,128)S(1)}, f32[4,128]{1,0:T(4,128)}, u32[]{:S(2)}) copy-start(f32[4,128]{1,0:T(4,128)} %geometry_ref.9) | copy-start | bytes 6148
  30.1 9.3 %copy-start.4 = (s32[2,8]{1,0:T(2,128)S(1)}, s32[2,8]{1,0:T(2,128)}, u32[]{:S(2)}) copy-start(s32[2,8]{1,0:T(2,128)} %wall_ref.3) | copy-start | bytes 196
  30.1 10.8 %copy-start.1 = (bf16[64,192]{1,0:T(8,128)(2,1)S(1)}, bf16[64,192]{1,0:T(8,128)(2,1)}, u32[]{:S(2)}) copy-start(bf16[64,192]{1,0:T(8,128)(2,1)} %constant.12.xmat_ref) | copy-start | bytes 73732
  32.6 4.0 %collective-permute-start.6 = (f32[5,1024]{1,0:T(8,128)S(1)}, f32[5,1024]{1,0:T(8,128)S(1)}, u32[]{:S(2)}, u32[]{:S(2)}) collective-permute-start(f32[5,1024]{1,0:T(8,128)S(1)} %get-tuple-element.44), channel_id=1, source_target_pairs={{0,1},{1,0},{2,3},{3,2},{4,5},{5,4},{6,7},{7,6},{8,9},{9,8},{10,11... | collective-permute-start | bytes 61448 | tf_op jit(solution)/shard_map/ppermute | solution.py:723
  37.2 3.7 %collective-permute-start.10 = (f32[16,128]{1,0:T(8,128)S(1)}, f32[16,128]{1,0:T(8,128)S(1)}, u32[]{:S(2)}, u32[]{:S(2)}) collective-permute-start(f32[16,128]{1,0:T(8,128)S(1)} %shard_map.107.own_ref), channel_id=1, source_target_pairs={{0,1},{1,0},{2,3},{3,2},{4,5},{5,4},{6,7},{7,6},{8,9},{9,8},{10,11... | collective-permute-start | bytes 24584 | tf_op jit(solution)/shard_map/ppermute | solution.py:723
  38.7 2.2 %collective-permute-start.9 = (f32[16,128]{1,0:T(8,128)S(1)}, f32[16,128]{1,0:T(8,128)S(1)}, u32[]{:S(2)}, u32[]{:S(2)}) collective-permute-start(f32[16,128]{1,0:T(8,128)S(1)} %shard_map.107.own_ref), channel_id=1, source_target_pairs={{1,2},{2,1},{3,4},{4,3},{5,6},{6,5},{7,8},{8,7},{9,10},{10,9},{11,... | collective-permute-start | bytes 24584 | tf_op jit(solution)/shard_map/ppermute | solution.py:723
  43.2 5.9 %collective-permute-start.11 = (f32[128,128]{1,0:T(8,128)S(1)}, f32[128,128]{1,0:T(8,128)S(1)}, u32[]{:S(2)}, u32[]{:S(2)}) collective-permute-start(f32[128,128]{1,0:T(8,128)S(1)} %get-tuple-element.55), channel_id=1, source_target_pairs={{1,2},{2,1},{3,4},{4,3},{5,6},{6,5},{7,8},{8,7},{9,10},{10,9},{11,... | collective-permute-start | bytes 196616 | tf_op jit(solution)/shard_map/ppermute | solution.py:723
  43.8 7.5 %collective-permute-start.12 = (f32[128,128]{1,0:T(8,128)S(1)}, f32[128,128]{1,0:T(8,128)S(1)}, u32[]{:S(2)}, u32[]{:S(2)}) collective-permute-start(f32[128,128]{1,0:T(8,128)S(1)} %get-tuple-element.56), channel_id=1, source_target_pairs={{0,1},{1,0},{2,3},{3,2},{4,5},{5,4},{6,7},{7,6},{8,9},{9,8},{10,11... | collective-permute-start | bytes 196616 | tf_op jit(solution)/shard_map/ppermute | solution.py:723
  51.9 9.2 %collective-permute-start.13 = (f32[64,128]{1,0:T(8,128)S(1)}, f32[64,128]{1,0:T(8,128)S(1)}, u32[]{:S(2)}, u32[]{:S(2)}) collective-permute-start(f32[64,128]{1,0:T(8,128)S(1)} %get-tuple-element.62), channel_id=1, source_target_pairs={{1,2},{2,1},{3,4},{4,3},{5,6},{6,5},{7,8},{8,7},{9,10},{10,9},{11,... | collective-permute-start | bytes 98312 | tf_op jit(solution)/shard_map/ppermute | solution.py:723
  52.6 10.4 %collective-permute-start.14 = (f32[64,128]{1,0:T(8,128)S(1)}, f32[64,128]{1,0:T(8,128)S(1)}, u32[]{:S(2)}, u32[]{:S(2)}) collective-permute-start(f32[64,128]{1,0:T(8,128)S(1)} %get-tuple-element.63), channel_id=1, source_target_pairs={{0,1},{1,0},{2,3},{3,2},{4,5},{5,4},{6,7},{7,6},{8,9},{9,8},{10,11... | collective-permute-start | bytes 98312 | tf_op jit(solution)/shard_map/ppermute | solution.py:723
  64.2 28.4 %collective-permute-start.15 = (f32[64,128]{1,0:T(8,128)S(1)}, f32[64,128]{1,0:T(8,128)S(1)}, u32[]{:S(2)}, u32[]{:S(2)}) collective-permute-start(f32[64,128]{1,0:T(8,128)S(1)} %get-tuple-element.67), channel_id=1, source_target_pairs={{1,2},{2,1},{3,4},{4,3},{5,6},{6,5},{7,8},{8,7},{9,10},{10,9},{11,... | collective-permute-start | bytes 98312 | tf_op jit(solution)/shard_map/ppermute | solution.py:723
  64.9 27.7 %collective-permute-start.16 = (f32[64,128]{1,0:T(8,128)S(1)}, f32[64,128]{1,0:T(8,128)S(1)}, u32[]{:S(2)}, u32[]{:S(2)}) collective-permute-start(f32[64,128]{1,0:T(8,128)S(1)} %get-tuple-element.68), channel_id=1, source_target_pairs={{0,1},{1,0},{2,3},{3,2},{4,5},{5,4},{6,7},{7,6},{8,9},{9,8},{10,11... | collective-permute-start | bytes 98312 | tf_op jit(solution)/shard_map/ppermute | solution.py:723
  70.2 30.4 %all-to-all-start = ((f32[64,1,128]{2,1,0:T(1,128)}), f32[64,1,128]{2,1,0:T(1,128)S(1)}, u32[]{:S(2)}, u32[]{:S(2)}) async-start(f32[64,1,128]{2,1,0:T(1,128)} %bitcast.4), calls=%async_computation | async-start | bytes 65536 | tf_op jit(solution)/shard_map/all_to_all | solution.py:716

commit v6 on v5

--- a/solution.py
+++ b/solution.py
@@ -9,7 +9,6 @@
 from jax.sharding import PartitionSpec as P
 
 
-HIGHEST = lax.Precision.HIGHEST
 N_DOM = 64
 N_REC = 2048
 CAP = 1024
@@ -17,7 +16,7 @@
 BY_DOT = 3
 LANES = 128
 BLOCK = 512
-CHUNK = 104
+HALF = 256
 
 
 def both_ways(lows, distance):
@@ -26,14 +25,24 @@
 
 CROSS_1 = both_ways(range(1, N_DOM - 1, 2), 1)
 INNER_1 = both_ways(range(0, N_DOM - 1, 2), 1)
-CROSS_2 = both_ways([q for q in range(N_DOM - 2) if q % 4 >= 2], 2)
+MIDDLE_1 = both_ways([q for q in range(N_DOM - 1) if q % 4 == 1], 1)
+SHIFTED = [[(4 * g + 2 + t) % N_DOM for t in range(4)] for g in range(16)]
 INNER_2 = both_ways([q for q in range(N_DOM - 2) if q % 4 < 2], 2)
 
 
-def from_above(q):
-    odd = q % 2 == 1
-    late = q % 4 >= 2
-    return odd, jnp.logical_not(odd), late, jnp.logical_not(late)
+def pick_sides(q, inner_1, middle, inner_2, far):
+    r = q % 4
+    p = (q + 2) % 4
+
+    def across(off):
+        return far(jnp.clip(p + off, 0, 3))
+
+    return (
+        jnp.where(r < 2, across(-2), inner_2),
+        jnp.where(r == 0, across(-1), jnp.where(r == 2, middle, inner_1)),
+        jnp.where(r == 3, across(1), jnp.where(r == 1, middle, inner_1)),
+        jnp.where(r >= 2, across(2), inner_2),
+    )
 
 
 def legendre_pair(values, degree):
@@ -165,17 +174,14 @@
     return jnp.where(iota((1, LANES), 1) == at, value, 0.0)
 
 
-def by_side(q, cross_1, inner_1, cross_2=None, inner_2=None):
-    above = from_above(q)
-    out = (jnp.where(above[0], inner_1, cross_1), jnp.where(above[0], cross_1, inner_1))
-    if cross_2 is not None:
-        out += (jnp.where(above[2], inner_2, cross_2), jnp.where(above[2], cross_2, inner_2))
-    return out
+def by_side(q, cross, inner):
+    odd = q % 2 == 1
+    return jnp.where(odd, inner, cross), jnp.where(odd, cross, inner)
 
 
 def route_kernel(
-    place_ref, weights_ref, owner_ref, element_ref, geometry_ref, wall_ref, forcing_ref,
-    cross_1_ref, inner_1_ref, cross_2_ref, inner_2_ref, own_ref, moves_ref, slots_ref,
+    place_ref, weights_ref, owner_ref, element_ref, inner_1_ref, middle_ref, inner_2_ref,
+    far_ref, own_ref, moves_ref, slots_ref,
 ):
     q = place_ref[0]
     width = N_REC
@@ -218,21 +224,32 @@
         slot = jnp.where(lane < totals[s : s + 1, :], packs[s // 2][at : at + 4, :CAP], 0.0)
         for c in range(8):
             slots_ref[s, 4 * c : 4 * c + 4, :] = slot[:, c * LANES : (c + 1) * LANES]
-    above = from_above(q)
-    bottom, top = forcing_ref[0:64, :], forcing_ref[448:512, :]
+    slots_ref[5] = jnp.zeros((32, LANES), jnp.float32)
+    r = q % 4
+    p = (q + 2) % 4
+    inner_1_ref[...] = slots_ref[jnp.where(q % 2 == 0, 3, 1)]
+    middle_ref[...] = slots_ref[jnp.where(r == 1, 3, 1)]
+    inner_2_ref[...] = slots_ref[jnp.where(r < 2, 4, 0)]
+    for t in range(4):
+        off = t - p
+        inside = (r + off >= 0) & (r + off <= 3)
+        beyond = (off < -2) | (off > 2)
+        far_ref[t] = slots_ref[jnp.where(inside | beyond, 5, off + 2)]
+    own_ref[...] = slots_ref[2]
+
+
+def heads_kernel(place_ref, geometry_ref, wall_ref, forcing_ref, cross_ref, inner_ref):
+    odd = place_ref[0] % 2 == 1
     spread = jnp.where(iota((8, LANES), 1) % 8 == iota((8, LANES), 0), 1.0, 0.0)
     wall = lax.dot(
         wall_ref[...].astype(jnp.float32), spread, preferred_element_type=jnp.float32
     )
-    for target_ref, up in ((cross_1_ref, above[0]), (inner_1_ref, above[1])):
-        target_ref[0:32, :] = jnp.where(up, slots_ref[3], slots_ref[1])
-        target_ref[32:36, :] = geometry_ref[...]
-        target_ref[36:38, :] = wall
-        target_ref[38:40, :] = jnp.zeros((2, LANES), jnp.float32)
-        target_ref[40:104, :] = jnp.where(up, top, bottom)
-    for target_ref, up in ((cross_2_ref, above[2]), (inner_2_ref, above[3])):
-        target_ref[...] = jnp.where(up, slots_ref[4], slots_ref[0])
-    own_ref[...] = slots_ref[2]
+    bottom, top = forcing_ref[0:64, :], forcing_ref[448:512, :]
+    for target_ref, up in ((cross_ref, odd), (inner_ref, jnp.logical_not(odd))):
+        target_ref[0:4, :] = geometry_ref[...]
+        target_ref[4:6, :] = wall
+        target_ref[6:8, :] = jnp.zeros((2, LANES), jnp.float32)
+        target_ref[8:72, :] = jnp.where(up, top, bottom)
 
 
 def split_kernel(fields_ref, out_ref):
@@ -266,23 +283,34 @@
 def eval_kernel(*refs):
     fields_ref, donors_ref, *refs = refs
     half = len(refs) // 2
+    pairs = []
     for source, target in zip(refs[:half], refs[half:]):
+        if len(source.shape) == 2:
+            pairs.append((source, target))
+        else:
+            pairs += [(source.at[t], target.at[t]) for t in range(source.shape[0])]
+    for source, target in pairs:
         words = source[0:32, :]
         valid = jnp.where((iota((32, LANES), 0) % 4 == 3) & (words > 0.0), 1, 0)
-        blocks = (jnp.sum(valid) + BLOCK - 1) // BLOCK
-
-        def one_block(b, carry, source=source, target=target):
-            start = pl.multiple_of(b * BLOCK, BLOCK)
-            tiles = source[pl.ds(pl.multiple_of(b * 16, 16), 16), :]
-            words = jnp.concatenate([tiles[4 * n : 4 * n + 4, :] for n in range(4)], axis=1)
+        count = jnp.sum(valid)
+        blocks = (count + HALF - 1) // BLOCK
+        left = (count - blocks * BLOCK + BLOCK - 1) // BLOCK
+
+        def one_block(b, first, size, source=source, target=target):
+            start = pl.multiple_of(b * size + first, HALF)
+            rows = size // 32
+            tiles = source[pl.ds(pl.multiple_of(b * rows + first // 32, 8), rows), :]
+            words = jnp.concatenate(
+                [tiles[4 * n : 4 * n + 4, :] for n in range(rows // 4)], axis=1
+            )
             element = words[3:4, :].astype(jnp.int32) - 1
-            hot_rows = iota((LANES, BLOCK), 0)
+            hot_rows = iota((LANES, size), 0)
             hot = (hot_rows == element).astype(jnp.float32).astype(jnp.bfloat16)
             hot = jnp.concatenate([hot, hot], axis=0)
             element = jnp.maximum(element, 0)
             along = [basis_rows(words[d : d + 1, :]) for d in range(3)]
-            row = iota((8, BLOCK), 0)
-            wx = jnp.broadcast_to(along[0][0], (8, BLOCK))
+            row = iota((8, size), 0)
+            wx = jnp.broadcast_to(along[0][0], (8, size))
             for i in range(1, 8):
                 wx = jnp.where(row == i, along[0][i], wx)
 
@@ -306,7 +334,7 @@
                     over_j * wx[:, part], axis=0, keepdims=True
                 )
 
-            gathers = [(f, h) for f in range(BY_DOT, FIELDS) for h in range(BLOCK // LANES)]
+            gathers = [(f, h) for f in range(BY_DOT, FIELDS) for h in range(size // LANES)]
             for f in range(BY_DOT):
                 picked = lax.dot(fields_ref[f], hot, preferred_element_type=jnp.float32)
                 share = -(-len(gathers) // (BY_DOT - f))
@@ -319,22 +347,30 @@
                 over_j = over_k[0:8, :] * along[1][0]
                 for j in range(1, 8):
                     over_j = over_j + over_k[8 * j : 8 * j + 8, :] * along[1][j]
-                target[f : f + 1, pl.ds(start, BLOCK)] = jnp.sum(
+                target[f : f + 1, pl.ds(start, size)] = jnp.sum(
                     over_j * wx, axis=0, keepdims=True
                 )
+
+        def whole(b, carry, one_block=one_block):
+            one_block(b, 0, BLOCK)
             return carry
 
-        lax.fori_loop(0, blocks, one_block, 0)
+        def part(b, carry, one_block=one_block, first=blocks * BLOCK):
+            one_block(b, first, HALF)
+            return carry
+
+        lax.fori_loop(0, blocks, whole, 0)
+        lax.fori_loop(0, left, part, 0)
 
 
 def unpack_kernel(
-    place_ref, cross_1_ref, inner_1_ref, cross_2_ref, inner_2_ref, own_ref, moves_ref, owner_ref,
+    place_ref, inner_1_ref, middle_ref, inner_2_ref, far_ref, own_ref, moves_ref, owner_ref,
     out_ref,
 ):
     q = place_ref[0]
     width = N_REC
-    below_1, above_1, below_2, above_2 = by_side(
-        q, cross_1_ref[...], inner_1_ref[...], cross_2_ref[...], inner_2_ref[...]
+    below_2, below_1, above_1, above_2 = pick_sides(
+        q, inner_1_ref[...], middle_ref[...], inner_2_ref[...], lambda t: far_ref[t]
     )
     zeros = jnp.zeros((FIELDS, CAP), jnp.float32)
     values = [
@@ -358,13 +394,14 @@
 
 
 def share_kernel(
-    place_ref, cross_1_ref, inner_1_ref, cross_2_ref, inner_2_ref, own_ref, moves_ref, owner_ref,
-    share_ref,
+    place_ref, inner_1_ref, middle_ref, inner_2_ref, far_ref, own_ref, moves_ref, owner_ref,
+    cross_head_ref, inner_head_ref, share_ref, cross_ref, inner_ref,
 ):
     q = place_ref[0]
     width = N_REC
-    below_1, above_1, below_2, above_2 = by_side(
-        q, *(ref[0:1, :] for ref in (cross_1_ref, inner_1_ref, cross_2_ref, inner_2_ref))
+    below_2, below_1, above_1, above_2 = pick_sides(
+        q, inner_1_ref[0:1, :], middle_ref[0:1, :], inner_2_ref[0:1, :],
+        lambda t: far_ref[t, 0:1, :],
     )
     row = iota((8, CAP), 0)
     values = jnp.broadcast_to(below_2, (8, CAP))
@@ -382,6 +419,9 @@
     out = jnp.sum(jnp.where(mine, values, 0.0), axis=0, keepdims=True)
     for n in range(16):
         share_ref[n : n + 1, :] = out[:, n * LANES : (n + 1) * LANES]
+    for target_ref, head_ref in ((cross_ref, cross_head_ref), (inner_ref, inner_head_ref)):
+        target_ref[0:16, :] = share_ref[...]
+        target_ref[16:88, :] = head_ref[...]
 
 
 def prep_kernel(
@@ -389,7 +429,7 @@
     inverse_ref, free_ref, load_ref, beside_ref, plane_ref, below_ref, above_ref,
 ):
     q = place_ref[0]
-    below_ref[...], above_ref[...] = by_side(q, cross_ref[32:104, :], inner_ref[32:104, :])
+    below_ref[...], above_ref[...] = by_side(q, cross_ref[16:88, :], inner_ref[16:88, :])
     beside_ref[0:8, :] = below_ref[0:8, :]
     beside_ref[8:16, :] = above_ref[0:8, :]
     wcol = w_column()
@@ -513,31 +553,36 @@
     inner_ref, v_ref, face_ref,
 ):
     q = place_ref[0]
-    below, above = by_side(q, cross_in_ref[...], inner_in_ref[...])
-    pick_row = iota((8, LANES), 0)
-    pick_lane = iota((8, LANES), 1)
+    below, above = by_side(q, cross_in_ref[0:16, :], inner_in_ref[0:16, :])
+    pick_row = iota((32, 2 * LANES), 0)
+    pick_lane = iota((32, 2 * LANES), 1)
+    odd = pick_lane // LANES
     picks = [
-        [
-            jnp.where(pick_lane == pick_row * 16 + (8 * odd + 7 * s), 1.0, 0.0)
-            for odd in range(2)
-        ]
+        jnp.where(
+            (pick_lane % LANES == pick_row % 8 * 16 + (8 * odd + 7 * s)) & (pick_row < 24), 1.0, 0.0
+        ).astype(jnp.bfloat16)
         for s in range(2)
     ]
+
+    def bf16_parts(value):
+        parts = []
+        for _ in range(3):
+            part = value.astype(jnp.bfloat16)
+            parts.append(part.astype(jnp.float32))
+            value = value - parts[-1]
+        return jnp.concatenate([*parts, jnp.zeros_like(value)], axis=0).astype(jnp.bfloat16)
 
     layers = (below, own_ref[...], above)
     received = {off: [] for off in range(-1, 2)}
     for s in range(2):
         values = jnp.concatenate([layer[8 * s : 8 * s + 8, :] for layer in layers], axis=1)
-        halves = [
-            lax.dot_general(
-                values, picks[s][odd], (((0,), (0,)), ((), ())),
-                precision=HIGHEST, preferred_element_type=jnp.float32,
-            )
-            for odd in range(2)
-        ]
+        spread = lax.dot_general(
+            bf16_parts(values), picks[s], (((0,), (0,)), ((), ())),
+            preferred_element_type=jnp.float32,
+        )
         for n in range(3):
             at = n * LANES
-            plane = halves[0][at : at + 64, :] + halves[1][at + 64 : at + 128, :]
+            plane = spread[at : at + 64, :LANES] + spread[at + 64 : at + 128, LANES:]
             received[n - 1].append([plane[8 * k : 8 * k + 8, :] for k in range(8)])
     lane = iota((8, LANES), 1)
     j_row = iota((8, LANES), 0)
@@ -602,14 +647,14 @@
         jnp.zeros((1, LANES), jnp.float32),
     )
     send_faces(q, u_ref, cross_ref, inner_ref)
-    up = from_above(q)[0]
+    up = q % 2 == 1
     bottom, top = lift_ref[0:64, :], lift_ref[64:128, :]
     cross_ref[64:128, :] = jnp.where(up, top, bottom)
     inner_ref[64:128, :] = jnp.where(up, bottom, top)
 
 
 def send_faces(q, u_ref, cross_ref, inner_ref):
-    up = from_above(q)[0]
+    up = q % 2 == 1
     bottom, top = u_ref[0:64, :], u_ref[448:512, :]
     cross_ref[0:64, :] = jnp.where(up, top, bottom)
     inner_ref[0:64, :] = jnp.where(up, bottom, top)
@@ -716,12 +761,18 @@
     return lax.all_to_all(value, "dom", 0, 0, tiled=True)
 
 
-def to_neighbours(cross_1, inner_1, cross_2=None, inner_2=None):
-    lists = ((cross_1, CROSS_1), (cross_2, CROSS_2), (inner_1, INNER_1), (inner_2, INNER_2))
-    moved = []
-    for value, pairs in lists:
-        moved.append(None if value is None else lax.ppermute(value, "dom", pairs))
-    return [moved[n] for n in (0, 2, 1, 3) if moved[n] is not None]
+def to_four(inner_1, middle, inner_2, far):
+    far = lax.all_to_all(far, "dom", 0, 0, tiled=True, axis_index_groups=SHIFTED)
+    near = []
+    for value, pairs in ((inner_1, INNER_1), (middle, MIDDLE_1), (inner_2, INNER_2)):
+        near.append(lax.ppermute(value, "dom", pairs))
+    return (*near, far)
+
+
+def to_two(cross, inner):
+    cross = lax.ppermute(cross, "dom", CROSS_1)
+    inner = lax.ppermute(inner, "dom", INNER_1)
+    return cross, inner
 
 
 def body(donor_fields, interp_weights, donor_owner, donor_element, geometry, wall_flag, forcing):
@@ -731,46 +782,51 @@
     owner = donor_owner.reshape(1, N_REC)
     element = donor_element.reshape(1, N_REC)
     asked = ((32, LANES), F32)
-    with_head = ((CHUNK, LANES), F32)
     *requests, own, moves = call(
         route_kernel,
         (
             place,
             *(
                 pltpu.with_memory_space_constraint(value, pltpu.HBM)
-                for value in (interp_weights, owner, element, geometry, wall_flag, forcing)
+                for value in (interp_weights, owner, element)
             ),
         ),
-        (with_head, with_head, asked, asked, asked, ((8, CAP), jnp.int32)),
-        scratch=(((5, 32, LANES), F32),),
-    )
-    requests = to_neighbours(*requests)
+        (asked, asked, asked, ((4, 32, LANES), F32), asked, ((8, CAP), jnp.int32)),
+        scratch=(((6, 32, LANES), F32),),
+    )
+    requests = to_four(*requests)
     (fields,) = call(
         split_kernel, (donors,), (((BY_DOT, 512, 256), jnp.bfloat16),), smem_first=False,
     )
     answer = ((FIELDS, CAP), F32)
-    own_answer, inner_1 = call(
-        eval_kernel, (fields, donors, own, requests[1]), (answer,) * 2,
+    (far,) = call(
+        eval_kernel, (fields, donors, requests[3]), (((4, FIELDS, CAP), F32),),
         flops=3_000_000_000, smem_first=False, mib=24,
     )
-    cross_1, cross_2, inner_2 = call(
-        eval_kernel, (fields, donors, requests[0], requests[2], requests[3]), (answer,) * 3,
+    own_answer, inner_1, middle, inner_2 = call(
+        eval_kernel, (fields, donors, own, *requests[:3]), (answer,) * 4,
         flops=4_000_000_000, smem_first=False, mib=24,
     )
-    answered = to_neighbours(cross_1, inner_1, cross_2, inner_2)
+    answered = to_four(inner_1, middle, inner_2, far)
+    head = ((72, LANES), F32)
+    heads = call(heads_kernel, (place, geometry, wall_flag, forcing), (head, head))
+    unpacked = (place, *answered, own_answer, moves, owner)
+    with_head = ((88, LANES), F32)
+    share, *spread = call(
+        share_kernel, (*unpacked, *heads), (((16, LANES), F32), with_head, with_head)
+    )
+    (interface,) = call(unpack_kernel, unpacked, (((FIELDS, N_REC), F32),))
+    spread = to_two(*spread)
     inverse, free, load, beside = call(
-        prep_kernel, (place, geometry, wall_flag, forcing, requests[0], requests[1]),
+        prep_kernel, (place, geometry, wall_flag, forcing, *spread),
         (FIELD, FIELD, FIELD, ((16, LANES), F32)),
         scratch=(((64, LANES), F32), ((72, LANES), F32), ((72, LANES), F32)),
     )
-    unpacked = (place, *answered, own_answer, moves, owner)
-    (share,) = call(share_kernel, unpacked, (((16, LANES), F32),))
-    (interface,) = call(unpack_kernel, unpacked, (((FIELDS, N_REC), F32),))
     face = ((64, LANES), F32)
     two_faces = ((128, LANES), F32)
     w0, u, edge, lift, moments, *faces = call(
         first_kernel,
-        (place, share, *to_neighbours(share, share), geometry, beside, inverse, free,
+        (place, share, *spread, geometry, beside, inverse, free,
          load, xmat),
         (FIELD, FIELD, two_faces, two_faces, ((1, LANES), F32), two_faces, two_faces),
         scratch=(FIELD, two_faces),
@@ -778,16 +834,16 @@
     fixed = (geometry, inverse, free, xmat)
     w1, u, moments, *faces, w0_faces = call(
         functools.partial(next_kernel, 2),
-        (place, w0, u, *to_neighbours(*faces), *fixed, moments, load, lift),
+        (place, w0, u, *to_two(*faces), *fixed, moments, load, lift),
         (FIELD, FIELD, ((1, LANES), F32), face, face, two_faces), scratch=(FIELD,),
     )
     w2, u, moments, *faces = call(
         functools.partial(next_kernel, 4),
-        (place, w1, u, *to_neighbours(*faces), *fixed, moments),
+        (place, w1, u, *to_two(*faces), *fixed, moments),
         (FIELD, FIELD, ((N_DOM, LANES), F32), face, face), scratch=(FIELD,),
     )
     sums = to_all(moments)
-    (image,) = call(image_kernel, (place, u, *to_neighbours(*faces), free), (FIELD,))
+    (image,) = call(image_kernel, (place, u, *to_two(*faces), free), (FIELD,))
     velocity, residual = call(
         last_kernel, (w0, w0_faces, w1, w2, image, inverse, edge, sums), (FIELD, FIELD), smem_first=False,
     )

time: 103 us -> 103 us (level)
  waiting for transfers between devices: 16.8 us -> 15.3 us
  Pallas kernels: 14.9 us -> 16 us
    all_to_all x0 -> x2, starting transfers between devices: none -> 21.2 us  [to_four(): lax.all_to_all(far, 'dom', 0, 0, tiled=True, axis_index_groups=SHIFTED)]
    ppermute x16 -> x14, starting transfers between devices: 48.8 us -> 33.3 us  [the longest x4 18.3 us: to_two(): inner = lax.ppermute(inner, 'dom', INNER_1)]
    all_to_all x1, starting transfers between devices: 20.9 us -> 15.7 us  [to_all(): return lax.all_to_all(value, 'dom', 0, 0, tiled=True)]
    ppermute x16 -> x14, waiting for transfers between devices: 8.79 us -> 7.29 us  [the longest x4 5.5 us: to_two(): inner = lax.ppermute(inner, 'dom', INNER_1)]
    pallas_call x12 -> x13, Pallas kernels: 14.9 us -> 16 us  [call(): pl.pallas_call(kernel, out_shape=out_shape, in_specs=specs, out_specs=[VM...]
  transfers between devices with their start and end apart: 18 -> 18, of which waited for: 6 -> 5; matrix products, arithmetic and copies ran while one was open for 0% -> 0% of each run, Pallas kernels for 8% -> 9%
where the time goes in v6:
time: 103 us; the launch traced here: 102 us
  starting transfers between devices  70.3 us (68%)
  Pallas kernels  16 us (16%)
  waiting for transfers between devices  15.3 us (15%)
    all_to_all x2, starting transfers between devices, to_four(): lax.all_to_all(far, 'dom', 0, 0, tiled=True, axis_index_groups=SHIFTED)  21.2 us
    ppermute x4, starting transfers between devices, to_two(): inner = lax.ppermute(inner, 'dom', INNER_1)  18.3 us
    pallas_call x13, Pallas kernels, call(): pl.pallas_call(kernel, out_shape=out_shape, in_specs=specs, out_specs=[VM...  16 us
    all_to_all x1, starting transfers between devices, to_all(): return lax.all_to_all(value, 'dom', 0, 0, tiled=True)  15.7 us
    ppermute x6, starting transfers between devices, to_four(): near.append(lax.ppermute(value, 'dom', pairs))  12.4 us
    all_to_all x1, waiting for transfers between devices, to_all(): return lax.all_to_all(value, 'dom', 0, 0, tiled=True)  7.96 us
    ppermute x4, waiting for transfers between devices, to_two(): inner = lax.ppermute(inner, 'dom', INNER_1)  5.5 us
    ppermute x4, starting transfers between devices, to_two(): cross = lax.ppermute(cross, 'dom', CROSS_1)  2.63 us
  transfers between devices with their start and end apart: 18, of which 5 were waited for; matrix products, arithmetic and copies ran while one was open for 0% of the time, Pallas kernels for 9%

profile of v6, /device:TPU:0, one launch (start us, length us, event | category | flops | bytes accessed | tf_op | source)
XLA Modules:
  0.0 102.4 jit_solution(4027582830409716061)
XLA Ops:
  0.7 2.8 %shard_map.104 = (f32[32,128]{1,0:T(8,128)S(1)}, f32[32,128]{1,0:T(8,128)S(1)}, f32[32,128]{1,0:T(8,128)S(1)}, f32[4,32,128]{2,1,0:T(8,128)}, f32[32,128]{1,0:T(8,128)S(1)}, /*index=5*/s32[8,1024]{1,0:T(8,128)S(1)}) custom-call(s32[1]{0:T(128)} %bitcast.place_ref, f32[3,8,2048]{2,1,0:T(8,128)} %weights_ref.1, s32[1,2048]{1,0:T(1,128)} %bitcast.8, ...), custom_call_target="tpu_custom_call" | custom-call | flops 100000 | bytes 1000000 | tf_op jit(solution)/shard_map/pallas_call | solution.py:745
  3.6 12.2 %all-to-all-start = ((f32[4,32,128]{2,1,0:T(8,128)}), f32[4,32,128]{2,1,0:T(8,128)S(1)}, u32[]{:S(2)}, u32[]{:S(2)}) async-start(f32[4,32,128]{2,1,0:T(8,128)} %get-tuple-element.49), calls=%async_computation | async-start | bytes 131072 | tf_op jit(solution)/shard_map/all_to_all | solution.py:765
  16.4 5.4 %collective-permute-start.3 = (f32[32,128]{1,0:T(8,128)S(1)}, f32[32,128]{1,0:T(8,128)S(1)}, u32[]{:S(2)}, u32[]{:S(2)}) collective-permute-start(f32[32,128]{1,0:T(8,128)S(1)} %get-tuple-element.45), channel_id=1, source_target_pairs={{0,2},{2,0},{1,3},{3,1},{4,6},{6,4},{5,7},{7,5},{8,10},{10,8},{9,1... | collective-permute-start | bytes 49160 | tf_op jit(solution)/shard_map/ppermute | solution.py:768
  22.0 1.2 %shard_map.106 = f32[4,5,1024]{2,1,0:T(8,128)} custom-call(bf16[3,512,256]{2,1,0:T(8,128)(2,1)S(1)} %shard_map.103.refs_0_, f32[5,512,128]{2,1,0:T(8,128)S(1)} %collective-permute-done.fields_ref.refs_1_, f32[4,32,128]{2,1,0:T(8,128)S(1)} %all-to-all-done.refs_2_), custom_call_target="tpu_custom_call" | custom-call | flops 3000000000 | bytes 1000000 | tf_op jit(solution)/shard_map/pallas_call | solution.py:745
  23.3 9.0 %all-to-all-start.1 = ((f32[4,5,1024]{2,1,0:T(8,128)}), f32[4,5,1024]{2,1,0:T(8,128)S(1)}, u32[]{:S(2)}, u32[]{:S(2)}) async-start(f32[4,5,1024]{2,1,0:T(8,128)} %shard_map.106), calls=%async_computation.1 | async-start | bytes 262144 | tf_op jit(solution)/shard_map/all_to_all | solution.py:765
  32.4 3.5 %shard_map.105 = (f32[5,1024]{1,0:T(8,128)S(1)}, f32[5,1024]{1,0:T(8,128)S(1)}, f32[5,1024]{1,0:T(8,128)S(1)}, f32[5,1024]{1,0:T(8,128)S(1)}) custom-call(bf16[3,512,256]{2,1,0:T(8,128)(2,1)S(1)} %shard_map.103.refs_0_, f32[5,512,128]{2,1,0:T(8,128)S(1)} %collective-permute-done.fields_ref.refs_1_, f32[32,128]{1,0:T(8,128)S(1)} %get-tuple-element.42.refs_2_, ...), custom_call_target="tpu_custom_call" | custom-call | flops 4000000000 | bytes 1000000 | tf_op jit(solution)/shard_map/pallas_call | solution.py:745
  35.9 1.5 %collective-permute-start.4 = (f32[5,1024]{1,0:T(8,128)S(1)}, f32[5,1024]{1,0:T(8,128)S(1)}, u32[]{:S(2)}, u32[]{:S(2)}) collective-permute-start(f32[5,1024]{1,0:T(8,128)S(1)} %get-tuple-element.46), channel_id=1, source_target_pairs={{0,1},{1,0},{2,3},{3,2},{4,5},{5,4},{6,7},{7,6},{8,9},{9,8},{10,11... | collective-permute-start | bytes 61448 | tf_op jit(solution)/shard_map/ppermute | solution.py:768
  38.0 4.2 %collective-permute-start.6 = (f32[5,1024]{1,0:T(8,128)S(1)}, f32[5,1024]{1,0:T(8,128)S(1)}, u32[]{:S(2)}, u32[]{:S(2)}) collective-permute-start(f32[5,1024]{1,0:T(8,128)S(1)} %get-tuple-element.48), channel_id=1, source_target_pairs={{0,2},{2,0},{1,3},{3,1},{4,6},{6,4},{5,7},{7,5},{8,10},{10,8},{9,1... | collective-permute-start | bytes 61448 | tf_op jit(solution)/shard_map/ppermute | solution.py:768
  42.4 1.8 %collective-permute-done.6.inner_2_ref = f32[5,1024]{1,0:T(8,128)S(1)} collective-permute-done((f32[5,1024]{1,0:T(8,128)S(1)}, f32[5,1024]{1,0:T(8,128)S(1)}, u32[]{:S(2)}, u32[]{:S(2)}) %collective-permute-start.6) | collective-permute-done | bytes 20512 | tf_op jit(solution)/shard_map/ppermute | solution.py:768
  44.7 0.7 collective-permute-start.7
  45.4 4.8 %collective-permute-start.8 = (f32[88,128]{1,0:T(8,128)S(1)}, f32[88,128]{1,0:T(8,128)S(1)}, u32[]{:S(2)}, u32[]{:S(2)}) collective-permute-start(f32[88,128]{1,0:T(8,128)S(1)} %get-tuple-element.56), channel_id=1, source_target_pairs={{0,1},{1,0},{2,3},{3,2},{4,5},{5,4},{6,7},{7,6},{8,9},{9,8},{10,11... | collective-permute-start | bytes 135176 | tf_op jit(solution)/shard_map/ppermute | solution.py:774
  50.2 2.0 %collective-permute-done.8.inner_ref.inner_in_ref = f32[88,128]{1,0:T(8,128)S(1)} collective-permute-done((f32[88,128]{1,0:T(8,128)S(1)}, f32[88,128]{1,0:T(8,128)S(1)}, u32[]{:S(2)}, u32[]{:S(2)}) %collective-permute-start.8) | collective-permute-done | bytes 45088 | tf_op jit(solution)/shard_map/ppermute | solution.py:774
  52.2 0.9 shard_map.109
  53.2 1.6 %shard_map.110 = (f32[512,128]{1,0:T(8,128)S(1)}, f32[512,128]{1,0:T(8,128)S(1)}, f32[128,128]{1,0:T(8,128)S(1)}, f32[128,128]{1,0:T(8,128)S(1)}, f32[1,128]{1,0...) custom-call(s32[1]{0:T(128)} %bitcast.place_ref, f32[16,128]{1,0:T(8,128)S(1)} %get-tuple-element.54.own_ref, ...), custom_call_target="tpu_custom_call" | custom-call | flops 100000 | bytes 1000000 | tf_op jit(solution)/shard_map/pallas_call | solution.py:745
  54.8 2.1 %collective-permute-start.10 = (f32[128,128]{1,0:T(8,128)S(1)}, f32[128,128]{1,0:T(8,128)S(1)}, u32[]{:S(2)}, u32[]{:S(2)}) collective-permute-start(f32[128,128]{1,0:T(8,128)S(1)} %get-tuple-element.64), channel_id=1, source_target_pairs={{0,1},{1,0},{2,3},{3,2},{4,5},{5,4},{6,7},{7,6},{8,9},{9,8},{10,11... | collective-permute-start | bytes 196616 | tf_op jit(solution)/shard_map/ppermute | solution.py:774
  57.6 1.6 %collective-permute-done.10.inner_in_ref = f32[128,128]{1,0:T(8,128)S(1)} collective-permute-done((f32[128,128]{1,0:T(8,128)S(1)}, f32[128,128]{1,0:T(8,128)S(1)}, u32[]{:S(2)}, u32[]{:S(2)}) %collective-permute-start.10) | collective-permute-done | bytes 65568 | tf_op jit(solution)/shard_map/ppermute | solution.py:774
  60.4 5.8 %collective-permute-start.12 = (f32[64,128]{1,0:T(8,128)S(1)}, f32[64,128]{1,0:T(8,128)S(1)}, u32[]{:S(2)}, u32[]{:S(2)}) collective-permute-start(f32[64,128]{1,0:T(8,128)S(1)} %get-tuple-element.71), channel_id=1, source_target_pairs={{0,1},{1,0},{2,3},{3,2},{4,5},{5,4},{6,7},{7,6},{8,9},{9,8},{10,11... | collective-permute-start | bytes 98312 | tf_op jit(solution)/shard_map/ppermute | solution.py:774
  66.2 1.9 %collective-permute-done.12.inner_in_ref = f32[64,128]{1,0:T(8,128)S(1)} collective-permute-done((f32[64,128]{1,0:T(8,128)S(1)}, f32[64,128]{1,0:T(8,128)S(1)}, u32[]{:S(2)}, u32[]{:S(2)}) %collective-permute-start.12) | collective-permute-done | bytes 32800 | tf_op jit(solution)/shard_map/ppermute | solution.py:774
  68.1 1.2 %shard_map.112 = (f32[512,128]{1,0:T(8,128)S(1)}, f32[512,128]{1,0:T(8,128)S(1)}, f32[64,128]{1,0:T(8,128)}, f32[64,128]{1,0:T(8,128)S(1)}, f32[64,128]{1,0:T(8,128)S(1)}) custom-call(s32[1]{0:T(128)} %bitcast.place_ref, f32[512,128]{1,0:T(8,128)S(1)} %get-tuple-element.68.w_old_ref.w1_ref, f32[512,128]{1,0:T(8,128)S(1)} %get-tuple-element.69.u_old_ref, ...), custom_call_target="tpu_custom_call" | custom-call | flops 100000 | bytes 1000000 | tf_op jit(solution)/shard_map/pallas_call | solution.py:745
  70.0 5.6 %collective-permute-start.14 = (f32[64,128]{1,0:T(8,128)S(1)}, f32[64,128]{1,0:T(8,128)S(1)}, u32[]{:S(2)}, u32[]{:S(2)}) collective-permute-start(f32[64,128]{1,0:T(8,128)S(1)} %get-tuple-element.76), channel_id=1, source_target_pairs={{0,1},{1,0},{2,3},{3,2},{4,5},{5,4},{6,7},{7,6},{8,9},{9,8},{10,11... | collective-permute-start | bytes 98312 | tf_op jit(solution)/shard_map/ppermute | solution.py:774
  75.6 15.7 %all-to-all-start.2 = ((f32[64,1,128]{2,1,0:T(1,128)}), f32[64,1,128]{2,1,0:T(1,128)S(1)}, u32[]{:S(2)}, u32[]{:S(2)}) async-start(f32[64,1,128]{2,1,0:T(1,128)} %bitcast.4), calls=%async_computation.2 | async-start | bytes 65536 | tf_op jit(solution)/shard_map/all_to_all | solution.py:761
  91.3 1.5 %shard_map.115 = f32[5,2048]{1,0:T(8,128)} custom-call(s32[1]{0:T(128)} %bitcast.place_ref, f32[5,1024]{1,0:T(8,128)S(1)} %collective-permute-done.4.inner_1_ref, f32[5,1024]{1,0:T(8,128)S(1)} %collective-permute-done.5.middle_ref, f32[5,1024]{1,0:T(8,128)S(1)} %collective-permute-done.6.inner_2_ref, f32[4,5,1024]{2,1,0:T(8,128)S(1)} %all-to-all-done.1.far_ref, ...), custom_call_target="tpu_custom_call" | custom-call | flops 100000 | bytes 1000000 | tf_op jit(solution)/shard_map/pallas_call | solution.py:745
  92.9 8.0 %all-to-all-done.2 = f32[64,1,128]{2,1,0:T(1,128)S(1)} async-done(((f32[64,1,128]{2,1,0:T(1,128)}), f32[64,1,128]{2,1,0:T(1,128)S(1)}, u32[]{:S(2)}, u32[]{:S(2)}) %all-to-all-start.2) | async-done | bytes 32800 | tf_op jit(solution)/shard_map/all_to_all | solution.py:761
  100.8 1.6 %shard_map.114 = (f32[512,128]{1,0:T(8,128)}, f32[512,128]{1,0:T(8,128)}) custom-call(f32[512,128]{1,0:T(8,128)S(1)} %get-tuple-element.61.w_old_ref.w0_ref, f32[128,128]{1,0:T(8,128)S(1)} %get-tuple-element.67.face_ref, f32[512,128]{1,0:T(8,128)S(1)} %get-tuple-element.68.w_old_ref.w1_ref, f32[512,128]{1,0:T(8,128)S(1)} %get-tuple-element.73.w2_ref, ...), custom_call_target="tpu_custom_call" | custom-call | flops 100000 | bytes 1000000 | tf_op jit(solution)/shard_map/pallas_call | solution.py:745
  (35 shorter events, 5.0 us)
Async XLA Ops:
  0.6 21.2 %collective-permute-start = (f32[5,512,128]{2,1,0:T(8,128)}, f32[5,512,128]{2,1,0:T(8,128)S(1)}, u32[]{:S(2)}, u32[]{:S(2)}) collective-permute-start(f32[5,512,128]{2,1,0:T(8,128)} %param.8), channel_id=1, source_target_pairs={{0,64},{64,0},{1,65},{65,1},{2,66},{66,2},{3,67},{67,3},{4,68},{68... | collective-permute-start | bytes 3932168 | tf_op jit(solution)/shard_map/ppermute | solution.py:781
  3.6 18.5 %all-to-all-start = ((f32[4,32,128]{2,1,0:T(8,128)}), f32[4,32,128]{2,1,0:T(8,128)S(1)}, u32[]{:S(2)}, u32[]{:S(2)}) async-start(f32[4,32,128]{2,1,0:T(8,128)} %get-tuple-element.49), calls=%async_computation | async-start | bytes 131072 | tf_op jit(solution)/shard_map/all_to_all | solution.py:765
  15.8 16.5 %collective-permute-start.1 = (f32[32,128]{1,0:T(8,128)S(1)}, f32[32,128]{1,0:T(8,128)S(1)}, u32[]{:S(2)}, u32[]{:S(2)}) collective-permute-start(f32[32,128]{1,0:T(8,128)S(1)} %get-tuple-element.43), channel_id=1, source_target_pairs={{0,1},{1,0},{2,3},{3,2},{4,5},{5,4},{6,7},{7,6},{8,9},{9,8},{10,11... | collective-permute-start | bytes 49160 | tf_op jit(solution)/shard_map/ppermute | solution.py:768
  15.8 16.5 %collective-permute-start.2 = (f32[32,128]{1,0:T(8,128)S(1)}, f32[32,128]{1,0:T(8,128)S(1)}, u32[]{:S(2)}, u32[]{:S(2)}) collective-permute-start(f32[32,128]{1,0:T(8,128)S(1)} %get-tuple-element.44), channel_id=1, source_target_pairs={{1,2},{2,1},{5,6},{6,5},{9,10},{10,9},{13,14},{14,13},{17,18},{18,... | collective-permute-start | bytes 49160 | tf_op jit(solution)/shard_map/ppermute | solution.py:768
  16.4 15.9 %collective-permute-start.3 = (f32[32,128]{1,0:T(8,128)S(1)}, f32[32,128]{1,0:T(8,128)S(1)}, u32[]{:S(2)}, u32[]{:S(2)}) collective-permute-start(f32[32,128]{1,0:T(8,128)S(1)} %get-tuple-element.45), channel_id=1, source_target_pairs={{0,2},{2,0},{1,3},{3,1},{4,6},{6,4},{5,7},{7,5},{8,10},{10,8},{9,1... | collective-permute-start | bytes 49160 | tf_op jit(solution)/shard_map/ppermute | solution.py:768
  23.3 20.8 %all-to-all-start.1 = ((f32[4,5,1024]{2,1,0:T(8,128)}), f32[4,5,1024]{2,1,0:T(8,128)S(1)}, u32[]{:S(2)}, u32[]{:S(2)}) async-start(f32[4,5,1024]{2,1,0:T(8,128)} %shard_map.106), calls=%async_computation.1 | async-start | bytes 262144 | tf_op jit(solution)/shard_map/all_to_all | solution.py:765
  32.3 9.9 %copy-start = (f32[512,128]{1,0:T(8,128)S(1)}, f32[512,128]{1,0:T(8,128)}, u32[]{:S(2)}) copy-start(f32[512,128]{1,0:T(8,128)} %forcing_ref.3) | copy-start | bytes 786436
  32.3 9.9 %copy-start.3 = (f32[4,128]{1,0:T(4,128)S(1)}, f32[4,128]{1,0:T(4,128)}, u32[]{:S(2)}) copy-start(f32[4,128]{1,0:T(4,128)} %geometry_ref.9) | copy-start | bytes 6148
  32.3 9.9 %copy-start.4 = (s32[2,8]{1,0:T(2,128)S(1)}, s32[2,8]{1,0:T(2,128)}, u32[]{:S(2)}) copy-start(s32[2,8]{1,0:T(2,128)} %wall_ref.3) | copy-start | bytes 196
  32.4 11.8 %copy-start.2 = (s32[2048,1]{0,1:T(1,128)S(1)}, s32[2048,1]{0,1:T(1,128)}, u32[]{:S(2)}) copy-start(s32[2048,1]{0,1:T(1,128)} %param.10) | copy-start | bytes 24580
  32.4 20.8 %copy-start.1 = (bf16[64,192]{1,0:T(8,128)(2,1)S(1)}, bf16[64,192]{1,0:T(8,128)(2,1)}, u32[]{:S(2)}) copy-start(bf16[64,192]{1,0:T(8,128)(2,1)} %constant.12.xmat_ref) | copy-start | bytes 73732
  35.9 6.5 %collective-permute-start.4 = (f32[5,1024]{1,0:T(8,128)S(1)}, f32[5,1024]{1,0:T(8,128)S(1)}, u32[]{:S(2)}, u32[]{:S(2)}) collective-permute-start(f32[5,1024]{1,0:T(8,128)S(1)} %get-tuple-element.46), channel_id=1, source_target_pairs={{0,1},{1,0},{2,3},{3,2},{4,5},{5,4},{6,7},{7,6},{8,9},{9,8},{10,11... | collective-permute-start | bytes 61448 | tf_op jit(solution)/shard_map/ppermute | solution.py:768
  37.4 5.0 %collective-permute-start.5 = (f32[5,1024]{1,0:T(8,128)S(1)}, f32[5,1024]{1,0:T(8,128)S(1)}, u32[]{:S(2)}, u32[]{:S(2)}) collective-permute-start(f32[5,1024]{1,0:T(8,128)S(1)} %get-tuple-element.47), channel_id=1, source_target_pairs={{1,2},{2,1},{5,6},{6,5},{9,10},{10,9},{13,14},{14,13},{17,18},{18,... | collective-permute-start | bytes 61448 | tf_op jit(solution)/shard_map/ppermute | solution.py:768
  38.0 6.1 %collective-permute-start.6 = (f32[5,1024]{1,0:T(8,128)S(1)}, f32[5,1024]{1,0:T(8,128)S(1)}, u32[]{:S(2)}, u32[]{:S(2)}) collective-permute-start(f32[5,1024]{1,0:T(8,128)S(1)} %get-tuple-element.48), channel_id=1, source_target_pairs={{0,2},{2,0},{1,3},{3,1},{4,6},{6,4},{5,7},{7,5},{8,10},{10,8},{9,1... | collective-permute-start | bytes 61448 | tf_op jit(solution)/shard_map/ppermute | solution.py:768
  44.7 5.5 %collective-permute-start.7 = (f32[88,128]{1,0:T(8,128)S(1)}, f32[88,128]{1,0:T(8,128)S(1)}, u32[]{:S(2)}, u32[]{:S(2)}) collective-permute-start(f32[88,128]{1,0:T(8,128)S(1)} %get-tuple-element.55), channel_id=1, source_target_pairs={{1,2},{2,1},{3,4},{4,3},{5,6},{6,5},{7,8},{8,7},{9,10},{10,9},{11,... | collective-permute-start | bytes 135176 | tf_op jit(solution)/shard_map/ppermute | solution.py:773
  45.4 6.8 %collective-permute-start.8 = (f32[88,128]{1,0:T(8,128)S(1)}, f32[88,128]{1,0:T(8,128)S(1)}, u32[]{:S(2)}, u32[]{:S(2)}) collective-permute-start(f32[88,128]{1,0:T(8,128)S(1)} %get-tuple-element.56), channel_id=1, source_target_pairs={{0,1},{1,0},{2,3},{3,2},{4,5},{5,4},{6,7},{7,6},{8,9},{9,8},{10,11... | collective-permute-start | bytes 135176 | tf_op jit(solution)/shard_map/ppermute | solution.py:774
  54.8 4.3 %collective-permute-start.10 = (f32[128,128]{1,0:T(8,128)S(1)}, f32[128,128]{1,0:T(8,128)S(1)}, u32[]{:S(2)}, u32[]{:S(2)}) collective-permute-start(f32[128,128]{1,0:T(8,128)S(1)} %get-tuple-element.64), channel_id=1, source_target_pairs={{0,1},{1,0},{2,3},{3,2},{4,5},{5,4},{6,7},{7,6},{8,9},{9,8},{10,11... | collective-permute-start | bytes 196616 | tf_op jit(solution)/shard_map/ppermute | solution.py:774
  56.9 2.2 %collective-permute-start.9 = (f32[128,128]{1,0:T(8,128)S(1)}, f32[128,128]{1,0:T(8,128)S(1)}, u32[]{:S(2)}, u32[]{:S(2)}) collective-permute-start(f32[128,128]{1,0:T(8,128)S(1)} %get-tuple-element.63), channel_id=1, source_target_pairs={{1,2},{2,1},{3,4},{4,3},{5,6},{6,5},{7,8},{8,7},{9,10},{10,9},{11,... | collective-permute-start | bytes 196616 | tf_op jit(solution)/shard_map/ppermute | solution.py:773
  59.8 6.5 %collective-permute-start.11 = (f32[64,128]{1,0:T(8,128)S(1)}, f32[64,128]{1,0:T(8,128)S(1)}, u32[]{:S(2)}, u32[]{:S(2)}) collective-permute-start(f32[64,128]{1,0:T(8,128)S(1)} %get-tuple-element.70), channel_id=1, source_target_pairs={{1,2},{2,1},{3,4},{4,3},{5,6},{6,5},{7,8},{8,7},{9,10},{10,9},{11,... | collective-permute-start | bytes 98312 | tf_op jit(solution)/shard_map/ppermute | solution.py:773
  60.4 7.7 %collective-permute-start.12 = (f32[64,128]{1,0:T(8,128)S(1)}, f32[64,128]{1,0:T(8,128)S(1)}, u32[]{:S(2)}, u32[]{:S(2)}) collective-permute-start(f32[64,128]{1,0:T(8,128)S(1)} %get-tuple-element.71), channel_id=1, source_target_pairs={{0,1},{1,0},{2,3},{3,2},{4,5},{5,4},{6,7},{7,6},{8,9},{9,8},{10,11... | collective-permute-start | bytes 98312 | tf_op jit(solution)/shard_map/ppermute | solution.py:774
  69.4 23.4 %collective-permute-start.13 = (f32[64,128]{1,0:T(8,128)S(1)}, f32[64,128]{1,0:T(8,128)S(1)}, u32[]{:S(2)}, u32[]{:S(2)}) collective-permute-start(f32[64,128]{1,0:T(8,128)S(1)} %get-tuple-element.75), channel_id=1, source_target_pairs={{1,2},{2,1},{3,4},{4,3},{5,6},{6,5},{7,8},{8,7},{9,10},{10,9},{11,... | collective-permute-start | bytes 98312 | tf_op jit(solution)/shard_map/ppermute | solution.py:773
  70.0 22.8 %collective-permute-start.14 = (f32[64,128]{1,0:T(8,128)S(1)}, f32[64,128]{1,0:T(8,128)S(1)}, u32[]{:S(2)}, u32[]{:S(2)}) collective-permute-start(f32[64,128]{1,0:T(8,128)S(1)} %get-tuple-element.76), channel_id=1, source_target_pairs={{0,1},{1,0},{2,3},{3,2},{4,5},{5,4},{6,7},{7,6},{8,9},{9,8},{10,11... | collective-permute-start | bytes 98312 | tf_op jit(solution)/shard_map/ppermute | solution.py:774
  75.6 25.2 %all-to-all-start.2 = ((f32[64,1,128]{2,1,0:T(1,128)}), f32[64,1,128]{2,1,0:T(1,128)S(1)}, u32[]{:S(2)}, u32[]{:S(2)}) async-start(f32[64,1,128]{2,1,0:T(1,128)} %bitcast.4), calls=%async_computation.2 | async-start | bytes 65536 | tf_op jit(solution)/shard_map/all_to_all | solution.py:761

commit v7 on v5

--- a/solution.py
+++ b/solution.py
@@ -9,7 +9,6 @@
 from jax.sharding import PartitionSpec as P
 
 
-HIGHEST = lax.Precision.HIGHEST
 N_DOM = 64
 N_REC = 2048
 CAP = 1024
@@ -17,6 +16,7 @@
 BY_DOT = 3
 LANES = 128
 BLOCK = 512
+HALF = 256
 CHUNK = 104
 
 
@@ -27,6 +27,8 @@
 CROSS_1 = both_ways(range(1, N_DOM - 1, 2), 1)
 INNER_1 = both_ways(range(0, N_DOM - 1, 2), 1)
 CROSS_2 = both_ways([q for q in range(N_DOM - 2) if q % 4 >= 2], 2)
+MIDDLE_1 = both_ways([q for q in range(N_DOM - 1) if q % 4 == 1], 1)
+SHIFTED = [[(4 * g + 2 + t) % N_DOM for t in range(4)] for g in range(16)]
 INNER_2 = both_ways([q for q in range(N_DOM - 2) if q % 4 < 2], 2)
 
 
@@ -34,6 +36,21 @@
     odd = q % 2 == 1
     late = q % 4 >= 2
     return odd, jnp.logical_not(odd), late, jnp.logical_not(late)
+
+
+def pick_sides(q, inner_1, middle, inner_2, far):
+    r = q % 4
+    p = (q + 2) % 4
+
+    def across(off):
+        return far(jnp.clip(p + off, 0, 3))
+
+    return (
+        jnp.where(r < 2, across(-2), inner_2),
+        jnp.where(r == 0, across(-1), jnp.where(r == 2, middle, inner_1)),
+        jnp.where(r == 3, across(1), jnp.where(r == 1, middle, inner_1)),
+        jnp.where(r >= 2, across(2), inner_2),
+    )
 
 
 def legendre_pair(values, degree):
@@ -269,20 +286,25 @@
     for source, target in zip(refs[:half], refs[half:]):
         words = source[0:32, :]
         valid = jnp.where((iota((32, LANES), 0) % 4 == 3) & (words > 0.0), 1, 0)
-        blocks = (jnp.sum(valid) + BLOCK - 1) // BLOCK
-
-        def one_block(b, carry, source=source, target=target):
-            start = pl.multiple_of(b * BLOCK, BLOCK)
-            tiles = source[pl.ds(pl.multiple_of(b * 16, 16), 16), :]
-            words = jnp.concatenate([tiles[4 * n : 4 * n + 4, :] for n in range(4)], axis=1)
+        count = jnp.sum(valid)
+        blocks = (count + HALF - 1) // BLOCK
+        left = (count - blocks * BLOCK + BLOCK - 1) // BLOCK
+
+        def one_block(b, first, size, source=source, target=target):
+            start = pl.multiple_of(b * size + first, HALF)
+            rows = size // 32
+            tiles = source[pl.ds(pl.multiple_of(b * rows + first // 32, 8), rows), :]
+            words = jnp.concatenate(
+                [tiles[4 * n : 4 * n + 4, :] for n in range(rows // 4)], axis=1
+            )
             element = words[3:4, :].astype(jnp.int32) - 1
-            hot_rows = iota((LANES, BLOCK), 0)
+            hot_rows = iota((LANES, size), 0)
             hot = (hot_rows == element).astype(jnp.float32).astype(jnp.bfloat16)
             hot = jnp.concatenate([hot, hot], axis=0)
             element = jnp.maximum(element, 0)
             along = [basis_rows(words[d : d + 1, :]) for d in range(3)]
-            row = iota((8, BLOCK), 0)
-            wx = jnp.broadcast_to(along[0][0], (8, BLOCK))
+            row = iota((8, size), 0)
+            wx = jnp.broadcast_to(along[0][0], (8, size))
             for i in range(1, 8):
                 wx = jnp.where(row == i, along[0][i], wx)
 
@@ -306,7 +328,7 @@
                     over_j * wx[:, part], axis=0, keepdims=True
                 )
 
-            gathers = [(f, h) for f in range(BY_DOT, FIELDS) for h in range(BLOCK // LANES)]
+            gathers = [(f, h) for f in range(BY_DOT, FIELDS) for h in range(size // LANES)]
             for f in range(BY_DOT):
                 picked = lax.dot(fields_ref[f], hot, preferred_element_type=jnp.float32)
                 share = -(-len(gathers) // (BY_DOT - f))
@@ -319,22 +341,40 @@
                 over_j = over_k[0:8, :] * along[1][0]
                 for j in range(1, 8):
                     over_j = over_j + over_k[8 * j : 8 * j + 8, :] * along[1][j]
-                target[f : f + 1, pl.ds(start, BLOCK)] = jnp.sum(
+                target[f : f + 1, pl.ds(start, size)] = jnp.sum(
                     over_j * wx, axis=0, keepdims=True
                 )
+
+        def whole(b, carry, one_block=one_block):
+            one_block(b, 0, BLOCK)
             return carry
 
-        lax.fori_loop(0, blocks, one_block, 0)
+        def part(b, carry, one_block=one_block, first=blocks * BLOCK):
+            one_block(b, first, HALF)
+            return carry
+
+        lax.fori_loop(0, blocks, whole, 0)
+        lax.fori_loop(0, left, part, 0)
+
+
+def eval_far_kernel(place_ref, fields_ref, donors_ref, *refs):
+    *refs, far_ref = refs
+    eval_kernel(fields_ref, donors_ref, *refs)
+    cross_1_ref, cross_2_ref, _ = refs[3:]
+    r = place_ref[0] % 4
+    far_ref[...] = jnp.zeros(far_ref.shape, jnp.float32)
+    far_ref[r] = cross_2_ref[...]
+    far_ref[jnp.where(r % 2 == 0, r + 1, r - 1)] = cross_1_ref[...]
 
 
 def unpack_kernel(
-    place_ref, cross_1_ref, inner_1_ref, cross_2_ref, inner_2_ref, own_ref, moves_ref, owner_ref,
+    place_ref, inner_1_ref, middle_ref, inner_2_ref, far_ref, own_ref, moves_ref, owner_ref,
     out_ref,
 ):
     q = place_ref[0]
     width = N_REC
-    below_1, above_1, below_2, above_2 = by_side(
-        q, cross_1_ref[...], inner_1_ref[...], cross_2_ref[...], inner_2_ref[...]
+    below_2, below_1, above_1, above_2 = pick_sides(
+        q, inner_1_ref[...], middle_ref[...], inner_2_ref[...], lambda t: far_ref[t]
     )
     zeros = jnp.zeros((FIELDS, CAP), jnp.float32)
     values = [
@@ -358,13 +398,14 @@
 
 
 def share_kernel(
-    place_ref, cross_1_ref, inner_1_ref, cross_2_ref, inner_2_ref, own_ref, moves_ref, owner_ref,
+    place_ref, inner_1_ref, middle_ref, inner_2_ref, far_ref, own_ref, moves_ref, owner_ref,
     share_ref,
 ):
     q = place_ref[0]
     width = N_REC
-    below_1, above_1, below_2, above_2 = by_side(
-        q, *(ref[0:1, :] for ref in (cross_1_ref, inner_1_ref, cross_2_ref, inner_2_ref))
+    below_2, below_1, above_1, above_2 = pick_sides(
+        q, inner_1_ref[0:1, :], middle_ref[0:1, :], inner_2_ref[0:1, :],
+        lambda t: far_ref[t, 0:1, :],
     )
     row = iota((8, CAP), 0)
     values = jnp.broadcast_to(below_2, (8, CAP))
@@ -514,30 +555,35 @@
 ):
     q = place_ref[0]
     below, above = by_side(q, cross_in_ref[...], inner_in_ref[...])
-    pick_row = iota((8, LANES), 0)
-    pick_lane = iota((8, LANES), 1)
+    pick_row = iota((32, 2 * LANES), 0)
+    pick_lane = iota((32, 2 * LANES), 1)
+    odd = pick_lane // LANES
     picks = [
-        [
-            jnp.where(pick_lane == pick_row * 16 + (8 * odd + 7 * s), 1.0, 0.0)
-            for odd in range(2)
-        ]
+        jnp.where(
+            (pick_lane % LANES == pick_row % 8 * 16 + (8 * odd + 7 * s)) & (pick_row < 24), 1.0, 0.0
+        ).astype(jnp.bfloat16)
         for s in range(2)
     ]
+
+    def bf16_parts(value):
+        parts = []
+        for _ in range(3):
+            part = value.astype(jnp.bfloat16)
+            parts.append(part.astype(jnp.float32))
+            value = value - parts[-1]
+        return jnp.concatenate([*parts, jnp.zeros_like(value)], axis=0).astype(jnp.bfloat16)
 
     layers = (below, own_ref[...], above)
     received = {off: [] for off in range(-1, 2)}
     for s in range(2):
         values = jnp.concatenate([layer[8 * s : 8 * s + 8, :] for layer in layers], axis=1)
-        halves = [
-            lax.dot_general(
-                values, picks[s][odd], (((0,), (0,)), ((), ())),
-                precision=HIGHEST, preferred_element_type=jnp.float32,
-            )
-            for odd in range(2)
-        ]
+        spread = lax.dot_general(
+            bf16_parts(values), picks[s], (((0,), (0,)), ((), ())),
+            preferred_element_type=jnp.float32,
+        )
         for n in range(3):
             at = n * LANES
-            plane = halves[0][at : at + 64, :] + halves[1][at + 64 : at + 128, :]
+            plane = spread[at : at + 64, :LANES] + spread[at + 64 : at + 128, LANES:]
             received[n - 1].append([plane[8 * k : 8 * k + 8, :] for k in range(8)])
     lane = iota((8, LANES), 1)
     j_row = iota((8, LANES), 0)
@@ -724,6 +770,14 @@
     return [moved[n] for n in (0, 2, 1, 3) if moved[n] is not None]
 
 
+def to_four(inner_1, middle, inner_2, far):
+    far = lax.all_to_all(far, "dom", 0, 0, tiled=True, axis_index_groups=SHIFTED)
+    near = []
+    for value, pairs in ((inner_1, INNER_1), (middle, MIDDLE_1), (inner_2, INNER_2)):
+        near.append(lax.ppermute(value, "dom", pairs))
+    return (*near, far)
+
+
 def body(donor_fields, interp_weights, donor_owner, donor_element, geometry, wall_flag, forcing):
     place = lax.axis_index("dom").astype(jnp.int32).reshape(1)
     xmat = x_matrix()
@@ -753,11 +807,12 @@
         eval_kernel, (fields, donors, own, requests[1]), (answer,) * 2,
         flops=3_000_000_000, smem_first=False, mib=24,
     )
-    cross_1, cross_2, inner_2 = call(
-        eval_kernel, (fields, donors, requests[0], requests[2], requests[3]), (answer,) * 3,
-        flops=4_000_000_000, smem_first=False, mib=24,
-    )
-    answered = to_neighbours(cross_1, inner_1, cross_2, inner_2)
+    middle, _, inner_2, far = call(
+        eval_far_kernel, (place, fields, donors, requests[0], requests[2], requests[3]),
+        (answer, answer, answer, ((4, FIELDS, CAP), F32)),
+        flops=4_000_000_000, mib=24,
+    )
+    answered = to_four(inner_1, middle, inner_2, far)
     inverse, free, load, beside = call(
         prep_kernel, (place, geometry, wall_flag, forcing, requests[0], requests[1]),
         (FIELD, FIELD, FIELD, ((16, LANES), F32)),

time: 103 us -> 103 us (level)
    ppermute x16 -> x12, starting transfers between devices: 48.8 us -> 31.6 us  [to_neighbours(): moved.append(None if value is None else lax.ppermute(value, 'dom', pairs))]
    all_to_all x0 -> x1, starting transfers between devices: none -> 10.1 us  [to_four(): lax.all_to_all(far, 'dom', 0, 0, tiled=True, axis_index_groups=SHIFTED)]
    ppermute x0 -> x3, starting transfers between devices: none -> 6.14 us  [to_four(): near.append(lax.ppermute(value, 'dom', pairs))]
    ppermute x16 -> x12, waiting for transfers between devices: 8.79 us -> 6.72 us  [to_neighbours(): moved.append(None if value is None else lax.ppermute(value, 'dom', pairs))]
    ppermute x0 -> x3, waiting for transfers between devices: none -> 1.89 us  [to_four(): near.append(lax.ppermute(value, 'dom', pairs))]
    all_to_all x1, starting transfers between devices: 20.9 us -> 22 us  [to_all(): return lax.all_to_all(value, 'dom', 0, 0, tiled=True)]
  transfers between devices with their start and end apart: 18 -> 18, of which waited for: 6 -> 6; matrix products, arithmetic and copies ran while one was open for 0% -> 0% of each run, Pallas kernels for 8% -> 9%
where the time goes in v7:
time: 103 us; the launch traced here: 102 us
  starting transfers between devices  70 us (68%)
  waiting for transfers between devices  16.6 us (16%)
  Pallas kernels  15 us (15%)
    ppermute x12, starting transfers between devices, to_neighbours(): moved.append(None if value is None else lax.ppermute(value, 'dom', pairs))  31.6 us
    all_to_all x1, starting transfers between devices, to_all(): return lax.all_to_all(value, 'dom', 0, 0, tiled=True)  22 us
    pallas_call x12, Pallas kernels, call(): pl.pallas_call(kernel, out_shape=out_shape, in_specs=specs, out_specs=[VM...  15 us
    all_to_all x1, starting transfers between devices, to_four(): lax.all_to_all(far, 'dom', 0, 0, tiled=True, axis_index_groups=SHIFTED)  10.1 us
    all_to_all x1, waiting for transfers between devices, to_all(): return lax.all_to_all(value, 'dom', 0, 0, tiled=True)  7.96 us
    ppermute x12, waiting for transfers between devices, to_neighbours(): moved.append(None if value is None else lax.ppermute(value, 'dom', pairs))  6.72 us
    ppermute x3, starting transfers between devices, to_four(): near.append(lax.ppermute(value, 'dom', pairs))  6.14 us
  transfers between devices with their start and end apart: 18, of which 6 were waited for; matrix products, arithmetic and copies ran while one was open for 0% of the time, Pallas kernels for 9%

profile of v7, /device:TPU:0, one launch (start us, length us, event | category | flops | bytes accessed | tf_op | source)
XLA Modules:
  0.0 102.4 jit_solution(12262539880037196151)
XLA Ops:
  0.7 2.4 %shard_map.104 = (f32[104,128]{1,0:T(8,128)S(1)}, f32[104,128]{1,0:T(8,128)S(1)}, f32[32,128]{1,0:T(8,128)S(1)}, f32[32,128]{1,0:T(8,128)S(1)}, f32[32,128]{1,0:T(8,128)S(1)}, /*index=5*/s32[8,1024]{1,0:T(8,128)S(1)}) custom-call(s32[1]{0:T(128)} %bitcast.place_ref, f32[3,8,2048]{2,1,0:T(8,128)} %weights_ref.1, s32[1,2048]{1,0:T(1,128)} %bitcast.8, ...), custom_call_target="tpu_custom_call" | custom-call | flops 100000 | bytes 1000000 | tf_op jit(solution)/shard_map/pallas_call | solution.py:746
  3.1 0.7 collective-permute-start.3
  4.4 10.1 %collective-permute-start.5 = (f32[32,128]{1,0:T(8,128)S(1)}, f32[32,128]{1,0:T(8,128)S(1)}, u32[]{:S(2)}, u32[]{:S(2)}) collective-permute-start(f32[32,128]{1,0:T(8,128)S(1)} %get-tuple-element.43), channel_id=1, source_target_pairs={{0,2},{2,0},{1,3},{3,1},{4,6},{6,4},{5,7},{7,5},{8,10},{10,8},{9,1... | collective-permute-start | bytes 49160 | tf_op jit(solution)/shard_map/ppermute | solution.py:769
  14.9 1.5 %collective-permute-done.5.refs_2_ = f32[32,128]{1,0:T(8,128)S(1)} collective-permute-done((f32[32,128]{1,0:T(8,128)S(1)}, f32[32,128]{1,0:T(8,128)S(1)}, u32[]{:S(2)}, u32[]{:S(2)}) %collective-permute-start.5) | collective-permute-done | bytes 16416 | tf_op jit(solution)/shard_map/ppermute | solution.py:769
  16.5 1.8 %shard_map.106 = (f32[5,1024]{1,0:T(8,128)S(1)}, f32[5,1024]{1,0:T(8,128)}, f32[5,1024]{1,0:T(8,128)S(1)}, f32[4,5,1024]{2,1,0:T(8,128)}) custom-call(s32[1]{0:T(128)} %bitcast.place_ref, bf16[3,512,256]{2,1,0:T(8,128)(2,1)S(1)} %shard_map.103.refs_0_.fields_ref, f32[5,512,128]{2,1,0:T(8,128)S(1)} %collective-permute-done.fields_ref.refs_1_.donors_ref, ...), custom_call_target="tpu_custom_call" | custom-call | flops 4000000000 | bytes 1000000 | tf_op jit(solution)/shard_map/pallas_call | solution.py:746
  18.3 10.1 %all-to-all-start = ((f32[4,5,1024]{2,1,0:T(8,128)}), f32[4,5,1024]{2,1,0:T(8,128)S(1)}, u32[]{:S(2)}, u32[]{:S(2)}) async-start(f32[4,5,1024]{2,1,0:T(8,128)} %get-tuple-element.46), calls=%async_computation | async-start | bytes 262144 | tf_op jit(solution)/shard_map/all_to_all | solution.py:774
  28.5 2.5 %shard_map.105 = (f32[5,1024]{1,0:T(8,128)S(1)}, f32[5,1024]{1,0:T(8,128)S(1)}) custom-call(bf16[3,512,256]{2,1,0:T(8,128)(2,1)S(1)} %shard_map.103.refs_0_.fields_ref, f32[5,512,128]{2,1,0:T(8,128)S(1)} %collective-permute-done.fields_ref.refs_1_.donors_ref, f32[32,128]{1,0:T(8,128)S(1)} %get-tuple-element.38.refs_2_, ...), custom_call_target="tpu_custom_call" | custom-call | flops 3000000000 | bytes 1000000 | tf_op jit(solution)/shard_map/pallas_call | solution.py:746
  31.7 5.4 %collective-permute-start.7 = (f32[5,1024]{1,0:T(8,128)S(1)}, f32[5,1024]{1,0:T(8,128)S(1)}, u32[]{:S(2)}, u32[]{:S(2)}) collective-permute-start(f32[5,1024]{1,0:T(8,128)S(1)} %get-tuple-element.45), channel_id=1, source_target_pairs={{0,2},{2,0},{1,3},{3,1},{4,6},{6,4},{5,7},{7,5},{8,10},{10,8},{9,1... | collective-permute-start | bytes 61448 | tf_op jit(solution)/shard_map/ppermute | solution.py:777
  37.1 1.9 %collective-permute-done.7.inner_2_ref = f32[5,1024]{1,0:T(8,128)S(1)} collective-permute-done((f32[5,1024]{1,0:T(8,128)S(1)}, f32[5,1024]{1,0:T(8,128)S(1)}, u32[]{:S(2)}, u32[]{:S(2)}) %collective-permute-start.7) | collective-permute-done | bytes 20512 | tf_op jit(solution)/shard_map/ppermute | solution.py:777
  40.3 4.8 %collective-permute-start.9 = (f32[16,128]{1,0:T(8,128)S(1)}, f32[16,128]{1,0:T(8,128)S(1)}, u32[]{:S(2)}, u32[]{:S(2)}) collective-permute-start(f32[16,128]{1,0:T(8,128)S(1)} %shard_map.107.own_ref), channel_id=1, source_target_pairs={{0,1},{1,0},{2,3},{3,2},{4,5},{5,4},{6,7},{7,6},{8,9},{9,8},{10,11... | collective-permute-start | bytes 24584 | tf_op jit(solution)/shard_map/ppermute | solution.py:769
  45.1 0.9 shard_map.108
  46.1 0.7 collective-permute-done.9.inner_in_ref
  46.8 1.6 %shard_map.109 = (f32[512,128]{1,0:T(8,128)S(1)}, f32[512,128]{1,0:T(8,128)S(1)}, f32[128,128]{1,0:T(8,128)S(1)}, f32[128,128]{1,0:T(8,128)S(1)}, f32[1,128]{1,0...) custom-call(s32[1]{0:T(128)} %bitcast.place_ref, f32[16,128]{1,0:T(8,128)S(1)} %shard_map.107.own_ref, ...), custom_call_target="tpu_custom_call" | custom-call | flops 100000 | bytes 1000000 | tf_op jit(solution)/shard_map/pallas_call | solution.py:746
  48.4 0.7 collective-permute-start.10
  49.1 3.5 %collective-permute-start.11 = (f32[128,128]{1,0:T(8,128)S(1)}, f32[128,128]{1,0:T(8,128)S(1)}, u32[]{:S(2)}, u32[]{:S(2)}) collective-permute-start(f32[128,128]{1,0:T(8,128)S(1)} %get-tuple-element.56), channel_id=1, source_target_pairs={{0,1},{1,0},{2,3},{3,2},{4,5},{5,4},{6,7},{7,6},{8,9},{9,8},{10,11... | collective-permute-start | bytes 196616 | tf_op jit(solution)/shard_map/ppermute | solution.py:769
  52.6 2.2 %collective-permute-done.11.inner_in_ref = f32[128,128]{1,0:T(8,128)S(1)} collective-permute-done((f32[128,128]{1,0:T(8,128)S(1)}, f32[128,128]{1,0:T(8,128)S(1)}, u32[]{:S(2)}, u32[]{:S(2)}) %collective-permute-start.11) | collective-permute-done | bytes 65568 | tf_op jit(solution)/shard_map/ppermute | solution.py:769
  56.1 5.4 %collective-permute-start.13 = (f32[64,128]{1,0:T(8,128)S(1)}, f32[64,128]{1,0:T(8,128)S(1)}, u32[]{:S(2)}, u32[]{:S(2)}) collective-permute-start(f32[64,128]{1,0:T(8,128)S(1)} %get-tuple-element.63), channel_id=1, source_target_pairs={{0,1},{1,0},{2,3},{3,2},{4,5},{5,4},{6,7},{7,6},{8,9},{9,8},{10,11... | collective-permute-start | bytes 98312 | tf_op jit(solution)/shard_map/ppermute | solution.py:769
  61.5 2.2 %collective-permute-done.13.inner_in_ref = f32[64,128]{1,0:T(8,128)S(1)} collective-permute-done((f32[64,128]{1,0:T(8,128)S(1)}, f32[64,128]{1,0:T(8,128)S(1)}, u32[]{:S(2)}, u32[]{:S(2)}) %collective-permute-start.13) | collective-permute-done | bytes 32800 | tf_op jit(solution)/shard_map/ppermute | solution.py:769
  63.7 1.2 %shard_map.111 = (f32[512,128]{1,0:T(8,128)S(1)}, f32[512,128]{1,0:T(8,128)S(1)}, f32[64,128]{1,0:T(8,128)}, f32[64,128]{1,0:T(8,128)S(1)}, f32[64,128]{1,0:T(8,128)S(1)}) custom-call(s32[1]{0:T(128)} %bitcast.place_ref, f32[512,128]{1,0:T(8,128)S(1)} %get-tuple-element.60.w_old_ref.w1_ref, f32[512,128]{1,0:T(8,128)S(1)} %get-tuple-element.61.u_old_ref, ...), custom_call_target="tpu_custom_call" | custom-call | flops 100000 | bytes 1000000 | tf_op jit(solution)/shard_map/pallas_call | solution.py:746
  65.6 3.7 %collective-permute-start.15 = (f32[64,128]{1,0:T(8,128)S(1)}, f32[64,128]{1,0:T(8,128)S(1)}, u32[]{:S(2)}, u32[]{:S(2)}) collective-permute-start(f32[64,128]{1,0:T(8,128)S(1)} %get-tuple-element.68), channel_id=1, source_target_pairs={{0,1},{1,0},{2,3},{3,2},{4,5},{5,4},{6,7},{7,6},{8,9},{9,8},{10,11... | collective-permute-start | bytes 98312 | tf_op jit(solution)/shard_map/ppermute | solution.py:769
  69.3 22.0 %all-to-all-start.1 = ((f32[64,1,128]{2,1,0:T(1,128)}), f32[64,1,128]{2,1,0:T(1,128)S(1)}, u32[]{:S(2)}, u32[]{:S(2)}) async-start(f32[64,1,128]{2,1,0:T(1,128)} %bitcast.4), calls=%async_computation.1 | async-start | bytes 65536 | tf_op jit(solution)/shard_map/all_to_all | solution.py:762
  91.3 1.5 %shard_map.114 = f32[5,2048]{1,0:T(8,128)} custom-call(s32[1]{0:T(128)} %bitcast.place_ref, f32[5,1024]{1,0:T(8,128)S(1)} %collective-permute-done.2.inner_1_ref, f32[5,1024]{1,0:T(8,128)S(1)} %collective-permute-done.6.middle_ref, f32[5,1024]{1,0:T(8,128)S(1)} %collective-permute-done.7.inner_2_ref, f32[4,5,1024]{2,1,0:T(8,128)S(1)} %all-to-all-done.far_ref, ...), custom_call_target="tpu_custom_call" | custom-call | flops 100000 | bytes 1000000 | tf_op jit(solution)/shard_map/pallas_call | solution.py:746
  92.8 8.0 %all-to-all-done.1 = f32[64,1,128]{2,1,0:T(1,128)S(1)} async-done(((f32[64,1,128]{2,1,0:T(1,128)}), f32[64,1,128]{2,1,0:T(1,128)S(1)}, u32[]{:S(2)}, u32[]{:S(2)}) %all-to-all-start.1) | async-done | bytes 32800 | tf_op jit(solution)/shard_map/all_to_all | solution.py:762
  100.8 1.6 %shard_map.113 = (f32[512,128]{1,0:T(8,128)}, f32[512,128]{1,0:T(8,128)}) custom-call(f32[512,128]{1,0:T(8,128)S(1)} %get-tuple-element.53.w_old_ref.w0_ref, f32[128,128]{1,0:T(8,128)S(1)} %get-tuple-element.59.face_ref, f32[512,128]{1,0:T(8,128)S(1)} %get-tuple-element.60.w_old_ref.w1_ref, f32[512,128]{1,0:T(8,128)S(1)} %get-tuple-element.65.w2_ref, ...), custom_call_target="tpu_custom_call" | custom-call | flops 100000 | bytes 1000000 | tf_op jit(solution)/shard_map/pallas_call | solution.py:746
  (34 shorter events, 5.1 us)
Async XLA Ops:
  0.6 14.1 %collective-permute-start = (f32[5,512,128]{2,1,0:T(8,128)}, f32[5,512,128]{2,1,0:T(8,128)S(1)}, u32[]{:S(2)}, u32[]{:S(2)}) collective-permute-start(f32[5,512,128]{2,1,0:T(8,128)} %param.8), channel_id=1, source_target_pairs={{0,64},{64,0},{1,65},{65,1},{2,66},{66,2},{3,67},{67,3},{4,68},{68... | collective-permute-start | bytes 3932168 | tf_op jit(solution)/shard_map/ppermute | solution.py:784
  3.1 13.4 %collective-permute-start.3 = (f32[104,128]{1,0:T(8,128)S(1)}, f32[104,128]{1,0:T(8,128)S(1)}, u32[]{:S(2)}, u32[]{:S(2)}) collective-permute-start(f32[104,128]{1,0:T(8,128)S(1)} %get-tuple-element.41), channel_id=1, source_target_pairs={{1,2},{2,1},{3,4},{4,3},{5,6},{6,5},{7,8},{8,7},{9,10},{10,9},{11,... | collective-permute-start | bytes 159752 | tf_op jit(solution)/shard_map/ppermute | solution.py:769
  3.8 11.1 %collective-permute-start.4 = (f32[32,128]{1,0:T(8,128)S(1)}, f32[32,128]{1,0:T(8,128)S(1)}, u32[]{:S(2)}, u32[]{:S(2)}) collective-permute-start(f32[32,128]{1,0:T(8,128)S(1)} %get-tuple-element.42), channel_id=1, source_target_pairs={{2,4},{4,2},{3,5},{5,3},{6,8},{8,6},{7,9},{9,7},{10,12},{12,10},{1... | collective-permute-start | bytes 49160 | tf_op jit(solution)/shard_map/ppermute | solution.py:769
  4.4 12.0 %collective-permute-start.5 = (f32[32,128]{1,0:T(8,128)S(1)}, f32[32,128]{1,0:T(8,128)S(1)}, u32[]{:S(2)}, u32[]{:S(2)}) collective-permute-start(f32[32,128]{1,0:T(8,128)S(1)} %get-tuple-element.43), channel_id=1, source_target_pairs={{0,2},{2,0},{1,3},{3,1},{4,6},{6,4},{5,7},{7,5},{8,10},{10,8},{9,1... | collective-permute-start | bytes 49160 | tf_op jit(solution)/shard_map/ppermute | solution.py:769
  14.6 13.9 %collective-permute-start.1 = (f32[104,128]{1,0:T(8,128)S(1)}, f32[104,128]{1,0:T(8,128)S(1)}, u32[]{:S(2)}, u32[]{:S(2)}) collective-permute-start(f32[104,128]{1,0:T(8,128)S(1)} %get-tuple-element.39), channel_id=1, source_target_pairs={{0,1},{1,0},{2,3},{3,2},{4,5},{5,4},{6,7},{7,6},{8,9},{9,8},{10,11... | collective-permute-start | bytes 159752 | tf_op jit(solution)/shard_map/ppermute | solution.py:769
  18.3 20.7 %all-to-all-start = ((f32[4,5,1024]{2,1,0:T(8,128)}), f32[4,5,1024]{2,1,0:T(8,128)S(1)}, u32[]{:S(2)}, u32[]{:S(2)}) async-start(f32[4,5,1024]{2,1,0:T(8,128)} %get-tuple-element.46), calls=%async_computation | async-start | bytes 262144 | tf_op jit(solution)/shard_map/all_to_all | solution.py:774
  28.4 10.6 %copy-start.2 = (s32[2048,1]{0,1:T(1,128)S(1)}, s32[2048,1]{0,1:T(1,128)}, u32[]{:S(2)}) copy-start(s32[2048,1]{0,1:T(1,128)} %param.10) | copy-start | bytes 24580
  28.4 16.7 %copy-start = (f32[512,128]{1,0:T(8,128)S(1)}, f32[512,128]{1,0:T(8,128)}, u32[]{:S(2)}) copy-start(f32[512,128]{1,0:T(8,128)} %forcing_ref.3) | copy-start | bytes 786436
  28.5 16.7 %copy-start.3 = (f32[4,128]{1,0:T(4,128)S(1)}, f32[4,128]{1,0:T(4,128)}, u32[]{:S(2)}) copy-start(f32[4,128]{1,0:T(4,128)} %geometry_ref.9) | copy-start | bytes 6148
  28.5 16.7 %copy-start.4 = (s32[2,8]{1,0:T(2,128)S(1)}, s32[2,8]{1,0:T(2,128)}, u32[]{:S(2)}) copy-start(s32[2,8]{1,0:T(2,128)} %wall_ref.3) | copy-start | bytes 196
  28.5 18.3 %copy-start.1 = (bf16[64,192]{1,0:T(8,128)(2,1)S(1)}, bf16[64,192]{1,0:T(8,128)(2,1)}, u32[]{:S(2)}) copy-start(bf16[64,192]{1,0:T(8,128)(2,1)} %constant.12.xmat_ref) | copy-start | bytes 73732
  31.0 6.2 %collective-permute-start.2 = (f32[5,1024]{1,0:T(8,128)S(1)}, f32[5,1024]{1,0:T(8,128)S(1)}, u32[]{:S(2)}, u32[]{:S(2)}) collective-permute-start(f32[5,1024]{1,0:T(8,128)S(1)} %get-tuple-element.40), channel_id=1, source_target_pairs={{0,1},{1,0},{2,3},{3,2},{4,5},{5,4},{6,7},{7,6},{8,9},{9,8},{10,11... | collective-permute-start | bytes 61448 | tf_op jit(solution)/shard_map/ppermute | solution.py:777
  31.1 6.1 %collective-permute-start.6 = (f32[5,1024]{1,0:T(8,128)S(1)}, f32[5,1024]{1,0:T(8,128)S(1)}, u32[]{:S(2)}, u32[]{:S(2)}) collective-permute-start(f32[5,1024]{1,0:T(8,128)S(1)} %get-tuple-element.44), channel_id=1, source_target_pairs={{1,2},{2,1},{5,6},{6,5},{9,10},{10,9},{13,14},{14,13},{17,18},{18,... | collective-permute-start | bytes 61448 | tf_op jit(solution)/shard_map/ppermute | solution.py:777
  31.7 7.3 %collective-permute-start.7 = (f32[5,1024]{1,0:T(8,128)S(1)}, f32[5,1024]{1,0:T(8,128)S(1)}, u32[]{:S(2)}, u32[]{:S(2)}) collective-permute-start(f32[5,1024]{1,0:T(8,128)S(1)} %get-tuple-element.45), channel_id=1, source_target_pairs={{0,2},{2,0},{1,3},{3,1},{4,6},{6,4},{5,7},{7,5},{8,10},{10,8},{9,1... | collective-permute-start | bytes 61448 | tf_op jit(solution)/shard_map/ppermute | solution.py:777
  39.7 6.4 %collective-permute-start.8 = (f32[16,128]{1,0:T(8,128)S(1)}, f32[16,128]{1,0:T(8,128)S(1)}, u32[]{:S(2)}, u32[]{:S(2)}) collective-permute-start(f32[16,128]{1,0:T(8,128)S(1)} %shard_map.107.own_ref), channel_id=1, source_target_pairs={{1,2},{2,1},{3,4},{4,3},{5,6},{6,5},{7,8},{8,7},{9,10},{10,9},{11,... | collective-permute-start | bytes 24584 | tf_op jit(solution)/shard_map/ppermute | solution.py:769
  40.3 6.4 %collective-permute-start.9 = (f32[16,128]{1,0:T(8,128)S(1)}, f32[16,128]{1,0:T(8,128)S(1)}, u32[]{:S(2)}, u32[]{:S(2)}) collective-permute-start(f32[16,128]{1,0:T(8,128)S(1)} %shard_map.107.own_ref), channel_id=1, source_target_pairs={{0,1},{1,0},{2,3},{3,2},{4,5},{5,4},{6,7},{7,6},{8,9},{9,8},{10,11... | collective-permute-start | bytes 24584 | tf_op jit(solution)/shard_map/ppermute | solution.py:769
  48.4 4.2 %collective-permute-start.10 = (f32[128,128]{1,0:T(8,128)S(1)}, f32[128,128]{1,0:T(8,128)S(1)}, u32[]{:S(2)}, u32[]{:S(2)}) collective-permute-start(f32[128,128]{1,0:T(8,128)S(1)} %get-tuple-element.55), channel_id=1, source_target_pairs={{1,2},{2,1},{3,4},{4,3},{5,6},{6,5},{7,8},{8,7},{9,10},{10,9},{11,... | collective-permute-start | bytes 196616 | tf_op jit(solution)/shard_map/ppermute | solution.py:769
  49.1 5.8 %collective-permute-start.11 = (f32[128,128]{1,0:T(8,128)S(1)}, f32[128,128]{1,0:T(8,128)S(1)}, u32[]{:S(2)}, u32[]{:S(2)}) collective-permute-start(f32[128,128]{1,0:T(8,128)S(1)} %get-tuple-element.56), channel_id=1, source_target_pairs={{0,1},{1,0},{2,3},{3,2},{4,5},{5,4},{6,7},{7,6},{8,9},{9,8},{10,11... | collective-permute-start | bytes 196616 | tf_op jit(solution)/shard_map/ppermute | solution.py:769
  55.5 6.0 %collective-permute-start.12 = (f32[64,128]{1,0:T(8,128)S(1)}, f32[64,128]{1,0:T(8,128)S(1)}, u32[]{:S(2)}, u32[]{:S(2)}) collective-permute-start(f32[64,128]{1,0:T(8,128)S(1)} %get-tuple-element.62), channel_id=1, source_target_pairs={{1,2},{2,1},{3,4},{4,3},{5,6},{6,5},{7,8},{8,7},{9,10},{10,9},{11,... | collective-permute-start | bytes 98312 | tf_op jit(solution)/shard_map/ppermute | solution.py:769
  56.1 7.6 %collective-permute-start.13 = (f32[64,128]{1,0:T(8,128)S(1)}, f32[64,128]{1,0:T(8,128)S(1)}, u32[]{:S(2)}, u32[]{:S(2)}) collective-permute-start(f32[64,128]{1,0:T(8,128)S(1)} %get-tuple-element.63), channel_id=1, source_target_pairs={{0,1},{1,0},{2,3},{3,2},{4,5},{5,4},{6,7},{7,6},{8,9},{9,8},{10,11... | collective-permute-start | bytes 98312 | tf_op jit(solution)/shard_map/ppermute | solution.py:769
  65.0 27.8 %collective-permute-start.14 = (f32[64,128]{1,0:T(8,128)S(1)}, f32[64,128]{1,0:T(8,128)S(1)}, u32[]{:S(2)}, u32[]{:S(2)}) collective-permute-start(f32[64,128]{1,0:T(8,128)S(1)} %get-tuple-element.67), channel_id=1, source_target_pairs={{1,2},{2,1},{3,4},{4,3},{5,6},{6,5},{7,8},{8,7},{9,10},{10,9},{11,... | collective-permute-start | bytes 98312 | tf_op jit(solution)/shard_map/ppermute | solution.py:769
  65.6 27.2 %collective-permute-start.15 = (f32[64,128]{1,0:T(8,128)S(1)}, f32[64,128]{1,0:T(8,128)S(1)}, u32[]{:S(2)}, u32[]{:S(2)}) collective-permute-start(f32[64,128]{1,0:T(8,128)S(1)} %get-tuple-element.68), channel_id=1, source_target_pairs={{0,1},{1,0},{2,3},{3,2},{4,5},{5,4},{6,7},{7,6},{8,9},{9,8},{10,11... | collective-permute-start | bytes 98312 | tf_op jit(solution)/shard_map/ppermute | solution.py:769
  69.3 31.5 %all-to-all-start.1 = ((f32[64,1,128]{2,1,0:T(1,128)}), f32[64,1,128]{2,1,0:T(1,128)S(1)}, u32[]{:S(2)}, u32[]{:S(2)}) async-start(f32[64,1,128]{2,1,0:T(1,128)} %bitcast.4), calls=%async_computation.1 | async-start | bytes 65536 | tf_op jit(solution)/shard_map/all_to_all | solution.py:762

commit v8 on v7

--- a/solution.py
+++ b/solution.py
@@ -360,7 +360,7 @@
 def eval_far_kernel(place_ref, fields_ref, donors_ref, *refs):
     *refs, far_ref = refs
     eval_kernel(fields_ref, donors_ref, *refs)
-    cross_1_ref, cross_2_ref, _ = refs[3:]
+    cross_1_ref, cross_2_ref = refs[2:]
     r = place_ref[0] % 4
     far_ref[...] = jnp.zeros(far_ref.shape, jnp.float32)
     far_ref[r] = cross_2_ref[...]
@@ -807,10 +807,14 @@
         eval_kernel, (fields, donors, own, requests[1]), (answer,) * 2,
         flops=3_000_000_000, smem_first=False, mib=24,
     )
-    middle, _, inner_2, far = call(
-        eval_far_kernel, (place, fields, donors, requests[0], requests[2], requests[3]),
-        (answer, answer, answer, ((4, FIELDS, CAP), F32)),
-        flops=4_000_000_000, mib=24,
+    middle, _, far = call(
+        eval_far_kernel, (place, fields, donors, requests[0], requests[2]),
+        (answer, answer, ((4, FIELDS, CAP), F32)),
+        flops=3_000_000_000, mib=24,
+    )
+    (inner_2,) = call(
+        eval_kernel, (fields, donors, requests[3]), (answer,),
+        flops=1_000_000_000, smem_first=False, mib=24,
     )
     answered = to_four(inner_1, middle, inner_2, far)
     inverse, free, load, beside = call(

time: 103 us -> 103 us (level)
  waiting for transfers between devices: 16.6 us -> 18.2 us
  starting transfers between devices: 70 us -> 68.5 us
    ppermute x3, starting transfers between devices: 6.14 us -> 1.52 us  [to_four(): near.append(lax.ppermute(value, 'dom', pairs))]
    ppermute x3, waiting for transfers between devices: 1.89 us -> 5.39 us  [to_four(): near.append(lax.ppermute(value, 'dom', pairs))]
    all_to_all x1, starting transfers between devices: 10.1 us -> 12.8 us  [to_four(): lax.all_to_all(far, 'dom', 0, 0, tiled=True, axis_index_groups=SHIFTED)]
    ppermute x12, waiting for transfers between devices: 6.72 us -> 4.89 us  [to_neighbours(): moved.append(None if value is None else lax.ppermute(value, 'dom', pairs))]
    pallas_call x12 -> x13, Pallas kernels: 15 us -> 15 us  [call(): pl.pallas_call(kernel, out_shape=out_shape, in_specs=specs, out_specs=[VM...]
  transfers between devices with their start and end apart: 18 -> 18, of which waited for: 6 -> 5; matrix products, arithmetic and copies ran while one was open for 0% -> 0% of each run, Pallas kernels for 9% -> 9%
where the time goes in v8:
time: 103 us
  starting transfers between devices  68.5 us (67%)
  waiting for transfers between devices  18.2 us (18%)
  Pallas kernels  15 us (15%)
    ppermute x12, starting transfers between devices, to_neighbours(): moved.append(None if value is None else lax.ppermute(value, 'dom', pairs))  31.8 us
    all_to_all x1, starting transfers between devices, to_all(): return lax.all_to_all(value, 'dom', 0, 0, tiled=True)  22.4 us
    pallas_call x13, Pallas kernels, call(): pl.pallas_call(kernel, out_shape=out_shape, in_specs=specs, out_specs=[VM...  15 us
    all_to_all x1, starting transfers between devices, to_four(): lax.all_to_all(far, 'dom', 0, 0, tiled=True, axis_index_groups=SHIFTED)  12.8 us
    all_to_all x1, waiting for transfers between devices, to_all(): return lax.all_to_all(value, 'dom', 0, 0, tiled=True)  7.96 us
    ppermute x3, waiting for transfers between devices, to_four(): near.append(lax.ppermute(value, 'dom', pairs))  5.39 us
    ppermute x12, waiting for transfers between devices, to_neighbours(): moved.append(None if value is None else lax.ppermute(value, 'dom', pairs))  4.89 us
  transfers between devices with their start and end apart: 18, of which 5 were waited for; matrix products, arithmetic and copies ran while one was open for 0% of the time, Pallas kernels for 9%

profile of v8, /device:TPU:0, one launch (start us, length us, event | category | flops | bytes accessed | tf_op | source)
XLA Modules:
  0.0 102.7 jit_solution(6002241515273880424)
XLA Ops:
  0.7 2.4 %shard_map.104 = (f32[104,128]{1,0:T(8,128)S(1)}, f32[104,128]{1,0:T(8,128)S(1)}, f32[32,128]{1,0:T(8,128)S(1)}, f32[32,128]{1,0:T(8,128)S(1)}, f32[32,128]{1,0:T(8,128)S(1)}, /*index=5*/s32[8,1024]{1,0:T(8,128)S(1)}) custom-call(s32[1]{0:T(128)} %bitcast.place_ref, f32[3,8,2048]{2,1,0:T(8,128)} %weights_ref.1, s32[1,2048]{1,0:T(1,128)} %bitcast.8, ...), custom_call_target="tpu_custom_call" | custom-call | flops 100000 | bytes 1000000 | tf_op jit(solution)/shard_map/pallas_call | solution.py:746
  3.1 1.8 %collective-permute-start.1 = (f32[104,128]{1,0:T(8,128)S(1)}, f32[104,128]{1,0:T(8,128)S(1)}, u32[]{:S(2)}, u32[]{:S(2)}) collective-permute-start(f32[104,128]{1,0:T(8,128)S(1)} %get-tuple-element.38), channel_id=1, source_target_pairs={{0,1},{1,0},{2,3},{3,2},{4,5},{5,4},{6,7},{7,6},{8,9},{9,8},{10,11... | collective-permute-start | bytes 159752 | tf_op jit(solution)/shard_map/ppermute | solution.py:769
  6.2 9.2 %collective-permute-start.6 = (f32[32,128]{1,0:T(8,128)S(1)}, f32[32,128]{1,0:T(8,128)S(1)}, u32[]{:S(2)}, u32[]{:S(2)}) collective-permute-start(f32[32,128]{1,0:T(8,128)S(1)} %get-tuple-element.43), channel_id=1, source_target_pairs={{0,2},{2,0},{1,3},{3,1},{4,6},{6,4},{5,7},{7,5},{8,10},{10,8},{9,1... | collective-permute-start | bytes 49160 | tf_op jit(solution)/shard_map/ppermute | solution.py:769
  15.6 2.5 %shard_map.105 = (f32[5,1024]{1,0:T(8,128)S(1)}, f32[5,1024]{1,0:T(8,128)S(1)}) custom-call(bf16[3,512,256]{2,1,0:T(8,128)(2,1)S(1)} %shard_map.103.refs_0_.fields_ref, f32[5,512,128]{2,1,0:T(8,128)S(1)} %collective-permute-done.fields_ref.refs_1_.donors_ref, f32[32,128]{1,0:T(8,128)S(1)} %get-tuple-element.37.refs_2_, ...), custom_call_target="tpu_custom_call" | custom-call | flops 3000000000 | bytes 1000000 | tf_op jit(solution)/shard_map/pallas_call | solution.py:746
  18.1 0.8 collective-permute-start.2
  18.8 1.0 shard_map.106
  20.5 12.8 %all-to-all-start = ((f32[4,5,1024]{2,1,0:T(8,128)}), f32[4,5,1024]{2,1,0:T(8,128)S(1)}, u32[]{:S(2)}, u32[]{:S(2)}) async-start(f32[4,5,1024]{2,1,0:T(8,128)} %get-tuple-element.44), calls=%async_computation | async-start | bytes 262144 | tf_op jit(solution)/shard_map/all_to_all | solution.py:774
  33.3 0.9 shard_map.107
  34.3 5.4 %collective-permute-done.7.inner_2_ref = f32[5,1024]{1,0:T(8,128)S(1)} collective-permute-done((f32[5,1024]{1,0:T(8,128)S(1)}, f32[5,1024]{1,0:T(8,128)S(1)}, u32[]{:S(2)}, u32[]{:S(2)}) %collective-permute-start.7) | collective-permute-done | bytes 20512 | tf_op jit(solution)/shard_map/ppermute | solution.py:777
  41.0 2.0 %collective-permute-start.9 = (f32[16,128]{1,0:T(8,128)S(1)}, f32[16,128]{1,0:T(8,128)S(1)}, u32[]{:S(2)}, u32[]{:S(2)}) collective-permute-start(f32[16,128]{1,0:T(8,128)S(1)} %shard_map.108.own_ref), channel_id=1, source_target_pairs={{0,1},{1,0},{2,3},{3,2},{4,5},{5,4},{6,7},{7,6},{8,9},{9,8},{10,11... | collective-permute-start | bytes 24584 | tf_op jit(solution)/shard_map/ppermute | solution.py:769
  43.0 0.9 shard_map.109
  44.0 0.7 collective-permute-done.9.inner_in_ref
  44.7 1.6 %shard_map.110 = (f32[512,128]{1,0:T(8,128)S(1)}, f32[512,128]{1,0:T(8,128)S(1)}, f32[128,128]{1,0:T(8,128)S(1)}, f32[128,128]{1,0:T(8,128)S(1)}, f32[1,128]{1,0...) custom-call(s32[1]{0:T(128)} %bitcast.place_ref, f32[16,128]{1,0:T(8,128)S(1)} %shard_map.108.own_ref, ...), custom_call_target="tpu_custom_call" | custom-call | flops 100000 | bytes 1000000 | tf_op jit(solution)/shard_map/pallas_call | solution.py:746
  46.3 0.7 collective-permute-start.10
  47.0 5.5 %collective-permute-start.11 = (f32[128,128]{1,0:T(8,128)S(1)}, f32[128,128]{1,0:T(8,128)S(1)}, u32[]{:S(2)}, u32[]{:S(2)}) collective-permute-start(f32[128,128]{1,0:T(8,128)S(1)} %get-tuple-element.54), channel_id=1, source_target_pairs={{0,1},{1,0},{2,3},{3,2},{4,5},{5,4},{6,7},{7,6},{8,9},{9,8},{10,11... | collective-permute-start | bytes 196616 | tf_op jit(solution)/shard_map/ppermute | solution.py:769
  52.5 2.2 %collective-permute-done.11.inner_in_ref = f32[128,128]{1,0:T(8,128)S(1)} collective-permute-done((f32[128,128]{1,0:T(8,128)S(1)}, f32[128,128]{1,0:T(8,128)S(1)}, u32[]{:S(2)}, u32[]{:S(2)}) %collective-permute-start.11) | collective-permute-done | bytes 65568 | tf_op jit(solution)/shard_map/ppermute | solution.py:769
  56.0 4.0 %collective-permute-start.13 = (f32[64,128]{1,0:T(8,128)S(1)}, f32[64,128]{1,0:T(8,128)S(1)}, u32[]{:S(2)}, u32[]{:S(2)}) collective-permute-start(f32[64,128]{1,0:T(8,128)S(1)} %get-tuple-element.61), channel_id=1, source_target_pairs={{0,1},{1,0},{2,3},{3,2},{4,5},{5,4},{6,7},{7,6},{8,9},{9,8},{10,11... | collective-permute-start | bytes 98312 | tf_op jit(solution)/shard_map/ppermute | solution.py:769
  60.0 1.9 %collective-permute-done.13.inner_in_ref = f32[64,128]{1,0:T(8,128)S(1)} collective-permute-done((f32[64,128]{1,0:T(8,128)S(1)}, f32[64,128]{1,0:T(8,128)S(1)}, u32[]{:S(2)}, u32[]{:S(2)}) %collective-permute-start.13) | collective-permute-done | bytes 32800 | tf_op jit(solution)/shard_map/ppermute | solution.py:769
  61.9 1.2 %shard_map.112 = (f32[512,128]{1,0:T(8,128)S(1)}, f32[512,128]{1,0:T(8,128)S(1)}, f32[64,128]{1,0:T(8,128)}, f32[64,128]{1,0:T(8,128)S(1)}, f32[64,128]{1,0:T(8,128)S(1)}) custom-call(s32[1]{0:T(128)} %bitcast.place_ref, f32[512,128]{1,0:T(8,128)S(1)} %get-tuple-element.58.w_old_ref.w1_ref, f32[512,128]{1,0:T(8,128)S(1)} %get-tuple-element.59.u_old_ref, ...), custom_call_target="tpu_custom_call" | custom-call | flops 100000 | bytes 1000000 | tf_op jit(solution)/shard_map/pallas_call | solution.py:746
  63.8 5.4 %collective-permute-start.15 = (f32[64,128]{1,0:T(8,128)S(1)}, f32[64,128]{1,0:T(8,128)S(1)}, u32[]{:S(2)}, u32[]{:S(2)}) collective-permute-start(f32[64,128]{1,0:T(8,128)S(1)} %get-tuple-element.66), channel_id=1, source_target_pairs={{0,1},{1,0},{2,3},{3,2},{4,5},{5,4},{6,7},{7,6},{8,9},{9,8},{10,11... | collective-permute-start | bytes 98312 | tf_op jit(solution)/shard_map/ppermute | solution.py:769
  69.2 22.4 %all-to-all-start.1 = ((f32[64,1,128]{2,1,0:T(1,128)}), f32[64,1,128]{2,1,0:T(1,128)S(1)}, u32[]{:S(2)}, u32[]{:S(2)}) async-start(f32[64,1,128]{2,1,0:T(1,128)} %bitcast.4), calls=%async_computation.1 | async-start | bytes 65536 | tf_op jit(solution)/shard_map/all_to_all | solution.py:762
  91.5 1.5 %shard_map.115 = f32[5,2048]{1,0:T(8,128)} custom-call(s32[1]{0:T(128)} %bitcast.place_ref, f32[5,1024]{1,0:T(8,128)S(1)} %collective-permute-done.2.inner_1_ref, f32[5,1024]{1,0:T(8,128)S(1)} %collective-permute-done.5.middle_ref, f32[5,1024]{1,0:T(8,128)S(1)} %collective-permute-done.7.inner_2_ref, f32[4,5,1024]{2,1,0:T(8,128)S(1)} %all-to-all-done.far_ref, ...), custom_call_target="tpu_custom_call" | custom-call | flops 100000 | bytes 1000000 | tf_op jit(solution)/shard_map/pallas_call | solution.py:746
  93.1 8.0 %all-to-all-done.1 = f32[64,1,128]{2,1,0:T(1,128)S(1)} async-done(((f32[64,1,128]{2,1,0:T(1,128)}), f32[64,1,128]{2,1,0:T(1,128)S(1)}, u32[]{:S(2)}, u32[]{:S(2)}) %all-to-all-start.1) | async-done | bytes 32800 | tf_op jit(solution)/shard_map/all_to_all | solution.py:762
  101.0 1.6 %shard_map.114 = (f32[512,128]{1,0:T(8,128)}, f32[512,128]{1,0:T(8,128)}) custom-call(f32[512,128]{1,0:T(8,128)S(1)} %get-tuple-element.51.w_old_ref.w0_ref, f32[128,128]{1,0:T(8,128)S(1)} %get-tuple-element.57.face_ref, f32[512,128]{1,0:T(8,128)S(1)} %get-tuple-element.58.w_old_ref.w1_ref, f32[512,128]{1,0:T(8,128)S(1)} %get-tuple-element.63.w2_ref, ...), custom_call_target="tpu_custom_call" | custom-call | flops 100000 | bytes 1000000 | tf_op jit(solution)/shard_map/pallas_call | solution.py:746
  (35 shorter events, 5.6 us)
Async XLA Ops:
  0.6 14.8 %collective-permute-start = (f32[5,512,128]{2,1,0:T(8,128)}, f32[5,512,128]{2,1,0:T(8,128)S(1)}, u32[]{:S(2)}, u32[]{:S(2)}) collective-permute-start(f32[5,512,128]{2,1,0:T(8,128)} %param.8), channel_id=1, source_target_pairs={{0,64},{64,0},{1,65},{65,1},{2,66},{66,2},{3,67},{67,3},{4,68},{68... | collective-permute-start | bytes 3932168 | tf_op jit(solution)/shard_map/ppermute | solution.py:784
  3.1 12.4 %collective-permute-start.1 = (f32[104,128]{1,0:T(8,128)S(1)}, f32[104,128]{1,0:T(8,128)S(1)}, u32[]{:S(2)}, u32[]{:S(2)}) collective-permute-start(f32[104,128]{1,0:T(8,128)S(1)} %get-tuple-element.38), channel_id=1, source_target_pairs={{0,1},{1,0},{2,3},{3,2},{4,5},{5,4},{6,7},{7,6},{8,9},{9,8},{10,11... | collective-permute-start | bytes 159752 | tf_op jit(solution)/shard_map/ppermute | solution.py:769
  4.9 14.0 %collective-permute-start.3 = (f32[104,128]{1,0:T(8,128)S(1)}, f32[104,128]{1,0:T(8,128)S(1)}, u32[]{:S(2)}, u32[]{:S(2)}) collective-permute-start(f32[104,128]{1,0:T(8,128)S(1)} %get-tuple-element.40), channel_id=1, source_target_pairs={{1,2},{2,1},{3,4},{4,3},{5,6},{6,5},{7,8},{8,7},{9,10},{10,9},{11,... | collective-permute-start | bytes 159752 | tf_op jit(solution)/shard_map/ppermute | solution.py:769
  5.5 13.3 %collective-permute-start.4 = (f32[32,128]{1,0:T(8,128)S(1)}, f32[32,128]{1,0:T(8,128)S(1)}, u32[]{:S(2)}, u32[]{:S(2)}) collective-permute-start(f32[32,128]{1,0:T(8,128)S(1)} %get-tuple-element.41), channel_id=1, source_target_pairs={{2,4},{4,2},{3,5},{5,3},{6,8},{8,6},{7,9},{9,7},{10,12},{12,10},{1... | collective-permute-start | bytes 49160 | tf_op jit(solution)/shard_map/ppermute | solution.py:769
  6.2 27.1 %collective-permute-start.6 = (f32[32,128]{1,0:T(8,128)S(1)}, f32[32,128]{1,0:T(8,128)S(1)}, u32[]{:S(2)}, u32[]{:S(2)}) collective-permute-start(f32[32,128]{1,0:T(8,128)S(1)} %get-tuple-element.43), channel_id=1, source_target_pairs={{0,2},{2,0},{1,3},{3,1},{4,6},{6,4},{5,7},{7,5},{8,10},{10,8},{9,1... | collective-permute-start | bytes 49160 | tf_op jit(solution)/shard_map/ppermute | solution.py:769
  18.1 16.2 %collective-permute-start.2 = (f32[5,1024]{1,0:T(8,128)S(1)}, f32[5,1024]{1,0:T(8,128)S(1)}, u32[]{:S(2)}, u32[]{:S(2)}) collective-permute-start(f32[5,1024]{1,0:T(8,128)S(1)} %get-tuple-element.39), channel_id=1, source_target_pairs={{0,1},{1,0},{2,3},{3,2},{4,5},{5,4},{6,7},{7,6},{8,9},{9,8},{10,11... | collective-permute-start | bytes 61448 | tf_op jit(solution)/shard_map/ppermute | solution.py:777
  19.8 14.5 %collective-permute-start.5 = (f32[5,1024]{1,0:T(8,128)S(1)}, f32[5,1024]{1,0:T(8,128)S(1)}, u32[]{:S(2)}, u32[]{:S(2)}) collective-permute-start(f32[5,1024]{1,0:T(8,128)S(1)} %get-tuple-element.42), channel_id=1, source_target_pairs={{1,2},{2,1},{5,6},{6,5},{9,10},{10,9},{13,14},{14,13},{17,18},{18,... | collective-permute-start | bytes 61448 | tf_op jit(solution)/shard_map/ppermute | solution.py:777
  20.5 19.2 %all-to-all-start = ((f32[4,5,1024]{2,1,0:T(8,128)}), f32[4,5,1024]{2,1,0:T(8,128)S(1)}, u32[]{:S(2)}, u32[]{:S(2)}) async-start(f32[4,5,1024]{2,1,0:T(8,128)} %get-tuple-element.44), calls=%async_computation | async-start | bytes 262144 | tf_op jit(solution)/shard_map/all_to_all | solution.py:774
  33.3 6.4 %copy-start.2 = (s32[2048,1]{0,1:T(1,128)S(1)}, s32[2048,1]{0,1:T(1,128)}, u32[]{:S(2)}) copy-start(s32[2048,1]{0,1:T(1,128)} %param.10) | copy-start | bytes 24580
  33.3 9.8 %copy-start = (f32[512,128]{1,0:T(8,128)S(1)}, f32[512,128]{1,0:T(8,128)}, u32[]{:S(2)}) copy-start(f32[512,128]{1,0:T(8,128)} %forcing_ref.3) | copy-start | bytes 786436
  33.3 9.8 %copy-start.3 = (f32[4,128]{1,0:T(4,128)S(1)}, f32[4,128]{1,0:T(4,128)}, u32[]{:S(2)}) copy-start(f32[4,128]{1,0:T(4,128)} %geometry_ref.9) | copy-start | bytes 6148
  33.3 9.8 %copy-start.4 = (s32[2,8]{1,0:T(2,128)S(1)}, s32[2,8]{1,0:T(2,128)}, u32[]{:S(2)}) copy-start(s32[2,8]{1,0:T(2,128)} %wall_ref.3) | copy-start | bytes 196
  33.3 11.4 %copy-start.1 = (bf16[64,192]{1,0:T(8,128)(2,1)S(1)}, bf16[64,192]{1,0:T(8,128)(2,1)}, u32[]{:S(2)}) copy-start(bf16[64,192]{1,0:T(8,128)(2,1)} %constant.12.xmat_ref) | copy-start | bytes 73732
  34.2 5.5 %collective-permute-start.7 = (f32[5,1024]{1,0:T(8,128)S(1)}, f32[5,1024]{1,0:T(8,128)S(1)}, u32[]{:S(2)}, u32[]{:S(2)}) collective-permute-start(f32[5,1024]{1,0:T(8,128)S(1)} %shard_map.107), channel_id=1, source_target_pairs={{0,2},{2,0},{1,3},{3,1},{4,6},{6,4},{5,7},{7,5},{8,10},{10,8},{9,1... | collective-permute-start | bytes 61448 | tf_op jit(solution)/shard_map/ppermute | solution.py:777
  40.3 3.7 %collective-permute-start.8 = (f32[16,128]{1,0:T(8,128)S(1)}, f32[16,128]{1,0:T(8,128)S(1)}, u32[]{:S(2)}, u32[]{:S(2)}) collective-permute-start(f32[16,128]{1,0:T(8,128)S(1)} %shard_map.108.own_ref), channel_id=1, source_target_pairs={{1,2},{2,1},{3,4},{4,3},{5,6},{6,5},{7,8},{8,7},{9,10},{10,9},{11,... | collective-permute-start | bytes 24584 | tf_op jit(solution)/shard_map/ppermute | solution.py:769
  41.0 3.7 %collective-permute-start.9 = (f32[16,128]{1,0:T(8,128)S(1)}, f32[16,128]{1,0:T(8,128)S(1)}, u32[]{:S(2)}, u32[]{:S(2)}) collective-permute-start(f32[16,128]{1,0:T(8,128)S(1)} %shard_map.108.own_ref), channel_id=1, source_target_pairs={{0,1},{1,0},{2,3},{3,2},{4,5},{5,4},{6,7},{7,6},{8,9},{9,8},{10,11... | collective-permute-start | bytes 24584 | tf_op jit(solution)/shard_map/ppermute | solution.py:769
  46.3 6.2 %collective-permute-start.10 = (f32[128,128]{1,0:T(8,128)S(1)}, f32[128,128]{1,0:T(8,128)S(1)}, u32[]{:S(2)}, u32[]{:S(2)}) collective-permute-start(f32[128,128]{1,0:T(8,128)S(1)} %get-tuple-element.53), channel_id=1, source_target_pairs={{1,2},{2,1},{3,4},{4,3},{5,6},{6,5},{7,8},{8,7},{9,10},{10,9},{11,... | collective-permute-start | bytes 196616 | tf_op jit(solution)/shard_map/ppermute | solution.py:769
  47.0 7.7 %collective-permute-start.11 = (f32[128,128]{1,0:T(8,128)S(1)}, f32[128,128]{1,0:T(8,128)S(1)}, u32[]{:S(2)}, u32[]{:S(2)}) collective-permute-start(f32[128,128]{1,0:T(8,128)S(1)} %get-tuple-element.54), channel_id=1, source_target_pairs={{0,1},{1,0},{2,3},{3,2},{4,5},{5,4},{6,7},{7,6},{8,9},{9,8},{10,11... | collective-permute-start | bytes 196616 | tf_op jit(solution)/shard_map/ppermute | solution.py:769
  55.4 4.7 %collective-permute-start.12 = (f32[64,128]{1,0:T(8,128)S(1)}, f32[64,128]{1,0:T(8,128)S(1)}, u32[]{:S(2)}, u32[]{:S(2)}) collective-permute-start(f32[64,128]{1,0:T(8,128)S(1)} %get-tuple-element.60), channel_id=1, source_target_pairs={{1,2},{2,1},{3,4},{4,3},{5,6},{6,5},{7,8},{8,7},{9,10},{10,9},{11,... | collective-permute-start | bytes 98312 | tf_op jit(solution)/shard_map/ppermute | solution.py:769
  56.0 5.9 %collective-permute-start.13 = (f32[64,128]{1,0:T(8,128)S(1)}, f32[64,128]{1,0:T(8,128)S(1)}, u32[]{:S(2)}, u32[]{:S(2)}) collective-permute-start(f32[64,128]{1,0:T(8,128)S(1)} %get-tuple-element.61), channel_id=1, source_target_pairs={{0,1},{1,0},{2,3},{3,2},{4,5},{5,4},{6,7},{7,6},{8,9},{9,8},{10,11... | collective-permute-start | bytes 98312 | tf_op jit(solution)/shard_map/ppermute | solution.py:769
  63.2 29.9 %collective-permute-start.14 = (f32[64,128]{1,0:T(8,128)S(1)}, f32[64,128]{1,0:T(8,128)S(1)}, u32[]{:S(2)}, u32[]{:S(2)}) collective-permute-start(f32[64,128]{1,0:T(8,128)S(1)} %get-tuple-element.65), channel_id=1, source_target_pairs={{1,2},{2,1},{3,4},{4,3},{5,6},{6,5},{7,8},{8,7},{9,10},{10,9},{11,... | collective-permute-start | bytes 98312 | tf_op jit(solution)/shard_map/ppermute | solution.py:769
  63.8 29.2 %collective-permute-start.15 = (f32[64,128]{1,0:T(8,128)S(1)}, f32[64,128]{1,0:T(8,128)S(1)}, u32[]{:S(2)}, u32[]{:S(2)}) collective-permute-start(f32[64,128]{1,0:T(8,128)S(1)} %get-tuple-element.66), channel_id=1, source_target_pairs={{0,1},{1,0},{2,3},{3,2},{4,5},{5,4},{6,7},{7,6},{8,9},{9,8},{10,11... | collective-permute-start | bytes 98312 | tf_op jit(solution)/shard_map/ppermute | solution.py:769
  69.2 31.9 %all-to-all-start.1 = ((f32[64,1,128]{2,1,0:T(1,128)}), f32[64,1,128]{2,1,0:T(1,128)S(1)}, u32[]{:S(2)}, u32[]{:S(2)}) async-start(f32[64,1,128]{2,1,0:T(1,128)} %bitcast.4), calls=%async_computation.1 | async-start | bytes 65536 | tf_op jit(solution)/shard_map/all_to_all | solution.py:762
